TPU v7x, 32 devices: a whole 2x2x4 slice. The times are simulated.
32 devices in a mesh: group: 8 (over z, x), rad: 4 (over y, core).
Axes of the slice: x: 2, y: 2, z: 4, core: 2. Of those that a mesh axis runs over, the one named last changes fastest.
Arguments:
- source_term: float32 [32, 128, 1024], P('group', 'rad'), may hold values from -6 to 6
- initial_guess: float32 [32, 128, 1024], P('group', 'rad'), may hold values from -3 to 3
- metric: float32 [3, 8, 32, 256], P(None, 'group', 'rad'), may hold values from 0.5 to 4
Outputs:
- solution: float32 [32, 128, 1024], P('group', 'rad')
- residual: float32 [32, 128, 1024], P('group', 'rad')
All inputs are finite; a program needn't handle non-finite values.
Results may differ from a plain program's by a relative error of at most 0.00025.
Values sent between devices are 32-bit elements; how exact they have to be, the bound alone decides.
No kernel may reach another device: no remote copies, remote signals or barrier semaphores. Data moves between devices by JAX's collectives and lax.ppermute only.
A program may use at most 128 MiB of HBM per device.

v0:
```python
import math

import jax
import jax.numpy as jnp
import numpy as np
from jax import lax
from jax.sharding import PartitionSpec as P

ITERS = 3


def passed_along(block, axis, distance):
    devices = range(lax.axis_size(axis))
    route = [(i - distance, i) for i in devices if i - distance in devices]
    return lax.ppermute(block, axis, route)


def passed_along_2(value, axis, steps):
    count = lax.axis_size(axis)
    pairs = [(source, (source + steps) % count) for source in range(count)]
    return lax.ppermute(value, axis, pairs)


def gll_tables():
    root = math.sqrt(3.0 / 7.0)
    points = np.array([-1.0, -root, 0.0, root, 1.0])
    weights = np.array([0.1, 49.0 / 90.0, 32.0 / 45.0, 49.0 / 90.0, 0.1])
    factor = np.array(
        [np.prod([points[a] - points[m] for m in range(5) if m != a]) for a in range(5)]
    )
    derivative = np.zeros((5, 5))
    for p in range(5):
        for a in range(5):
            if p == a:
                derivative[p, a] = np.sum(
                    [1.0 / (points[a] - points[m]) for m in range(5) if m != a]
                )
            else:
                derivative[p, a] = factor[p] / (factor[a] * (points[p] - points[a]))
    return (jnp.asarray(derivative, jnp.float32), jnp.asarray(weights, jnp.float32))


def apply_elements(elements, metric):
    derivative, weights = gll_tables()
    quad_weight = (
        weights[:, None, None] * weights[None, :, None] * weights[None, None, :]
    ).reshape(5, 5, 5, 1, 1, 1)
    high = lax.Precision.HIGHEST
    grad_x = jnp.einsum("pa,abcxyz->pbcxyz", derivative, elements, precision=high)
    result_sum = jnp.einsum(
        "pa,pbcxyz->abcxyz", derivative, grad_x * quad_weight * metric[0], precision=high
    )
    grad_r = jnp.einsum("qb,abcxyz->aqcxyz", derivative, elements, precision=high)
    result_sum = result_sum + jnp.einsum(
        "qb,aqcxyz->abcxyz", derivative, grad_r * quad_weight * metric[1], precision=high
    )
    grad_y = jnp.einsum("sc,abcxyz->absxyz", derivative, elements, precision=high)
    result_sum = result_sum + jnp.einsum(
        "sc,absxyz->abcxyz", derivative, grad_y * quad_weight * metric[2], precision=high
    )
    return result_sum


def element_diagonal(metric):
    derivative, weights = gll_tables()
    squared = jnp.sum(derivative * derivative * weights[:, None], axis=0)
    term_x = (squared[:, None, None] * weights[None, :, None] * weights[None, None, :]).reshape(
        5, 5, 5, 1, 1, 1
    )
    term_r = (weights[:, None, None] * squared[None, :, None] * weights[None, None, :]).reshape(
        5, 5, 5, 1, 1, 1
    )
    term_y = (weights[:, None, None] * weights[None, :, None] * squared[None, None, :]).reshape(
        5, 5, 5, 1, 1, 1
    )
    return term_x * metric[0] + term_r * metric[1] + term_y * metric[2]


def to_blocks(field):
    rows_x, rows_r, rows_y = field.shape
    shaped = field.reshape(rows_x // 4, 4, rows_r // 4, 4, rows_y // 4, 4)
    return shaped.transpose(1, 3, 5, 0, 2, 4)


def from_blocks(blocks):
    count_x, count_r, count_y = (blocks.shape[3], blocks.shape[4], blocks.shape[5])
    return blocks.transpose(3, 0, 4, 1, 5, 2).reshape(4 * count_x, 4 * count_r, 4 * count_y)


def extend_y(wide):
    return jnp.concatenate([wide, jnp.roll(wide[:, :, 0:1], -1, axis=5)], 2)


def fold_y(raw):
    first = raw[:, :, 0:1] + jnp.roll(raw[:, :, 4:5], 1, axis=5)
    return jnp.concatenate([first, raw[:, :, 1:4]], 2)


def assemble(raw):
    folded = fold_y(raw)
    count_r = folded.shape[4]
    below_r = passed_along(folded[:, 4:5, :, :, count_r - 1 :], "rad", 1)
    carried = jnp.concatenate([below_r, folded[:, 4:5, :, :, : count_r - 1]], 4)
    folded = jnp.concatenate([folded[:, 0:1] + carried, folded[:, 1:4]], 1)
    count_x = folded.shape[3]
    below_x = passed_along_2(folded[4:5, :, :, count_x - 1 :], "group", 1)
    carried = jnp.concatenate([below_x, folded[4:5, :, :, : count_x - 1]], 3)
    return jnp.concatenate([folded[0:1] + carried, folded[1:4]], 0)


def paired_sums(residual, smoothed, applied):
    return lax.psum((jnp.sum(residual * smoothed), jnp.sum(applied * smoothed)), ("group", "rad"))


def local(source_term, initial_guess, metric):

    def operate(field):
        above_x = passed_along_2(field[0:1, :, :, 0:1], "group", -1)
        plane_a = jnp.concatenate([field[0:1, :, :, 1:], above_x], 3)
        wide = jnp.concatenate([field, plane_a], 0)
        above_r = passed_along(wide[:, 0:1, :, :, 0:1], "rad", -1)
        plane_b = jnp.concatenate([wide[:, 0:1, :, :, 1:], above_r], 4)
        wide = jnp.concatenate([wide, plane_b], 1)
        return assemble(apply_elements(extend_y(wide), metric))

    diagonal = assemble(element_diagonal(metric))
    scaling = 1.0 / diagonal
    guess = to_blocks(initial_guess)
    residual = to_blocks(source_term) - operate(guess)
    solution = guess
    smoothed = scaling * residual
    applied = operate(smoothed)
    weighted_norm, curvature_sum = paired_sums(residual, smoothed, applied)
    step_size = weighted_norm / curvature_sum
    direction = smoothed
    searched = applied
    for iteration in range(ITERS):
        solution = solution + step_size * direction
        residual = residual - step_size * searched
        if iteration + 1 < ITERS:
            smoothed = scaling * residual
            applied = operate(smoothed)
            next_norm, curvature_sum = paired_sums(residual, smoothed, applied)
            ratio = next_norm / weighted_norm
            step_size = next_norm / (curvature_sum - ratio * next_norm / step_size)
            direction = smoothed + ratio * direction
            searched = applied + ratio * searched
            weighted_norm = next_norm
    return (from_blocks(solution), from_blocks(residual))


def solution(mesh):
    in_specs = (P("group", "rad", None), P("group", "rad", None), P(None, "group", "rad", None))
    out_specs = (P("group", "rad", None), P("group", "rad", None))
    return jax.shard_map(local, mesh=mesh, in_specs=in_specs, out_specs=out_specs, check_vma=False)
```

profile of v0, /device:TPU:0, one launch (start us, length us, event | category | flops | bytes accessed | tf_op | source)
XLA Modules:
  0.0 408.9 jit_solution(13129689504433719481)
XLA Ops:
  0.6 19.5 %reshape.564 = f32[1,4,8,4,256,4]{5,4,3,2,1,0:T(8,128)} reshape(f32[4,32,1024]{2,1,0:T(8,128)} %param.14) | data formatting | bytes 1048576 | tf_op jit(solution)/shard_map/reshape | solution.py:81
  20.1 10.1 %copy.48 = f32[1,4,8,4,256,4]{4,1,2,5,3,0:T(4,128)S(1)} copy(f32[1,4,8,4,256,4]{5,4,3,2,1,0:T(8,128)} %reshape.564) | data formatting | bytes 1048576 | tf_op jit(solution)/shard_map/reshape | solution.py:81
  30.3 6.1 %collective-permute-start = (f32[1,4,4,1,8,256]{5,0,4,2,1,3:T(1,128)S(1)}, f32[1,4,4,1,8,256]{5,0,4,2,1,3:T(1,128)S(1)}, u32[]{:S(2)}, u32[]{:S(2)}) collective-permute-start(f32[1,4,4,1,8,256]{5,0,4,2,1,3:T(1,128)S(1)} %slice.355), channel_id=1, source_target_pairs={{0,28},{4,0},{8,4},{12,8},{16,12},{20,16},{24,20},{28,24},{1,29},{... | collective-permute-start | bytes 393224 | tf_op jit(solution)/shard_map/ppermute | solution.py:21
  36.6 18.6 %reshape.565 = f32[1,4,8,4,256,4]{5,4,3,2,1,0:T(8,128)} reshape(f32[4,32,1024]{2,1,0:T(8,128)S(1)} %copy-done.7) | data formatting | bytes 1048576 | tf_op jit(solution)/shard_map/reshape | solution.py:81
  55.3 10.0 %copy.49 = f32[1,4,8,4,256,4]{4,1,2,5,3,0:T(4,128)S(1)} copy(f32[1,4,8,4,256,4]{5,4,3,2,1,0:T(8,128)} %reshape.565) | data formatting | bytes 1048576 | tf_op jit(solution)/shard_map/reshape | solution.py:81
  65.4 1.7 collective-permute-start.1
  67.1 1.4 collective-permute-done.1
  68.9 2.2 fusion.62
  71.2 2.2 fusion.66
  73.4 1.8 fusion.122
  76.3 2.1 fusion.64
  78.4 1.7 fusion.32
  80.1 14.8 %bitcast_add_fusion.6 = f32[5,5,5,1,8,256]{5,0,4,2,1,3:T(8,128)S(1)} fusion(f32[5,5,8,256,5]{3,4,2,1,0:T(8,128)S(1)} %fusion.32, f32[5,5,8,256,5]{3,4,2,1,0:T(8,128)S(1)} %fusion.64, f32[5,5,1,1,1]{0,1,4,3,2:T(8,128)S(1)} %copy-done.4, f32[5,5,5,8,256]{4,0,3,2,1:T(8,128)S(1)} %fusion.122, f32[8,256]{1,0:T(8,128)S(1)} %get-tuple-element.21, ...), kind=kOutput, calls=%fused_computation.57 | convolution fusion | flops 16384000 | bytes 4104792 | tf_op jit(solution)/shard_map/pa,pbcxyz->abcxyz/dot_general | solution.py:50
  95.5 3.9 collective-permute-start.2
  99.6 1.9 collective-permute-start.4
  102.9 8.2 %collective-permute-done.3 = f32[1,4,4,1,8,256]{5,0,4,2,1,3:T(1,128)S(1)} collective-permute-done((f32[1,4,4,1,8,256]{5,0,4,2,1,3:T(1,128)S(1)}, f32[1,4,4,1,8,256]{5,0,4,2,1,3:T(1,128)S(1)}, u32[]{:S(2)}, u32[]{:S(2)}) %collective-permute-start.3) | collective-permute-done | bytes 131104 | tf_op jit(solution)/shard_map/ppermute | solution.py:21
  111.3 1.7 collective-permute-done.5
  113.9 5.0 %collective-permute-done.6 = f32[1,4,4,1,8,256]{5,0,4,2,1,3:T(1,128)S(1)} collective-permute-done((f32[1,4,4,1,8,256]{5,0,4,2,1,3:T(1,128)S(1)}, f32[1,4,4,1,8,256]{5,0,4,2,1,3:T(1,128)S(1)}, u32[]{:S(2)}, u32[]{:S(2)}) %collective-permute-start.6) | collective-permute-done | bytes 131104 | tf_op jit(solution)/shard_map/ppermute | solution.py:21
  118.9 1.3 collective-permute-start.7
  120.2 1.7 collective-permute-done.7
  122.4 2.2 fusion.56
  124.6 2.1 fusion.60
  126.8 1.8 fusion.123
  128.6 1.7 fusion.28
  130.9 2.1 fusion.58
  133.0 3.0 bitcast_add_fusion.4
  136.5 2.4 collective-permute-start.8
  140.2 8.3 %collective-permute-done.9 = f32[1,4,4,1,8,256]{5,0,4,2,1,3:T(1,128)S(1)} collective-permute-done((f32[1,4,4,1,8,256]{5,0,4,2,1,3:T(1,128)S(1)}, f32[1,4,4,1,8,256]{5,0,4,2,1,3:T(1,128)S(1)}, u32[]{:S(2)}, u32[]{:S(2)}) %collective-permute-start.9) | collective-permute-done | bytes 131104 | tf_op jit(solution)/shard_map/ppermute | solution.py:21
  149.8 37.1 %all-reduce.2 = (f32[]{:T(128)}, f32[]{:T(128)}) all-reduce(f32[]{:T(128)} %get-tuple-element.7, f32[]{:T(128)} %get-tuple-element.6), channel_id=1, replica_groups=mesh['group'=8,'rad'=4] {'group','rad'}, use_global_device_ids=true, to_apply=%region_2.3 | all-reduce | flops 2 | bytes 16 | tf_op jit(solution)/shard_map/psum | solution.py:112
  188.2 1.6 fusion.120
  189.9 4.0 collective-permute-start.10
  194.0 2.5 collective-permute-done.10
  196.5 1.3 collective-permute-start.11
  197.9 1.7 collective-permute-done.11
  200.1 2.2 fusion.50
  202.3 2.1 fusion.54
  204.4 1.8 fusion.124
  206.2 1.7 fusion.24
  208.5 2.1 fusion.52
  210.7 2.8 bitcast_add_fusion.2
  213.9 4.2 %collective-permute-start.12 = (f32[5,1,4,1,1,256]{5,0,4,2,1,3:T(8,128)S(1)}, f32[5,1,4,1,1,256]{5,0,4,2,1,3:T(8,128)S(1)}, u32[]{:S(2)}, u32[]{:S(2)}) collective-permute-start(f32[5,1,4,1,1,256]{5,0,4,2,1,3:T(8,128)S(1)} %pad_maximum_fusion.30), channel_id=1, source_target_pairs={{0,1},{1,2},{2,3},{4,5},{5,6},{6,7},{8,9},{9,10},{10,11},{12,13},{... | collective-permute-start | bytes 61448 | tf_op jit(solution)/shard_map/ppermute | solution.py:15
  219.3 1.7 collective-permute-start.13
  221.1 7.4 %collective-permute-done.13 = f32[1,4,4,1,8,256]{5,0,4,2,1,3:T(1,128)S(1)} collective-permute-done((f32[1,4,4,1,8,256]{5,0,4,2,1,3:T(1,128)S(1)}, f32[1,4,4,1,8,256]{5,0,4,2,1,3:T(1,128)S(1)}, u32[]{:S(2)}, u32[]{:S(2)}) %collective-permute-start.13) | collective-permute-done | bytes 131104 | tf_op jit(solution)/shard_map/ppermute | solution.py:21
  230.5 38.6 %all-reduce.1 = (f32[]{:T(128)}, f32[]{:T(128)}) all-reduce(f32[]{:T(128)} %get-tuple-element.5, f32[]{:T(128)} %get-tuple-element.4), channel_id=1, replica_groups=mesh['group'=8,'rad'=4] {'group','rad'}, use_global_device_ids=true, to_apply=%region_6.7 | all-reduce | flops 2 | bytes 16 | tf_op jit(solution)/shard_map/psum | solution.py:112
  273.4 2.0 fusion.119
  275.6 3.3 collective-permute-start.14
  278.9 2.5 collective-permute-done.14
  281.4 1.3 collective-permute-start.15
  282.8 1.7 collective-permute-done.15
  285.0 2.2 fusion.44
  287.2 2.1 fusion.48
  289.3 1.8 fusion.125
  291.1 1.7 fusion.20
  293.4 2.1 fusion.46
  295.6 2.9 bitcast_add_fusion
  298.8 4.1 %collective-permute-start.16 = (f32[5,1,4,1,1,256]{5,0,4,2,1,3:T(8,128)S(1)}, f32[5,1,4,1,1,256]{5,0,4,2,1,3:T(8,128)S(1)}, u32[]{:S(2)}, u32[]{:S(2)}) collective-permute-start(f32[5,1,4,1,1,256]{5,0,4,2,1,3:T(8,128)S(1)} %pad_maximum_fusion.28), channel_id=1, source_target_pairs={{0,1},{1,2},{2,3},{4,5},{5,6},{6,7},{8,9},{9,10},{10,11},{12,13},{... | collective-permute-start | bytes 61448 | tf_op jit(solution)/shard_map/ppermute | solution.py:15
  304.1 1.4 collective-permute-start.17
  305.7 7.0 %collective-permute-done.17 = f32[1,4,4,1,8,256]{5,0,4,2,1,3:T(1,128)S(1)} collective-permute-done((f32[1,4,4,1,8,256]{5,0,4,2,1,3:T(1,128)S(1)}, f32[1,4,4,1,8,256]{5,0,4,2,1,3:T(1,128)S(1)}, u32[]{:S(2)}, u32[]{:S(2)}) %collective-permute-start.17) | collective-permute-done | bytes 131104 | tf_op jit(solution)/shard_map/ppermute | solution.py:21
  314.1 38.3 %all-reduce = (f32[]{:T(128)}, f32[]{:T(128)}) all-reduce(f32[]{:T(128)} %get-tuple-element.3, f32[]{:T(128)} %get-tuple-element.2), channel_id=1, replica_groups=mesh['group'=8,'rad'=4] {'group','rad'}, use_global_device_ids=true, to_apply=%region_10.11 | all-reduce | flops 2 | bytes 16 | tf_op jit(solution)/shard_map/psum | solution.py:112
  356.1 2.9 subtract_bitcast_fusion
  359.0 9.6 %copy.84 = f32[1,4,8,4,256,4]{5,4,3,2,1,0:T(8,128)} copy(f32[1,4,8,4,256,4]{4,1,2,5,3,0:T(4,128)} %get-tuple-element.32) | data formatting | bytes 1048576 | tf_op jit(solution)/shard_map/transpose | solution.py:87
  368.6 15.8 %reshape.579 = f32[4,32,1024]{2,1,0:T(8,128)} reshape(f32[1,4,8,4,256,4]{5,4,3,2,1,0:T(8,128)} %copy.84) | data formatting | bytes 1048576 | tf_op jit(solution)/shard_map/reshape | solution.py:87
  384.4 8.5 %copy.83 = f32[1,4,8,4,256,4]{5,4,3,2,1,0:T(8,128)} copy(f32[1,4,8,4,256,4]{4,1,2,5,3,0:T(4,128)S(1)} %copy-done.5) | data formatting | bytes 1048576 | tf_op jit(solution)/shard_map/transpose | solution.py:87
  392.9 15.7 %reshape.578 = f32[4,32,1024]{2,1,0:T(8,128)} reshape(f32[1,4,8,4,256,4]{5,4,3,2,1,0:T(8,128)} %copy.83) | data formatting | bytes 1048576 | tf_op jit(solution)/shard_map/reshape | solution.py:87
  (110 shorter events, 18.2 us)
Async XLA Ops:
  20.1 16.3 %copy-start.9 = (f32[5]{0:T(128)S(1)}, f32[5]{0:T(128)}, u32[]{:S(2)}) copy-start(f32[5]{0:T(128)} %constant.15) | copy-start | bytes 64
  20.1 16.3 %copy-start.10 = (f32[5]{0:T(128)S(1)}, f32[5]{0:T(128)}, u32[]{:S(2)}) copy-start(f32[5]{0:T(128)} %constant.9.clone) | copy-start | bytes 64
  20.1 16.5 %copy-start.7 = (f32[4,32,1024]{2,1,0:T(8,128)S(1)}, f32[4,32,1024]{2,1,0:T(8,128)}, u32[]{:S(2)}) copy-start(f32[4,32,1024]{2,1,0:T(8,128)} %param.13) | copy-start | bytes 1572868
  30.3 35.0 %collective-permute-start = (f32[1,4,4,1,8,256]{5,0,4,2,1,3:T(1,128)S(1)}, f32[1,4,4,1,8,256]{5,0,4,2,1,3:T(1,128)S(1)}, u32[]{:S(2)}, u32[]{:S(2)}) collective-permute-start(f32[1,4,4,1,8,256]{5,0,4,2,1,3:T(1,128)S(1)} %slice.355), channel_id=1, source_target_pairs={{0,28},{4,0},{8,4},{12,8},{16,12},{20,16},{24,20},{28,24},{1,29},{... | collective-permute-start | bytes 393224 | tf_op jit(solution)/shard_map/ppermute | solution.py:21
  55.3 10.0 %copy-start.8 = (f32[3,1,8,256]{3,2,1,0:T(8,128)S(1)}, f32[3,1,8,256]{3,2,1,0:T(8,128)}, u32[]{:S(2)}) copy-start(f32[3,1,8,256]{3,2,1,0:T(8,128)} %param.15) | copy-start | bytes 73732
  65.4 3.6 copy-start.4
  65.4 3.1 collective-permute-start.1
  95.5 6.1 %collective-permute-start.2 = (f32[5,1,4,1,1,256]{5,0,4,2,1,3:T(8,128)S(1)}, f32[5,1,4,1,1,256]{5,0,4,2,1,3:T(8,128)S(1)}, u32[]{:S(2)}, u32[]{:S(2)}) collective-permute-start(f32[5,1,4,1,1,256]{5,0,4,2,1,3:T(8,128)S(1)} %pad_maximum_fusion.35), channel_id=1, source_target_pairs={{0,1},{1,2},{2,3},{4,5},{5,6},{6,7},{8,9},{9,10},{10,11},{12,13},{... | collective-permute-start | bytes 61448 | tf_op jit(solution)/shard_map/ppermute | solution.py:15
  99.6 2.8 collective-permute-start.4
  102.0 9.1 %collective-permute-start.3 = (f32[1,4,4,1,8,256]{5,0,4,2,1,3:T(1,128)S(1)}, f32[1,4,4,1,8,256]{5,0,4,2,1,3:T(1,128)S(1)}, u32[]{:S(2)}, u32[]{:S(2)}) collective-permute-start(f32[1,4,4,1,8,256]{5,0,4,2,1,3:T(1,128)S(1)} %slice.361), channel_id=1, source_target_pairs={{0,4},{4,8},{8,12},{12,16},{16,20},{20,24},{24,28},{28,0},{1,5},{5... | collective-permute-start | bytes 393224 | tf_op jit(solution)/shard_map/ppermute | solution.py:21
  102.8 85.4 %copy-start = (f32[3,4,4,1,8,256]{5,0,4,2,1,3:T(4,128)}, f32[3,4,4,1,8,256]{5,0,4,2,1,3:T(4,128)S(1)}, u32[]{:S(2)}) copy-start(f32[3,4,4,1,8,256]{5,0,4,2,1,3:T(4,128)S(1)} %slice.369) | copy-start | bytes 1179652
  102.8 10.1 %collective-permute-start.5 = (f32[1,4,4,1,8,256]{5,0,4,2,1,3:T(1,128)S(1)}, f32[1,4,4,1,8,256]{5,0,4,2,1,3:T(1,128)S(1)}, u32[]{:S(2)}, u32[]{:S(2)}) collective-permute-start(f32[1,4,4,1,8,256]{5,0,4,2,1,3:T(1,128)S(1)} %slice.368), channel_id=1, source_target_pairs={{0,4},{4,8},{8,12},{12,16},{16,20},{20,24},{24,28},{28,0},{1,5},{5... | collective-permute-start | bytes 393224 | tf_op jit(solution)/shard_map/ppermute | solution.py:21
  113.7 34.9 %copy-start.3 = (f32[4,4,4,1,8,256]{5,0,4,2,1,3:T(4,128)}, f32[4,4,4,1,8,256]{5,0,4,2,1,3:T(4,128)S(1)}, u32[]{:S(2)}) copy-start(f32[4,4,4,1,8,256]{5,0,4,2,1,3:T(4,128)S(1)} %get-tuple-element.19) | copy-start | bytes 1572868
  113.8 5.0 %collective-permute-start.6 = (f32[1,4,4,1,8,256]{5,0,4,2,1,3:T(1,128)S(1)}, f32[1,4,4,1,8,256]{5,0,4,2,1,3:T(1,128)S(1)}, u32[]{:S(2)}, u32[]{:S(2)}) collective-permute-start(f32[1,4,4,1,8,256]{5,0,4,2,1,3:T(1,128)S(1)} %slice.370), channel_id=1, source_target_pairs={{0,28},{4,0},{8,4},{12,8},{16,12},{20,16},{24,20},{28,24},{1,29},{... | collective-permute-start | bytes 393224 | tf_op jit(solution)/shard_map/ppermute | solution.py:21
  118.9 3.1 collective-permute-start.7
  136.5 3.2 collective-permute-start.8
  140.0 8.5 %collective-permute-start.9 = (f32[1,4,4,1,8,256]{5,0,4,2,1,3:T(1,128)S(1)}, f32[1,4,4,1,8,256]{5,0,4,2,1,3:T(1,128)S(1)}, u32[]{:S(2)}, u32[]{:S(2)}) collective-permute-start(f32[1,4,4,1,8,256]{5,0,4,2,1,3:T(1,128)S(1)} %slice.376), channel_id=1, source_target_pairs={{0,4},{4,8},{8,12},{12,16},{16,20},{20,24},{24,28},{28,0},{1,5},{5... | collective-permute-start | bytes 393224 | tf_op jit(solution)/shard_map/ppermute | solution.py:21
  189.9 6.6 %collective-permute-start.10 = (f32[1,4,4,1,8,256]{5,0,4,2,1,3:T(1,128)S(1)}, f32[1,4,4,1,8,256]{5,0,4,2,1,3:T(1,128)S(1)}, u32[]{:S(2)}, u32[]{:S(2)}) collective-permute-start(f32[1,4,4,1,8,256]{5,0,4,2,1,3:T(1,128)S(1)} %slice.378), channel_id=1, source_target_pairs={{0,28},{4,0},{8,4},{12,8},{16,12},{20,16},{24,20},{28,24},{1,29},{... | collective-permute-start | bytes 393224 | tf_op jit(solution)/shard_map/ppermute | solution.py:21
  196.5 3.1 collective-permute-start.11
  213.9 5.1 %collective-permute-start.12 = (f32[5,1,4,1,1,256]{5,0,4,2,1,3:T(8,128)S(1)}, f32[5,1,4,1,1,256]{5,0,4,2,1,3:T(8,128)S(1)}, u32[]{:S(2)}, u32[]{:S(2)}) collective-permute-start(f32[5,1,4,1,1,256]{5,0,4,2,1,3:T(8,128)S(1)} %pad_maximum_fusion.30), channel_id=1, source_target_pairs={{0,1},{1,2},{2,3},{4,5},{5,6},{6,7},{8,9},{9,10},{10,11},{12,13},{... | collective-permute-start | bytes 61448 | tf_op jit(solution)/shard_map/ppermute | solution.py:15
  219.3 9.2 %collective-permute-start.13 = (f32[1,4,4,1,8,256]{5,0,4,2,1,3:T(1,128)S(1)}, f32[1,4,4,1,8,256]{5,0,4,2,1,3:T(1,128)S(1)}, u32[]{:S(2)}, u32[]{:S(2)}) collective-permute-start(f32[1,4,4,1,8,256]{5,0,4,2,1,3:T(1,128)S(1)} %slice.384), channel_id=1, source_target_pairs={{0,4},{4,8},{8,12},{12,16},{16,20},{20,24},{24,28},{28,0},{1,5},{5... | collective-permute-start | bytes 393224 | tf_op jit(solution)/shard_map/ppermute | solution.py:21
  221.1 51.7 %copy-start.2 = (f32[3,4,4,1,8,256]{5,0,4,2,1,3:T(4,128)}, f32[3,4,4,1,8,256]{5,0,4,2,1,3:T(4,128)S(1)}, u32[]{:S(2)}) copy-start(f32[3,4,4,1,8,256]{5,0,4,2,1,3:T(4,128)S(1)} %slice.385) | copy-start | bytes 1179652
  228.6 0.7 copy-start.6
  275.4 37.4 %copy-start.1 = (f32[4,4,4,1,8,256]{5,0,4,2,1,3:T(4,128)}, f32[4,4,4,1,8,256]{5,0,4,2,1,3:T(4,128)S(1)}, u32[]{:S(2)}) copy-start(f32[4,4,4,1,8,256]{5,0,4,2,1,3:T(4,128)S(1)} %get-tuple-element.15) | copy-start | bytes 1572868
  275.6 5.8 %collective-permute-start.14 = (f32[1,4,4,1,8,256]{5,0,4,2,1,3:T(1,128)S(1)}, f32[1,4,4,1,8,256]{5,0,4,2,1,3:T(1,128)S(1)}, u32[]{:S(2)}, u32[]{:S(2)}) collective-permute-start(f32[1,4,4,1,8,256]{5,0,4,2,1,3:T(1,128)S(1)} %slice.386), channel_id=1, source_target_pairs={{0,28},{4,0},{8,4},{12,8},{16,12},{20,16},{24,20},{28,24},{1,29},{... | collective-permute-start | bytes 393224 | tf_op jit(solution)/shard_map/ppermute | solution.py:21
  281.4 3.1 collective-permute-start.15
  298.8 5.0 %collective-permute-start.16 = (f32[5,1,4,1,1,256]{5,0,4,2,1,3:T(8,128)S(1)}, f32[5,1,4,1,1,256]{5,0,4,2,1,3:T(8,128)S(1)}, u32[]{:S(2)}, u32[]{:S(2)}) collective-permute-start(f32[5,1,4,1,1,256]{5,0,4,2,1,3:T(8,128)S(1)} %pad_maximum_fusion.28), channel_id=1, source_target_pairs={{0,1},{1,2},{2,3},{4,5},{5,6},{6,7},{8,9},{9,10},{10,11},{12,13},{... | collective-permute-start | bytes 61448 | tf_op jit(solution)/shard_map/ppermute | solution.py:15
  304.1 8.6 %collective-permute-start.17 = (f32[1,4,4,1,8,256]{5,0,4,2,1,3:T(1,128)S(1)}, f32[1,4,4,1,8,256]{5,0,4,2,1,3:T(1,128)S(1)}, u32[]{:S(2)}, u32[]{:S(2)}) collective-permute-start(f32[1,4,4,1,8,256]{5,0,4,2,1,3:T(1,128)S(1)} %slice.392), channel_id=1, source_target_pairs={{0,4},{4,8},{8,12},{12,16},{16,20},{20,24},{24,28},{28,0},{1,5},{5... | collective-permute-start | bytes 393224 | tf_op jit(solution)/shard_map/ppermute | solution.py:21
  368.6 15.8 %copy-start.5 = (f32[1,4,8,4,256,4]{4,1,2,5,3,0:T(4,128)S(1)}, f32[1,4,8,4,256,4]{4,1,2,5,3,0:T(4,128)}, u32[]{:S(2)}) copy-start(f32[1,4,8,4,256,4]{4,1,2,5,3,0:T(4,128)} %get-tuple-element.33) | copy-start | bytes 1572868
where the time goes:
time: 413 us; the launch traced here: 409 us
  blocking collectives  114 us (28%)
  local copies, waits for them, and re-layouts  111 us (27%)
  matrix products  63.2 us (15%)
  waiting for transfers between devices  52 us (13%)
  starting transfers between devices  38.9 us (9%)
  other arithmetic  18.1 us (4%)
  between operations  11.3 us (3%)
    psum x3, blocking collectives, paired_sums(): lax.psum((jnp.sum(residual * smoothed), jnp.sum(applied * smoothed)), ('g...  114 us
    reshape x4, local copies, waits for them, and re-layouts, to_blocks(): shaped = field.reshape(rows_x // 4, 4, rows_r // 4, 4, rows_y // 4, 4)  58.2 us
    ppermute x9, waiting for transfers between devices, passed_along_2(): return lax.ppermute(value, axis, pairs)  42.6 us
    reshape x2, local copies, waits for them, and re-layouts, from_blocks(): blocks.transpose(3, 0, 4, 1, 5, 2)  31.5 us
    dot_general x4, matrix products, apply_elements(): jnp.einsum('pa,pbcxyz->abcxyz', derivative, grad_x * quad_weight * metric...  23.5 us
    ppermute x9, starting transfers between devices, passed_along(): return lax.ppermute(block, axis, route)  22.1 us
    transpose x2, local copies, waits for them, and re-layouts, from_blocks(): blocks.transpose(3, 0, 4, 1, 5, 2)  18.1 us
    ppermute x9, starting transfers between devices, passed_along_2(): return lax.ppermute(value, axis, pairs)  16.8 us
  transfers between devices with their start and end apart: 18, of which 16 were waited for; matrix products, arithmetic and copies ran while one was open for 8% of the time, Pallas kernels for 0%

commit v1 on v0

v1 whole, which is shorter than its diff:
```python
import math

import jax
import jax.numpy as jnp
import numpy as np
from jax import lax
from jax.experimental import pallas as pl
from jax.experimental.pallas import tpu as pltpu
from jax.sharding import PartitionSpec as P

F32 = jnp.float32
BF16 = jnp.bfloat16
LANES = 128
ROWS = 8
SHIFT = 1.145
DOTS = 6


def gll_tables():
    root = math.sqrt(3.0 / 7.0)
    points = np.array([-1.0, -root, 0.0, root, 1.0])
    weights = np.array([0.1, 49.0 / 90.0, 32.0 / 45.0, 49.0 / 90.0, 0.1])
    factor = np.array(
        [np.prod([points[a] - points[m] for m in range(5) if m != a]) for a in range(5)]
    )
    derivative = np.zeros((5, 5))
    for p in range(5):
        for a in range(5):
            if p == a:
                derivative[p, a] = np.sum(
                    [1.0 / (points[a] - points[m]) for m in range(5) if m != a]
                )
            else:
                derivative[p, a] = factor[p] / (factor[a] * (points[p] - points[a]))
    return derivative, weights


DERIVATIVE, WEIGHTS = gll_tables()
STIFF = DERIVATIVE.T @ np.diag(WEIGHTS) @ DERIVATIVE
K = [[float(v) for v in row] for row in STIFF]
W = [float(v) for v in WEIGHTS]


def line_operator(u):
    u0, u1, u2, u3, u4 = u
    s = u0 if u4 is None else u0 + u4
    o0 = u0 if u4 is None else u0 - u4
    t = u1 + u3
    o1 = u1 - u3
    q = u2 + u2
    d0 = s - q
    d1 = t - q
    e0 = (0.5 * (K[0][0] + K[0][4])) * d0 + (0.5 * (K[0][1] + K[0][3])) * d1
    e1 = (0.5 * (K[1][0] + K[1][4])) * d0 + (0.5 * (K[1][1] + K[1][3])) * d1
    p0 = (0.5 * (K[0][0] - K[0][4])) * o0 + (0.5 * (K[0][1] - K[0][3])) * o1
    p1 = (0.5 * (K[1][0] - K[1][4])) * o0 + (0.5 * (K[1][1] - K[1][3])) * o1
    e = e0 + e1
    return e0 + p0, e1 + p1, -(e + e), e1 - p1, e0 - p0


def last_row(u):
    return K[4][0] * u[0] + K[4][1] * u[1] + K[4][2] * u[2] + K[4][3] * u[3]


class Shape:
    def __init__(self, count_r, count_y):
        self.rows = count_r
        self.halves = count_y // LANES
        self.wide = 4 * LANES

    def row(self, index):
        return pl.ds(self.rows * index, self.rows)

    def lane(self, h, c):
        return pl.ds(self.wide * h + LANES * c, LANES)

    def half(self, h):
        return pl.ds(LANES * h, LANES)


def row_index(g):
    return lax.broadcasted_iota(jnp.int32, (g.rows, LANES), 0)


def lane_index(g):
    return lax.broadcasted_iota(jnp.int32, (g.rows, LANES), 1)


def next_lane(parts, lanes):
    rolled = [pltpu.roll(p, LANES - 1, 1) for p in parts]
    n = len(parts)
    return [jnp.where(lanes == LANES - 1, rolled[(h + 1) % n], rolled[h]) for h in range(n)]


def prev_lane(parts, lanes):
    rolled = [pltpu.roll(p, 1, 1) for p in parts]
    n = len(parts)
    return [jnp.where(lanes == 0, rolled[(h - 1) % n], rolled[h]) for h in range(n)]


def next_row(g, value, rows, last):
    return jnp.where(rows == g.rows - 1, last, pltpu.roll(value, g.rows - 1, 0))


def prev_row(value, rows, first):
    return jnp.where(rows == 0, first, pltpu.roll(value, 1, 0))


def permutation():
    source = lax.broadcasted_iota(jnp.int32, (4 * LANES, 4 * LANES), 0)
    target = lax.broadcasted_iota(jnp.int32, (4 * LANES, 4 * LANES), 1)
    wanted = (target % LANES) * 4 + target // LANES
    return jnp.where(source == wanted, 1.0, 0.0).astype(BF16)


def exact_dot(values, matrix, dims):
    one = values.astype(BF16)
    rest = values - one.astype(F32)
    two = rest.astype(BF16)
    three = (rest - two.astype(F32)).astype(BF16)
    dot = lambda v: lax.dot_general(v, matrix, (dims, ((), ())), preferred_element_type=F32)
    return (dot(one) + dot(two)) + dot(three)


def local_apply(g, u_ref, cx, cxp, cr, crp, cy, v_ref):
    rows = row_index(g)
    lanes = lane_index(g)
    for ab in range(16):
        u = [[u_ref[g.row(ab), g.lane(h, c)] for c in range(4)] for h in range(g.halves)]
        fifth = next_lane([u[h][0] for h in range(g.halves)], lanes)
        ends = []
        outs = []
        for h in range(g.halves):
            coef = cy[g.row(ab), g.half(h)]
            r = line_operator(u[h] + [fifth[h]])
            outs.append([coef * r[c] for c in range(4)])
            ends.append(coef * r[4])
        ends = prev_lane(ends, lanes)
        for h in range(g.halves):
            outs[h][0] = outs[h][0] + ends[h]
            for c in range(4):
                v_ref[g.row(ab), g.lane(h, c)] = outs[h][c]
    for h in range(g.halves):
        for c in range(4):
            at = g.lane(h, c)
            u = [[u_ref[g.row(4 * a + b), at] for b in range(4)] for a in range(4)]
            v = [[v_ref[g.row(4 * a + b), at] for b in range(4)] for a in range(4)]
            for b in range(4):
                coef = cx[g.row(b), at]
                r = line_operator([u[a][b] for a in range(4)] + [None])
                for a in range(4):
                    v[a][b] = v[a][b] + coef * r[a]
                v[0][b] = v[0][b] + K[4][4] * (cxp[g.row(b), at] * u[0][b])
            for a in range(4):
                coef = cr[g.row(a), at]
                r = line_operator(u[a] + [next_row(g, u[a][0], rows, 0.0)])
                for b in range(4):
                    v[a][b] = v[a][b] + coef * r[b]
                v[a][0] = v[a][0] + prev_row(coef * r[4], rows, 0.0)
                v[a][0] = v[a][0] + K[4][4] * (crp[g.row(a), at] * u[a][0])
            for a in range(4):
                for b in range(4):
                    v_ref[g.row(4 * a + b), at] = v[a][b]


def add_halo(g, v, coef_x, coef_r, above_x, below_x, above_r, below_r, rows):
    for b in range(4):
        reach = coef_x[b] * above_x[b]
        for a in range(4):
            v[a][b] = v[a][b] + K[a][4] * reach
        v[0][b] = v[0][b] + below_x[b]
    for a in range(4):
        reach = jnp.where(rows == g.rows - 1, coef_r[a] * above_r[a], 0.0)
        for b in range(4):
            v[a][b] = v[a][b] + K[b][4] * reach
        v[a][0] = v[a][0] + jnp.where(rows == 0, below_r[a], 0.0)


def send_planes(g, z, at, h, c, coef_x, coef_r, even_x, even_r, out):
    p1, p2, p3, p4 = out
    for b in range(4):
        down = z[0][b]
        up = coef_x[b] * last_row([z[a][b] for a in range(4)])
        p1[g.row(b), at] = jnp.where(even_x, up, down)
        p2[g.row(b), at] = jnp.where(even_x, down, up)
    for a in range(4):
        down = z[a][0][0:1]
        up = (coef_r[a] * last_row(z[a]))[g.rows - 1 :]
        p3[pl.ds(4 * a + c, 1), g.half(h)] = jnp.where(even_r, up, down)
        p4[pl.ds(4 * a + c, 1), g.half(h)] = jnp.where(even_r, down, up)


def positions():
    ix = lax.axis_index("group")
    ir = lax.axis_index("rad")
    top = ir == lax.axis_size("rad") - 1
    return ix % 2 == 0, ir % 2 == 0, ir == 0, top


def start_kernel(g):
    def body(x_hbm, m_hbm, x_ref, m_ref, p1, p2, p3, p4, corner, sems):
        copies = [pltpu.make_async_copy(x_hbm.at[a], x_ref.at[a], sems.at[a]) for a in range(4)]
        copies.append(pltpu.make_async_copy(m_hbm, m_ref, sems.at[4]))
        for copy in copies:
            copy.start()
        even_x, even_r, _, _ = positions()
        last = g.rows - 1
        n = 4 * g.rows
        span = LANES * g.halves
        corner[...] = jnp.zeros_like(corner)
        p3[...] = jnp.zeros_like(p3)
        p4[...] = jnp.zeros_like(p4)
        for copy in copies:
            copy.wait()
        down = x_ref[0]
        up = last_row([x_ref[a] for a in range(4)])
        p1[0:n] = jnp.where(even_x, up, down)
        p2[0:n] = jnp.where(even_x, down, up)
        for k in range(3):
            m = m_ref[k, 0]
            p1[pl.ds(n, g.rows), pl.ds(span * k, span)] = m
            p2[pl.ds(n, g.rows), pl.ds(span * k, span)] = m
            edge = m[last:]
            corner[pl.ds(k, 1), :] = edge
            p3[pl.ds(4, 1), pl.ds(span * k, span)] = edge
            p4[pl.ds(4, 1), pl.ds(span * k, span)] = edge
        p1[pl.ds(n, g.rows), pl.ds(span * 3, span)] = m
        p2[pl.ds(n, g.rows), pl.ds(span * 3, span)] = m
        for a in range(4):
            down = x_ref[a, 0:1]
            up = last_row([x_ref[a, pl.ds(4 * last + b, 1)] for b in range(4)])
            p3[pl.ds(a, 1)] = jnp.where(even_r, up, down)
            p4[pl.ds(a, 1)] = jnp.where(even_r, down, up)

    return body


def arrange_kernel(g):
    def body(x_ref, s_ref, xd, sd, matrix_ref, buffer):
        matrix = permutation()
        matrix_ref[...] = matrix
        for source, target in ((x_ref, xd), (s_ref, sd)):
            for h in range(g.halves):
                part = source[:, :, pl.ds(g.wide * h, g.wide)].reshape(16 * g.rows, g.wide)
                part = exact_dot(part, matrix, ((1,), (0,)))
                for c in range(4):
                    buffer[4 * h + c] = part[:, LANES * c : LANES * (c + 1)]
            for h in range(g.halves):
                for c in range(4):
                    for a in range(4):
                        for b in range(4):
                            pick = pl.ds(4 * g.rows * a + b, g.rows, 4)
                            target[g.row(4 * a + b), g.lane(h, c)] = buffer[4 * h + c, pick, :]

    return body


def first_kernel(g):
    def body(
        xd, sd, m_ref, matrix_ref, r1, r2, r3, r4, rc,
        cx, cxp, cr, crp, cy, inv, z_ref, p1, p2, p3, p4,
        planes, edges, vloc, buffer,
    ):
        even_x, even_r, bottom, top = positions()
        rows = row_index(g)
        lanes = lane_index(g)
        n = 4 * g.rows
        span = LANES * g.halves
        H = range(g.halves)
        matrix = matrix_ref[...]
        for h in H:
            at = pl.ds(g.wide * h, g.wide)
            one, two = r1[0:n, at], r2[0:n, at]
            both = jnp.concatenate([jnp.where(even_x, one, two), jnp.where(even_x, two, one)], 0)
            both = exact_dot(both, matrix, ((1,), (0,)))
            for c in range(4):
                buffer[4 * h + c] = both[:, LANES * c : LANES * (c + 1)]
            for c in range(4):
                for b in range(4):
                    planes[g.row(b), g.lane(h, c)] = buffer[4 * h + c, pl.ds(b, g.rows, 4), :]
                    planes[g.row(4 + b), g.lane(h, c)] = buffer[4 * h + c, pl.ds(n + b, g.rows, 4), :]
        one, two = r3[...], r4[...]
        edges[0:8] = jnp.where(even_r, one, two)
        edges[8:16] = jnp.where(even_r, two, one)
        low_all = edges[12:13, :]
        low = [[jnp.where(bottom, 0.0, low_all[:, span * k + LANES * h : span * k + LANES * (h + 1)]) for h in H] for k in range(3)]
        for h in H:
            at = pl.ds(g.wide * h, g.wide)
            edges[:, at] = exact_dot(edges[:, at], matrix, ((1,), (0,)))
        own = [[m_ref[k, 0, :, g.half(h)] for h in H] for k in range(3)]
        left = []
        for k in range(3):
            pair = []
            for h in H:
                at = pl.ds(span * k + LANES * h, LANES)
                pair.append(jnp.where(even_x, r2[pl.ds(n, g.rows), at], r1[pl.ds(n, g.rows), at]))
            left.append(pair)
        diag_low = [[jnp.where(bottom, 0.0, rc[pl.ds(k, 1), g.half(h)]) for h in H] for k in range(3)]

        def over_y(parts):
            before = prev_lane(parts, lanes)
            return [parts[h] + before[h] for h in H]

        def over_r(parts, edge):
            return [parts[h] + prev_row(parts[h], rows, edge[h]) for h in H]

        def lines_x(parts, edge):
            wide_r = over_r(parts, edge)
            return {(1, 1): parts, (1, 0): over_y(parts), (0, 1): wide_r, (0, 0): over_y(wide_r)}

        for target, table in ((cx, lines_x(own[0], low[0])), (cxp, lines_x(left[0], diag_low[0]))):
            for b in range(4):
                for c in range(4):
                    for h in H:
                        target[g.row(b), g.lane(h, c)] = (W[b] * W[c]) * table[(min(b, 1), min(c, 1))][h]
        zero = [jnp.zeros((g.rows, LANES), F32) for h in H]
        own_r = own[1]
        both_r = [own[1][h] + left[1][h] for h in H]
        table_r = {(1, 1): own_r, (1, 0): over_y(own_r), (0, 1): both_r, (0, 0): over_y(both_r)}
        own_l = [jnp.where(rows == 0, low[1][h], 0.0) for h in H]
        both_l = [jnp.where(rows == 0, low[1][h] + diag_low[1][h], 0.0) for h in H]
        table_l = {(1, 1): own_l, (1, 0): over_y(own_l), (0, 1): both_l, (0, 0): over_y(both_l)}
        for target, table in ((cr, table_r), (crp, table_l)):
            for a in range(4):
                for c in range(4):
                    for h in H:
                        target[g.row(a), g.lane(h, c)] = (W[a] * W[c]) * table[(min(a, 1), min(c, 1))][h]
        both_y = [own[2][h] + left[2][h] for h in H]
        low_y = [low[2][h] + diag_low[2][h] for h in H]
        table_y = {
            (1, 1): own[2],
            (1, 0): over_r(own[2], low[2]),
            (0, 1): both_y,
            (0, 0): over_r(both_y, low_y),
        }
        for a in range(4):
            for b in range(4):
                for h in H:
                    cy[g.row(4 * a + b), g.half(h)] = (W[a] * W[b]) * table_y[(min(a, 1), min(b, 1))][h]
        local_apply(g, xd, cx, cxp, cr, crp, cy, vloc)
        behind = {}
        for key in table_y:
            behind[key] = prev_lane(table_y[key], lanes)
        for h in H:
            for c in range(4):
                at = g.lane(h, c)
                coef_x = [cx[g.row(b), at] for b in range(4)]
                coef_r = [cr[g.row(a), at] for a in range(4)]
                v = [[vloc[g.row(4 * a + b), at] for b in range(4)] for a in range(4)]
                above_x = [planes[g.row(b), at] for b in range(4)]
                below_x = [cxp[g.row(b), at] * planes[g.row(4 + b), at] for b in range(4)]
                above_r = [jnp.where(top, 0.0, edges[pl.ds(a, 1), at]) for a in range(4)]
                below_r = [jnp.where(bottom, 0.0, crp[pl.ds(g.rows * a, 1), at] * edges[pl.ds(8 + a, 1), at]) for a in range(4)]
                add_halo(g, v, coef_x, coef_r, above_x, below_x, above_r, below_r, rows)
                z = [[None] * 4 for _ in range(4)]
                for a in range(4):
                    for b in range(4):
                        weight = W[a] * W[b]
                        key = (min(a, 1), min(b, 1))
                        diag = K[a][a] * coef_x[b] + K[b][b] * coef_r[a]
                        diag = diag + (K[c][c] * weight) * table_y[key][h]
                        if a == 0:
                            diag = diag + K[4][4] * cxp[g.row(b), at]
                        if b == 0:
                            diag = diag + K[4][4] * prev_row(coef_r[a], rows, crp[pl.ds(g.rows * a, 1), at])
                        if c == 0:
                            diag = diag + (K[4][4] * weight) * behind[key][h]
                        scale = 1.0 / diag
                        r = sd[g.row(4 * a + b), at] - v[a][b]
                        z[a][b] = scale * r
                        inv[g.row(4 * a + b), at] = scale
                        z_ref[g.row(4 * a + b), at] = z[a][b]
                send_planes(g, z, at, h, c, coef_x, coef_r, even_x, even_r, (p1, p2, p3, p4))

    return body


def restore(g, sources, targets, matrix, buffer):
    for source, target in zip(sources, targets):
        for h in range(g.halves):
            for c in range(4):
                for a in range(4):
                    for b in range(4):
                        pick = pl.ds(4 * g.rows * a + b, g.rows, 4)
                        buffer[4 * h + c, pick, :] = source[g.row(4 * a + b), g.lane(h, c)]
        for h in range(g.halves):
            part = jnp.concatenate([buffer[4 * h + c] for c in range(4)], 1)
            part = exact_dot(part, matrix, ((1,), (1,)))
            target[:, pl.ds(g.wide * h, g.wide)] = part


def inner_kernel(g, count, with_diagonal):
    def body(*refs):
        cx, cxp, cr, crp, cy, inv, matrix = refs[:7]
        many = refs[7 : 7 + count]
        v_ref, dots, z_plain = refs[7 + count : 10 + count]
        buffer = refs[-1]
        newest = many[-1]
        local_apply(g, newest, cx, cxp, cr, crp, cy, v_ref)
        totals = [jnp.zeros((g.rows, LANES), F32)] * count
        diagonal = refs[-2] if with_diagonal else None
        for ab in range(16):
            for h in range(g.halves):
                for c in range(4):
                    at = (g.row(ab), g.lane(h, c))
                    diag = 1.0 / inv[at]
                    if with_diagonal:
                        diagonal[at] = diag
                    weighted = diag * newest[at]
                    totals = [total + weighted * ref[at] for total, ref in zip(totals, many)]
        for i in range(count):
            dots[pl.ds(g.rows * i, g.rows), :] = totals[i]
        restore(g, [newest], [z_plain], matrix[...], buffer)
        if with_diagonal:
            restore(g, [diagonal], [refs[10 + count]], matrix[...], buffer)

    return body


def received(g, r1, r2, r3, r4, h, c, at, even_x, even_r, bottom, top):
    above_x, below_x, above_r, below_r = [], [], [], []
    for b in range(4):
        one, two = r1[g.row(b), at], r2[g.row(b), at]
        above_x.append(jnp.where(even_x, one, two))
        below_x.append(jnp.where(even_x, two, one))
    for a in range(4):
        one, two = r3[pl.ds(4 * a + c, 1), g.half(h)], r4[pl.ds(4 * a + c, 1), g.half(h)]
        above_r.append(jnp.where(top, 0.0, jnp.where(even_r, one, two)))
        below_r.append(jnp.where(bottom, 0.0, jnp.where(even_r, two, one)))
    return above_x, below_x, above_r, below_r


def next_kernel(g, pulls):
    def body(*refs):
        vloc, cx, cr, inv, r1, r2, r3, r4 = refs[:8]
        earlier = refs[8 : 8 + len(pulls)]
        z_ref, p1, p2, p3, p4 = refs[8 + len(pulls) :]
        even_x, even_r, bottom, top = positions()
        rows = row_index(g)
        for h in range(g.halves):
            for c in range(4):
                at = g.lane(h, c)
                coef_x = [cx[g.row(b), at] for b in range(4)]
                coef_r = [cr[g.row(a), at] for a in range(4)]
                v = [[vloc[g.row(4 * a + b), at] for b in range(4)] for a in range(4)]
                halo = received(g, r1, r2, r3, r4, h, c, at, even_x, even_r, bottom, top)
                add_halo(g, v, coef_x, coef_r, *halo, rows)
                z = [[None] * 4 for _ in range(4)]
                for a in range(4):
                    for b in range(4):
                        rw = g.row(4 * a + b)
                        value = inv[rw, at] * v[a][b]
                        for ref, pull in zip(earlier, pulls):
                            value = value - pull * ref[rw, at]
                        z[a][b] = value
                        z_ref[rw, at] = value
                send_planes(g, z, at, h, c, coef_x, coef_r, even_x, even_r, (p1, p2, p3, p4))

    return body


def last_kernel(g, devices):
    def body(vloc, cx, cr, z_ref, r1, r2, r3, r4, d0, d1, d2, v_ref, message):
        even_x, even_r, bottom, top = positions()
        rows = row_index(g)
        total = jnp.zeros((g.rows, LANES), F32)
        for h in range(g.halves):
            for c in range(4):
                at = g.lane(h, c)
                coef_x = [cx[g.row(b), at] for b in range(4)]
                coef_r = [cr[g.row(a), at] for a in range(4)]
                v = [[vloc[g.row(4 * a + b), at] for b in range(4)] for a in range(4)]
                halo = received(g, r1, r2, r3, r4, h, c, at, even_x, even_r, bottom, top)
                add_halo(g, v, coef_x, coef_r, *halo, rows)
                for a in range(4):
                    for b in range(4):
                        rw = g.row(4 * a + b)
                        v_ref[rw, at] = v[a][b]
                        total = total + z_ref[rw, at] * v[a][b]
        parts = []
        for ref in (d0, d1, d2):
            for i in range(ref.shape[0] // g.rows):
                parts.append(ref[pl.ds(g.rows * i, g.rows), :])
        parts.append(total)
        place = lax.broadcasted_iota(jnp.int32, (g.rows, LANES), 1)
        out = jnp.zeros((g.rows, LANES), F32)
        for i, part in enumerate(parts):
            out = out + jnp.where(place == i, jnp.sum(part, axis=1, keepdims=True), 0.0)
        row = jnp.sum(out, axis=0, keepdims=True)
        message[...] = jnp.broadcast_to(row, (devices, LANES))

    return body


def restore_kernel(g):
    def body(source, x_hbm, target, x_ref, buffer, sems):
        loads = [pltpu.make_async_copy(x_hbm.at[a], x_ref.at[a], sems.at[a]) for a in range(4)]
        for load in loads:
            load.start()
        restore(g, [source], [target], permutation(), buffer)
        for load in loads:
            load.wait()

    return body


def finish_kernel(g):
    def body(sums, x_ref, diag, z0, z1, z2, v3, solution_hbm, residual_hbm, solution_ref, residual_ref, sems):
        total = jnp.sum(sums[...], axis=0, keepdims=True)
        place = lax.broadcasted_iota(jnp.int32, (1, LANES), 1)
        dot = [jnp.sum(jnp.where(place == i, total, 0.0), axis=1, keepdims=True) for i in range(DOTS)]
        s00, s01, s11, s12, s22, m22 = dot
        m00 = s01 + SHIFT * s00
        m01 = s11 + SHIFT * s01
        m02 = s12 + SHIFT * s11
        m11 = m02
        m12 = s22 + SHIFT * s12
        l10 = m01 / m00
        l20 = m02 / m00
        d1 = m11 - l10 * m01
        t = m12 - l10 * m02
        l21 = t / d1
        d2 = m22 - l20 * m02 - l21 * t
        y1 = s01 - l10 * s00
        y2 = s11 - l20 * s00 - l21 * y1
        c2 = y2 / d2
        c1 = y1 / d1 - l21 * c2
        c0 = s00 / m00 - l10 * c1 - l20 * c2
        e0 = 1.0 - SHIFT * c0
        e1 = c0 + SHIFT * c1
        copies = []
        for a in range(4):
            at = pl.ds(4 * g.rows * a, 4 * g.rows)
            p0, p1, p2 = z0[at], z1[at], z2[at]
            residual_ref[a] = diag[at] * (e0 * p0 - (e1 * p1 + c1 * p2)) - c2 * v3[at]
            copies.append(pltpu.make_async_copy(residual_ref.at[a], residual_hbm.at[a], sems.at[4 + a]))
            copies[-1].start()
            solution_ref[a] = x_ref[a] + (c0 * p0 + (c1 * p1 + c2 * p2))
            copies.append(pltpu.make_async_copy(solution_ref.at[a], solution_hbm.at[a], sems.at[a]))
            copies[-1].start()
        for copy in copies:
            copy.wait()

    return body


def swaps(count, parity):
    pairs = []
    for i in range(count):
        step = 1 if i % 2 == parity else -1
        pairs.append((i, (i + step) % count))
    return pairs


VMEM = pl.BlockSpec(memory_space=pltpu.VMEM)
HBM = pl.BlockSpec(memory_space=pltpu.HBM)
MIB = 1024 * 1024


def call(body, args, outs, scratch=(), limit=6, in_specs=None, out_specs=None, aliases=None, flops=1000000):
    return pl.pallas_call(
        body,
        in_specs=in_specs or [VMEM] * len(args),
        out_specs=out_specs or [VMEM] * len(outs),
        out_shape=[jax.ShapeDtypeStruct(s, t) for s, t in outs],
        scratch_shapes=list(scratch),
        input_output_aliases=aliases or {},
        cost_estimate=pl.CostEstimate(flops=flops, bytes_accessed=1000000, transcendentals=0),
        compiler_params=pltpu.CompilerParams(vmem_limit_bytes=limit * MIB),
    )(*args)


def steps(source_term, initial_guess, metric):
    count_x, count_r, count_y = metric.shape[1:]
    assert count_x == 1 and count_r == ROWS and count_y % LANES == 0
    g = Shape(count_r, count_y)
    nx, nr = lax.axis_size("group"), lax.axis_size("rad")
    assert nx % 2 == 0 and nr % 2 == 0
    full = ((16 * count_r, 4 * count_y), F32)
    plane = ((4 * count_r, 4 * count_y), F32)
    edge = ((16, count_y), F32)
    natural = (initial_guess.shape, F32)

    def exchange(p1, p2, p3, p4):
        sends = ((p1, "group", nx, 0), (p2, "group", nx, 1), (p3, "rad", nr, 0), (p4, "rad", nr, 1))
        got = []
        for value, axis, count, parity in sends:
            got.append(lax.ppermute(value, axis, swaps(count, parity)))
        return tuple(got)

    guess = pltpu.with_memory_space_constraint(initial_guess, pltpu.HBM)
    x0, m0, p1, p2, p3, p4, corner = call(
        start_kernel(g),
        (guess, pltpu.with_memory_space_constraint(metric, pltpu.HBM)),
        [natural, (metric.shape, F32)]
        + [((5 * count_r, 4 * count_y), F32)] * 2 + [((8, 4 * count_y), F32)] * 2 + [((8, count_y), F32)],
        [pltpu.SemaphoreType.DMA((5,))],
        in_specs=[HBM, HBM],
    )
    got = exchange(p1, p2, p3, p4)
    diagonal = [
        (i * nr + j, ((i + 1) % nx) * nr + (j + 1) % nr) for i in range(nx) for j in range(nr)
    ]
    corner = lax.ppermute(corner, ("group", "rad"), diagonal)
    matrix = ((4 * LANES, 4 * LANES), BF16)
    tiles = pltpu.VMEM((4 * g.halves, 16 * count_r, LANES), F32)
    xd, sd, matrix = call(
        arrange_kernel(g),
        (x0, source_term),
        [full, full, matrix],
        [tiles],
    )
    outs = [plane, plane, plane, plane, ((16 * count_r, count_y), F32), full, full]
    outs += [plane, plane, edge, edge]
    cx, cxp, cr, crp, cy, inv, z0, *send = call(
        first_kernel(g),
        (xd, sd, m0, matrix, *got, corner),
        outs,
        [pltpu.VMEM((8 * count_r, 4 * count_y), F32), pltpu.VMEM((16, 4 * count_y), F32), pltpu.VMEM(*full), pltpu.VMEM((count_y // 32, 8 * count_r, LANES), F32)],
    )

    def inner(many, with_diagonal):
        return call(
            inner_kernel(g, len(many), with_diagonal),
            (cx, cxp, cr, crp, cy, inv, matrix, *many),
            [full, ((count_r * len(many), LANES), F32), full] + [full] * with_diagonal,
            [pltpu.VMEM(*full)] * with_diagonal + [tiles],
        )

    def step(vloc, got, earlier, pulls):
        z, *send = call(
            next_kernel(g, pulls),
            (vloc, cx, cr, inv, *got, *earlier),
            [full, plane, plane, edge, edge],
        )
        return z, send

    got = exchange(*send)
    vloc, d0, z0_n, diag_n = inner((z0,), True)
    z1, send = step(vloc, got, (z0,), (SHIFT,))
    got = exchange(*send)
    vloc, d1, z1_n = inner((z0, z1), False)
    z2, send = step(vloc, got, (z1,), (SHIFT,))
    got = exchange(*send)
    vloc, d2, z2_n = inner((z1, z2), False)
    v3, message = call(
        last_kernel(g, nx * nr),
        (vloc, cx, cr, z2, *got, d0, d1, d2),
        [full, ((nx * nr, LANES), F32)],
    )
    sums = lax.all_to_all(message, ("group", "rad"), 0, 0, tiled=True)
    v3_n, x0 = call(
        restore_kernel(g),
        (v3, guess),
        [full, natural],
        [tiles, pltpu.SemaphoreType.DMA((4,))],
        in_specs=[VMEM, HBM],
        aliases={0: 0},
    )
    return tuple(
        call(
            finish_kernel(g),
            (sums, x0, diag_n, z0_n, z1_n, z2_n, v3_n),
            [natural, natural],
            [pltpu.VMEM(*natural)] * 2 + [pltpu.SemaphoreType.DMA((8,))],
            out_specs=[HBM, HBM],
        )
    )


def solution(mesh):
    in_specs = (P("group", "rad", None), P("group", "rad", None), P(None, "group", "rad", None))
    out_specs = (P("group", "rad", None), P("group", "rad", None))
    return jax.shard_map(steps, mesh=mesh, in_specs=in_specs, out_specs=out_specs, check_vma=False)
```

time: 413 us -> 54.8 us (0.13)
  blocking collectives: 114 us -> 0 us
  local copies, waits for them, and re-layouts: 111 us -> 0.01 us
  matrix products: 63.2 us -> 0 us
  waiting for transfers between devices: 52 us -> 20.1 us
  starting transfers between devices: 38.9 us -> 20.4 us
  other arithmetic: 18.1 us -> 0 us
  Pallas kernels: 0 us -> 13.3 us
  between operations: 11.3 us -> 0.77 us
    psum x3 -> x0, blocking collectives: 114 us -> none  [paired_sums(): lax.psum((jnp.sum(residual * smoothed), jnp.sum(applied * smoothed)), ('g...]
    reshape x6 -> x0, local copies, waits for them, and re-layouts: 89.7 us -> none  [the longest x4 58.2 us: to_blocks(): shaped = field.reshape(rows_x // 4, 4, rows_r // 4, 4, rows_y // 4, 4)]
    dot_general x24 -> x0, matrix products: 63.2 us -> none  [the longest x4 23.5 us: apply_elements(): jnp.einsum('pa,pbcxyz->abcxyz', derivative, grad_x * quad_weight * metric...]
    ppermute x18 -> x17, waiting for transfers between devices: 52 us -> 14.3 us  [the longest x16 8.71 us: exchange(): got.append(lax.ppermute(value, axis, swaps(count, parity)))]
    ppermute x18 -> x17, starting transfers between devices: 38.9 us -> 17.7 us  [the longest x16 17.7 us: exchange(): got.append(lax.ppermute(value, axis, swaps(count, parity)))]
    transpose x2 -> x0, local copies, waits for them, and re-layouts: 18.1 us -> none  [from_blocks(): blocks.transpose(3, 0, 4, 1, 5, 2)]
    pallas_call x0 -> x11, Pallas kernels: none -> 13.3 us  [call(): pl.pallas_call(body, in_specs=in_specs or [VMEM] * len(args), out_specs=o...]
    all_to_all x0 -> x1, waiting for transfers between devices: none -> 5.85 us  [steps(): sums = lax.all_to_all(message, ('group', 'rad'), 0, 0, tiled=True)]
  transfers between devices with their start and end apart: 18 -> 18, of which waited for: 16 -> 9; matrix products, arithmetic and copies ran while one was open for 8% -> 0% of each run, Pallas kernels for 0% -> 14%
where the time goes in v1:
time: 54.8 us; the launch traced here: 54.6 us
  starting transfers between devices  20.4 us (37%)
  waiting for transfers between devices  20.1 us (37%)
  Pallas kernels  13.3 us (24%)
  between operations  0.77 us (1%)
    ppermute x16, starting transfers between devices, exchange(): got.append(lax.ppermute(value, axis, swaps(count, parity)))  17.7 us
    pallas_call x11, Pallas kernels, call(): pl.pallas_call(body, in_specs=in_specs or [VMEM] * len(args), out_specs=o...  13.3 us
    ppermute x16, waiting for transfers between devices, exchange(): got.append(lax.ppermute(value, axis, swaps(count, parity)))  8.71 us
    all_to_all x1, waiting for transfers between devices, steps(): sums = lax.all_to_all(message, ('group', 'rad'), 0, 0, tiled=True)  5.85 us
    ppermute x1, waiting for transfers between devices, steps(): corner = lax.ppermute(corner, ('group', 'rad'), diagonal)  5.54 us
    all_to_all x1, starting transfers between devices, steps(): sums = lax.all_to_all(message, ('group', 'rad'), 0, 0, tiled=True)  2.74 us
  transfers between devices with their start and end apart: 18, of which 9 were waited for; matrix products, arithmetic and copies ran while one was open for 0% of the time, Pallas kernels for 14%

profile of v1, /device:TPU:0, one launch (start us, length us, event | category | flops | bytes accessed | tf_op | source)
XLA Modules:
  0.0 54.6 jit_solution(7558204913439191712)
XLA Ops:
  0.6 0.0 copy-start
  0.6 1.3 %shard_map.50 = (f32[4,32,1024]{2,1,0:T(8,128)S(1)}, f32[3,1,8,256]{3,2,1,0:T(8,128)S(1)}, f32[40,1024]{1,0:T(8,128)S(1)}, f32[40,1024]{1,0:T(8,128)S(1)}, f32[8...) custom-call(f32[4,32,1024]{2,1,0:T(8,128)} %x_hbm.3, f32[3,1,8,256]{3,2,1,0:T(8,128)} %m_hbm.1), custom_call_target="tpu_custom_call" | custom-call | flops 1000000 | bytes 1000000 | tf_op jit(solution)/shard_map/pallas_call | solution.py:561
  1.9 3.0 %collective-permute-start = (f32[40,1024]{1,0:T(8,128)S(1)}, f32[40,1024]{1,0:T(8,128)S(1)}, u32[]{:S(2)}, u32[]{:S(2)}) collective-permute-start(f32[40,1024]{1,0:T(8,128)S(1)} %get-tuple-element.52), channel_id=1, source_target_pairs={{0,4},{4,0},{8,12},{12,8},{16,20},{20,16},{24,28},{28,24},{1,5},{5... | collective-permute-start | bytes 491528 | tf_op jit(solution)/shard_map/ppermute | solution.py:588
  4.9 3.6 %collective-permute-start.1 = (f32[40,1024]{1,0:T(8,128)S(1)}, f32[40,1024]{1,0:T(8,128)S(1)}, u32[]{:S(2)}, u32[]{:S(2)}) collective-permute-start(f32[40,1024]{1,0:T(8,128)S(1)} %get-tuple-element.53), channel_id=1, source_target_pairs={{0,28},{4,8},{8,4},{12,16},{16,12},{20,24},{24,20},{28,0},{1,29},{... | collective-permute-start | bytes 491528 | tf_op jit(solution)/shard_map/ppermute | solution.py:588
  8.5 0.0 collective-permute-start.2
  8.5 1.6 %collective-permute-start.3 = (f32[8,1024]{1,0:T(8,128)S(1)}, f32[8,1024]{1,0:T(8,128)S(1)}, u32[]{:S(2)}, u32[]{:S(2)}) collective-permute-start(f32[8,1024]{1,0:T(8,128)S(1)} %get-tuple-element.55), channel_id=1, source_target_pairs={{0,3},{1,2},{2,1},{3,0},{4,7},{5,6},{6,5},{7,4},{8,11},{9,10},{10,... | collective-permute-start | bytes 98312 | tf_op jit(solution)/shard_map/ppermute | solution.py:588
  10.2 0.0 collective-permute-start.4
  10.2 0.0 copy-done
  10.2 1.1 %shard_map.51 = (f32[128,1024]{1,0:T(8,128)S(1)}, f32[128,1024]{1,0:T(8,128)S(1)}, bf16[512,512]{1,0:T(8,128)(2,1)S(1)}) custom-call(f32[4,32,1024]{2,1,0:T(8,128)S(1)} %get-tuple-element.47.x_ref, f32[4,32,1024]{2,1,0:T(8,128)S(1)} %copy-done), custom_call_target="tpu_custom_call" | custom-call | flops 1000000 | bytes 1000000 | tf_op jit(solution)/shard_map/pallas_call | solution.py:561
  11.3 5.5 %collective-permute-done.4.rc = f32[8,256]{1,0:T(8,128)S(1)} collective-permute-done((f32[8,256]{1,0:T(8,128)S(1)}, f32[8,256]{1,0:T(8,128)S(1)}, u32[]{:S(2)}, u32[]{:S(2)}) %collective-permute-start.4) | collective-permute-done | bytes 8224 | tf_op jit(solution)/shard_map/ppermute | solution.py:604
  16.8 0.0 collective-permute-done.2.r3
  16.8 0.0 collective-permute-done.3.r4
  16.8 0.0 collective-permute-done.r1
  16.8 0.0 collective-permute-done.1.r2
  16.8 1.5 %shard_map.52 = (f32[32,1024]{1,0:T(8,128)S(1)}, f32[32,1024]{1,0:T(8,128)S(1)}, f32[32,1024]{1,0:T(8,128)S(1)}, f32[32,1024]{1,0:T(8,128)S(1)}, f32[128,256]{1,...) custom-call(f32[128,1024]{1,0:T(8,128)S(1)} %get-tuple-element.48.xd, ...), custom_call_target="tpu_custom_call" | custom-call | flops 1000000 | bytes 1000000 | tf_op jit(solution)/shard_map/pallas_call | solution.py:561
  18.4 0.1 collective-permute-start.5
  18.5 1.3 %collective-permute-start.6 = (f32[32,1024]{1,0:T(8,128)S(1)}, f32[32,1024]{1,0:T(8,128)S(1)}, u32[]{:S(2)}, u32[]{:S(2)}) collective-permute-start(f32[32,1024]{1,0:T(8,128)S(1)} %get-tuple-element.66), channel_id=1, source_target_pairs={{0,28},{4,8},{8,4},{12,16},{16,12},{20,24},{24,20},{28,0},{1,29},{... | collective-permute-start | bytes 393224 | tf_op jit(solution)/shard_map/ppermute | solution.py:588
  19.8 0.0 collective-permute-start.7
  19.8 1.6 %collective-permute-start.8 = (f32[16,256]{1,0:T(8,128)S(1)}, f32[16,256]{1,0:T(8,128)S(1)}, u32[]{:S(2)}, u32[]{:S(2)}) collective-permute-start(f32[16,256]{1,0:T(8,128)S(1)} %get-tuple-element.68), channel_id=1, source_target_pairs={{0,3},{1,2},{2,1},{3,0},{4,7},{5,6},{6,5},{7,4},{8,11},{9,10},{10,... | collective-permute-start | bytes 49160 | tf_op jit(solution)/shard_map/ppermute | solution.py:588
  21.4 2.4 %shard_map.53 = (f32[128,1024]{1,0:T(8,128)S(1)}, f32[8,128]{1,0:T(8,128)S(1)}, f32[128,1024]{1,0:T(8,128)S(1)}, f32[128,1024]{1,0:T(8,128)S(1)}) custom-call(f32[32,1024]{1,0:T(8,128)S(1)} %get-tuple-element.57.refs_0_.refs_1_.cx, f32[32,1024]{1,0:T(8,128)S(1)} %get-tuple-element.58.refs_1_, f32[32,1024]{1,0:T(8,128)S(1)} %get-tuple-element.59.refs_2_.cr, ...), custom_call_target="tpu_custom_call" | custom-call | flops 1000000 | bytes 1000000 | tf_op jit(solution)/shard_map/pallas_call | solution.py:561
  23.8 0.0 collective-permute-done.7.refs_6_
  23.8 0.0 collective-permute-done.8.refs_7_
  23.8 2.4 %collective-permute-done.5.refs_4_ = f32[32,1024]{1,0:T(8,128)S(1)} collective-permute-done((f32[32,1024]{1,0:T(8,128)S(1)}, f32[32,1024]{1,0:T(8,128)S(1)}, u32[]{:S(2)}, u32[]{:S(2)}) %collective-permute-start.5) | collective-permute-done | bytes 131104 | tf_op jit(solution)/shard_map/ppermute | solution.py:588
  26.2 0.0 collective-permute-done.6.refs_5_
  26.2 0.3 shard_map.54
  26.6 0.2 collective-permute-start.9
  26.8 1.4 %collective-permute-start.10 = (f32[32,1024]{1,0:T(8,128)S(1)}, f32[32,1024]{1,0:T(8,128)S(1)}, u32[]{:S(2)}, u32[]{:S(2)}) collective-permute-start(f32[32,1024]{1,0:T(8,128)S(1)} %get-tuple-element.72), channel_id=1, source_target_pairs={{0,28},{4,8},{8,4},{12,16},{16,12},{20,24},{24,20},{28,0},{1,29},{... | collective-permute-start | bytes 393224 | tf_op jit(solution)/shard_map/ppermute | solution.py:588
  28.2 0.0 collective-permute-start.11
  28.2 1.6 %collective-permute-start.12 = (f32[16,256]{1,0:T(8,128)S(1)}, f32[16,256]{1,0:T(8,128)S(1)}, u32[]{:S(2)}, u32[]{:S(2)}) collective-permute-start(f32[16,256]{1,0:T(8,128)S(1)} %get-tuple-element.74), channel_id=1, source_target_pairs={{0,3},{1,2},{2,1},{3,0},{4,7},{5,6},{6,5},{7,4},{8,11},{9,10},{10,... | collective-permute-start | bytes 49160 | tf_op jit(solution)/shard_map/ppermute | solution.py:588
  29.8 1.4 %shard_map.55 = (f32[128,1024]{1,0:T(8,128)S(1)}, f32[16,128]{1,0:T(8,128)S(1)}, f32[128,1024]{1,0:T(8,128)S(1)}) custom-call(f32[32,1024]{1,0:T(8,128)S(1)} %get-tuple-element.57.refs_0_.refs_1_.cx, f32[32,1024]{1,0:T(8,128)S(1)} %get-tuple-element.58.refs_1_, f32[32,1024]{1,0:T(8,128)S(1)} %get-tuple-element.59.refs_2_.cr, ...), custom_call_target="tpu_custom_call" | custom-call | flops 1000000 | bytes 1000000 | tf_op jit(solution)/shard_map/pallas_call | solution.py:561
  31.3 0.0 collective-permute-done.11.refs_6_
  31.3 0.1 collective-permute-done.12.refs_7_
  31.3 1.5 %collective-permute-done.9.refs_4_ = f32[32,1024]{1,0:T(8,128)S(1)} collective-permute-done((f32[32,1024]{1,0:T(8,128)S(1)}, f32[32,1024]{1,0:T(8,128)S(1)}, u32[]{:S(2)}, u32[]{:S(2)}) %collective-permute-start.9) | collective-permute-done | bytes 131104 | tf_op jit(solution)/shard_map/ppermute | solution.py:588
  32.8 1.6 %collective-permute-done.10.refs_5_ = f32[32,1024]{1,0:T(8,128)S(1)} collective-permute-done((f32[32,1024]{1,0:T(8,128)S(1)}, f32[32,1024]{1,0:T(8,128)S(1)}, u32[]{:S(2)}, u32[]{:S(2)}) %collective-permute-start.10) | collective-permute-done | bytes 131104 | tf_op jit(solution)/shard_map/ppermute | solution.py:588
  34.4 0.3 shard_map.56
  34.8 0.2 collective-permute-start.13
  34.9 1.6 %collective-permute-start.14 = (f32[32,1024]{1,0:T(8,128)S(1)}, f32[32,1024]{1,0:T(8,128)S(1)}, u32[]{:S(2)}, u32[]{:S(2)}) collective-permute-start(f32[32,1024]{1,0:T(8,128)S(1)} %get-tuple-element.78), channel_id=1, source_target_pairs={{0,28},{4,8},{8,4},{12,16},{16,12},{20,24},{24,20},{28,0},{1,29},{... | collective-permute-start | bytes 393224 | tf_op jit(solution)/shard_map/ppermute | solution.py:588
  36.6 0.0 collective-permute-start.15
  36.6 1.4 %collective-permute-start.16 = (f32[16,256]{1,0:T(8,128)S(1)}, f32[16,256]{1,0:T(8,128)S(1)}, u32[]{:S(2)}, u32[]{:S(2)}) collective-permute-start(f32[16,256]{1,0:T(8,128)S(1)} %get-tuple-element.80), channel_id=1, source_target_pairs={{0,3},{1,2},{2,1},{3,0},{4,7},{5,6},{6,5},{7,4},{8,11},{9,10},{10,... | collective-permute-start | bytes 49160 | tf_op jit(solution)/shard_map/ppermute | solution.py:588
  38.0 1.4 %shard_map.57 = (f32[128,1024]{1,0:T(8,128)S(1)}, f32[16,128]{1,0:T(8,128)S(1)}, f32[128,1024]{1,0:T(8,128)S(1)}) custom-call(f32[32,1024]{1,0:T(8,128)S(1)} %get-tuple-element.57.refs_0_.refs_1_.cx, f32[32,1024]{1,0:T(8,128)S(1)} %get-tuple-element.58.refs_1_, f32[32,1024]{1,0:T(8,128)S(1)} %get-tuple-element.59.refs_2_.cr, ...), custom_call_target="tpu_custom_call" | custom-call | flops 1000000 | bytes 1000000 | tf_op jit(solution)/shard_map/pallas_call | solution.py:561
  39.5 0.0 collective-permute-done.15.r3
  39.5 0.3 collective-permute-done.16.r4
  39.7 1.2 %collective-permute-done.13.r1 = f32[32,1024]{1,0:T(8,128)S(1)} collective-permute-done((f32[32,1024]{1,0:T(8,128)S(1)}, f32[32,1024]{1,0:T(8,128)S(1)}, u32[]{:S(2)}, u32[]{:S(2)}) %collective-permute-start.13) | collective-permute-done | bytes 131104 | tf_op jit(solution)/shard_map/ppermute | solution.py:588
  40.9 1.7 %collective-permute-done.14.r2 = f32[32,1024]{1,0:T(8,128)S(1)} collective-permute-done((f32[32,1024]{1,0:T(8,128)S(1)}, f32[32,1024]{1,0:T(8,128)S(1)}, u32[]{:S(2)}, u32[]{:S(2)}) %collective-permute-start.14) | collective-permute-done | bytes 131104 | tf_op jit(solution)/shard_map/ppermute | solution.py:588
  42.6 0.9 %shard_map.58 = (f32[128,1024]{1,0:T(8,128)S(1)}, f32[32,128]{1,0:T(8,128)}) custom-call(f32[128,1024]{1,0:T(8,128)S(1)} %get-tuple-element.76.vloc, f32[32,1024]{1,0:T(8,128)S(1)} %get-tuple-element.57.refs_0_.refs_1_.cx, f32[32,1024]{1,0:T(8,128)S(1)} %get-tuple-element.59.refs_2_.cr, f32[128,1024]{1,0:T(8,128)S(1)} %get-tuple-element.75.refs_8_.z_ref, ...), custom_call_target="tpu_custom_call" | custom-call | flops 1000000 | bytes 1000000 | tf_op jit(solution)/shard_map/pallas_call | solution.py:561
  43.5 2.7 %all-to-all-start = ((f32[32,1,128]{2,1,0:T(1,128)}), f32[32,1,128]{2,1,0:T(1,128)S(1)}, u32[]{:S(2)}, u32[]{:S(2)}) async-start(f32[32,1,128]{2,1,0:T(1,128)} %bitcast.1), calls=%async_computation | async-start | bytes 32768 | tf_op jit(solution)/shard_map/all_to_all | solution.py:651
  46.3 1.2 %shard_map.59 = (f32[128,1024]{1,0:T(8,128)S(1)}, f32[4,32,1024]{2,1,0:T(8,128)S(1)}) custom-call(f32[128,1024]{1,0:T(8,128)S(1)} %get-tuple-element.85.source, f32[4,32,1024]{2,1,0:T(8,128)} %x_hbm.3), custom_call_target="tpu_custom_call", output_to_operand_aliasing={{0}: (0, {})} | custom-call | flops 1000000 | bytes 1000000 | tf_op jit(solution)/shard_map/pallas_call | solution.py:561
  47.5 5.8 %all-to-all-done = f32[32,1,128]{2,1,0:T(1,128)S(1)} async-done(((f32[32,1,128]{2,1,0:T(1,128)}), f32[32,1,128]{2,1,0:T(1,128)S(1)}, u32[]{:S(2)}, u32[]{:S(2)}) %all-to-all-start) | async-done | bytes 16416 | tf_op jit(solution)/shard_map/all_to_all | solution.py:651
  53.4 1.3 %shard_map.60 = (f32[4,32,1024]{2,1,0:T(8,128)}, f32[4,32,1024]{2,1,0:T(8,128)}) custom-call(f32[32,128]{1,0:T(8,128)S(1)} %bitcast.4, f32[4,32,1024]{2,1,0:T(8,128)S(1)} %get-tuple-element.86.x_ref, f32[128,1024]{1,0:T(8,128)S(1)} %get-tuple-element.87.diag, f32[128,1024]{1,0:T(8,128)S(1)} %get-tuple-element.88.z0, f32[128,1024]{1,0:T(8,128)S(1)} %get-tuple-element.89.z1, ...), custom_call_target="tpu_custom_call" | custom-call | flops 1000000 | bytes 1000000 | tf_op jit(solution)/shard_map/pallas_call | solution.py:561
Async XLA Ops:
  0.6 9.5 %copy-start = (f32[4,32,1024]{2,1,0:T(8,128)S(1)}, f32[4,32,1024]{2,1,0:T(8,128)}, u32[]{:S(2)}) copy-start(f32[4,32,1024]{2,1,0:T(8,128)} %s_ref.1) | copy-start | bytes 1572868
  1.9 14.9 %collective-permute-start = (f32[40,1024]{1,0:T(8,128)S(1)}, f32[40,1024]{1,0:T(8,128)S(1)}, u32[]{:S(2)}, u32[]{:S(2)}) collective-permute-start(f32[40,1024]{1,0:T(8,128)S(1)} %get-tuple-element.52), channel_id=1, source_target_pairs={{0,4},{4,0},{8,12},{12,8},{16,20},{20,16},{24,28},{28,24},{1,5},{5... | collective-permute-start | bytes 491528 | tf_op jit(solution)/shard_map/ppermute | solution.py:588
  4.9 11.9 %collective-permute-start.1 = (f32[40,1024]{1,0:T(8,128)S(1)}, f32[40,1024]{1,0:T(8,128)S(1)}, u32[]{:S(2)}, u32[]{:S(2)}) collective-permute-start(f32[40,1024]{1,0:T(8,128)S(1)} %get-tuple-element.53), channel_id=1, source_target_pairs={{0,28},{4,8},{8,4},{12,16},{16,12},{20,24},{24,20},{28,0},{1,29},{... | collective-permute-start | bytes 491528 | tf_op jit(solution)/shard_map/ppermute | solution.py:588
  8.5 8.3 %collective-permute-start.2 = (f32[8,1024]{1,0:T(8,128)S(1)}, f32[8,1024]{1,0:T(8,128)S(1)}, u32[]{:S(2)}, u32[]{:S(2)}) collective-permute-start(f32[8,1024]{1,0:T(8,128)S(1)} %get-tuple-element.54), channel_id=1, source_target_pairs={{0,1},{1,0},{2,3},{3,2},{4,5},{5,4},{6,7},{7,6},{8,9},{9,8},{10,11... | collective-permute-start | bytes 98312 | tf_op jit(solution)/shard_map/ppermute | solution.py:588
  8.5 8.3 %collective-permute-start.3 = (f32[8,1024]{1,0:T(8,128)S(1)}, f32[8,1024]{1,0:T(8,128)S(1)}, u32[]{:S(2)}, u32[]{:S(2)}) collective-permute-start(f32[8,1024]{1,0:T(8,128)S(1)} %get-tuple-element.55), channel_id=1, source_target_pairs={{0,3},{1,2},{2,1},{3,0},{4,7},{5,6},{6,5},{7,4},{8,11},{9,10},{10,... | collective-permute-start | bytes 98312 | tf_op jit(solution)/shard_map/ppermute | solution.py:588
  10.2 6.7 %collective-permute-start.4 = (f32[8,256]{1,0:T(8,128)S(1)}, f32[8,256]{1,0:T(8,128)S(1)}, u32[]{:S(2)}, u32[]{:S(2)}) collective-permute-start(f32[8,256]{1,0:T(8,128)S(1)} %get-tuple-element.56), channel_id=1, source_target_pairs={{0,5},{1,6},{2,7},{3,4},{4,9},{5,10},{6,11},{7,8},{8,13},{9,14},{1... | collective-permute-start | bytes 24584 | tf_op jit(solution)/shard_map/ppermute | solution.py:604
  18.4 7.8 %collective-permute-start.5 = (f32[32,1024]{1,0:T(8,128)S(1)}, f32[32,1024]{1,0:T(8,128)S(1)}, u32[]{:S(2)}, u32[]{:S(2)}) collective-permute-start(f32[32,1024]{1,0:T(8,128)S(1)} %get-tuple-element.65), channel_id=1, source_target_pairs={{0,4},{4,0},{8,12},{12,8},{16,20},{20,16},{24,28},{28,24},{1,5},{5... | collective-permute-start | bytes 393224 | tf_op jit(solution)/shard_map/ppermute | solution.py:588
  18.5 7.8 %collective-permute-start.6 = (f32[32,1024]{1,0:T(8,128)S(1)}, f32[32,1024]{1,0:T(8,128)S(1)}, u32[]{:S(2)}, u32[]{:S(2)}) collective-permute-start(f32[32,1024]{1,0:T(8,128)S(1)} %get-tuple-element.66), channel_id=1, source_target_pairs={{0,28},{4,8},{8,4},{12,16},{16,12},{20,24},{24,20},{28,0},{1,29},{... | collective-permute-start | bytes 393224 | tf_op jit(solution)/shard_map/ppermute | solution.py:588
  19.8 4.0 %collective-permute-start.7 = (f32[16,256]{1,0:T(8,128)S(1)}, f32[16,256]{1,0:T(8,128)S(1)}, u32[]{:S(2)}, u32[]{:S(2)}) collective-permute-start(f32[16,256]{1,0:T(8,128)S(1)} %get-tuple-element.67), channel_id=1, source_target_pairs={{0,1},{1,0},{2,3},{3,2},{4,5},{5,4},{6,7},{7,6},{8,9},{9,8},{10,11... | collective-permute-start | bytes 49160 | tf_op jit(solution)/shard_map/ppermute | solution.py:588
  19.8 4.0 %collective-permute-start.8 = (f32[16,256]{1,0:T(8,128)S(1)}, f32[16,256]{1,0:T(8,128)S(1)}, u32[]{:S(2)}, u32[]{:S(2)}) collective-permute-start(f32[16,256]{1,0:T(8,128)S(1)} %get-tuple-element.68), channel_id=1, source_target_pairs={{0,3},{1,2},{2,1},{3,0},{4,7},{5,6},{6,5},{7,4},{8,11},{9,10},{10,... | collective-permute-start | bytes 49160 | tf_op jit(solution)/shard_map/ppermute | solution.py:588
  26.6 6.3 %collective-permute-start.9 = (f32[32,1024]{1,0:T(8,128)S(1)}, f32[32,1024]{1,0:T(8,128)S(1)}, u32[]{:S(2)}, u32[]{:S(2)}) collective-permute-start(f32[32,1024]{1,0:T(8,128)S(1)} %get-tuple-element.71), channel_id=1, source_target_pairs={{0,4},{4,0},{8,12},{12,8},{16,20},{20,16},{24,28},{28,24},{1,5},{5... | collective-permute-start | bytes 393224 | tf_op jit(solution)/shard_map/ppermute | solution.py:588
  26.8 7.7 %collective-permute-start.10 = (f32[32,1024]{1,0:T(8,128)S(1)}, f32[32,1024]{1,0:T(8,128)S(1)}, u32[]{:S(2)}, u32[]{:S(2)}) collective-permute-start(f32[32,1024]{1,0:T(8,128)S(1)} %get-tuple-element.72), channel_id=1, source_target_pairs={{0,28},{4,8},{8,4},{12,16},{16,12},{20,24},{24,20},{28,0},{1,29},{... | collective-permute-start | bytes 393224 | tf_op jit(solution)/shard_map/ppermute | solution.py:588
  28.2 3.1 %collective-permute-start.11 = (f32[16,256]{1,0:T(8,128)S(1)}, f32[16,256]{1,0:T(8,128)S(1)}, u32[]{:S(2)}, u32[]{:S(2)}) collective-permute-start(f32[16,256]{1,0:T(8,128)S(1)} %get-tuple-element.73), channel_id=1, source_target_pairs={{0,1},{1,0},{2,3},{3,2},{4,5},{5,4},{6,7},{7,6},{8,9},{9,8},{10,11... | collective-permute-start | bytes 49160 | tf_op jit(solution)/shard_map/ppermute | solution.py:588
  28.2 3.2 %collective-permute-start.12 = (f32[16,256]{1,0:T(8,128)S(1)}, f32[16,256]{1,0:T(8,128)S(1)}, u32[]{:S(2)}, u32[]{:S(2)}) collective-permute-start(f32[16,256]{1,0:T(8,128)S(1)} %get-tuple-element.74), channel_id=1, source_target_pairs={{0,3},{1,2},{2,1},{3,0},{4,7},{5,6},{6,5},{7,4},{8,11},{9,10},{10,... | collective-permute-start | bytes 49160 | tf_op jit(solution)/shard_map/ppermute | solution.py:588
  34.8 6.1 %collective-permute-start.13 = (f32[32,1024]{1,0:T(8,128)S(1)}, f32[32,1024]{1,0:T(8,128)S(1)}, u32[]{:S(2)}, u32[]{:S(2)}) collective-permute-start(f32[32,1024]{1,0:T(8,128)S(1)} %get-tuple-element.77), channel_id=1, source_target_pairs={{0,4},{4,0},{8,12},{12,8},{16,20},{20,16},{24,28},{28,24},{1,5},{5... | collective-permute-start | bytes 393224 | tf_op jit(solution)/shard_map/ppermute | solution.py:588
  34.9 7.7 %collective-permute-start.14 = (f32[32,1024]{1,0:T(8,128)S(1)}, f32[32,1024]{1,0:T(8,128)S(1)}, u32[]{:S(2)}, u32[]{:S(2)}) collective-permute-start(f32[32,1024]{1,0:T(8,128)S(1)} %get-tuple-element.78), channel_id=1, source_target_pairs={{0,28},{4,8},{8,4},{12,16},{16,12},{20,24},{24,20},{28,0},{1,29},{... | collective-permute-start | bytes 393224 | tf_op jit(solution)/shard_map/ppermute | solution.py:588
  36.6 2.9 %collective-permute-start.15 = (f32[16,256]{1,0:T(8,128)S(1)}, f32[16,256]{1,0:T(8,128)S(1)}, u32[]{:S(2)}, u32[]{:S(2)}) collective-permute-start(f32[16,256]{1,0:T(8,128)S(1)} %get-tuple-element.79), channel_id=1, source_target_pairs={{0,1},{1,0},{2,3},{3,2},{4,5},{5,4},{6,7},{7,6},{8,9},{9,8},{10,11... | collective-permute-start | bytes 49160 | tf_op jit(solution)/shard_map/ppermute | solution.py:588
  36.6 3.2 %collective-permute-start.16 = (f32[16,256]{1,0:T(8,128)S(1)}, f32[16,256]{1,0:T(8,128)S(1)}, u32[]{:S(2)}, u32[]{:S(2)}) collective-permute-start(f32[16,256]{1,0:T(8,128)S(1)} %get-tuple-element.80), channel_id=1, source_target_pairs={{0,3},{1,2},{2,1},{3,0},{4,7},{5,6},{6,5},{7,4},{8,11},{9,10},{10,... | collective-permute-start | bytes 49160 | tf_op jit(solution)/shard_map/ppermute | solution.py:588
  43.5 9.8 %all-to-all-start = ((f32[32,1,128]{2,1,0:T(1,128)}), f32[32,1,128]{2,1,0:T(1,128)S(1)}, u32[]{:S(2)}, u32[]{:S(2)}) async-start(f32[32,1,128]{2,1,0:T(1,128)} %bitcast.1), calls=%async_computation | async-start | bytes 32768 | tf_op jit(solution)/shard_map/all_to_all | solution.py:651

commit v2 on v1

--- a/solution.py
+++ b/solution.py
@@ -13,7 +13,8 @@
 LANES = 128
 ROWS = 8
 SHIFT = 1.145
-DOTS = 6
+DOTS = 5
+FOLD = LANES // 2
 
 
 def gll_tables():
@@ -113,13 +114,25 @@
     return jnp.where(source == wanted, 1.0, 0.0).astype(BF16)
 
 
-def exact_dot(values, matrix, dims):
-    one = values.astype(BF16)
-    rest = values - one.astype(F32)
-    two = rest.astype(BF16)
-    three = (rest - two.astype(F32)).astype(BF16)
-    dot = lambda v: lax.dot_general(v, matrix, (dims, ((), ())), preferred_element_type=F32)
-    return (dot(one) + dot(two)) + dot(three)
+def exact_dot(blocks, matrix, dims):
+    parts = []
+    for values in blocks:
+        one = values.astype(BF16)
+        rest = values - one.astype(F32)
+        two = rest.astype(BF16)
+        three = (rest - two.astype(F32)).astype(BF16)
+        parts += [one, two, three]
+    product = lax.dot_general(
+        jnp.concatenate(parts, 0), matrix, (dims, ((), ())), preferred_element_type=F32
+    )
+    out = []
+    first = 0
+    for values in blocks:
+        n = values.shape[0]
+        one, two, three = (product[first + n * i : first + n * (i + 1)] for i in range(3))
+        out.append((one + two) + three)
+        first += 3 * n
+    return out
 
 
 def local_apply(g, u_ref, cx, cxp, cr, crp, cy, v_ref):
@@ -199,8 +212,9 @@
 
 def start_kernel(g):
     def body(x_hbm, m_hbm, x_ref, m_ref, p1, p2, p3, p4, corner, sems):
-        copies = [pltpu.make_async_copy(x_hbm.at[a], x_ref.at[a], sems.at[a]) for a in range(4)]
-        copies.append(pltpu.make_async_copy(m_hbm, m_ref, sems.at[4]))
+        cut = [(a, g.row(b)) for b in range(4) for a in range(4)]
+        copies = [pltpu.make_async_copy(x_hbm.at[at], x_ref.at[at], sems.at[i]) for i, at in enumerate(cut)]
+        copies.append(pltpu.make_async_copy(m_hbm, m_ref, sems.at[16]))
         for copy in copies:
             copy.start()
         even_x, even_r, _, _ = positions()
@@ -210,12 +224,15 @@
         corner[...] = jnp.zeros_like(corner)
         p3[...] = jnp.zeros_like(p3)
         p4[...] = jnp.zeros_like(p4)
-        for copy in copies:
-            copy.wait()
-        down = x_ref[0]
-        up = last_row([x_ref[a] for a in range(4)])
-        p1[0:n] = jnp.where(even_x, up, down)
-        p2[0:n] = jnp.where(even_x, down, up)
+        for b in range(4):
+            at = g.row(b)
+            for copy in copies[4 * b : 4 * b + 4]:
+                copy.wait()
+            down = x_ref[0, at]
+            up = last_row([x_ref[a, at] for a in range(4)])
+            p1[at] = jnp.where(even_x, up, down)
+            p2[at] = jnp.where(even_x, down, up)
+        copies[-1].wait()
         for k in range(3):
             m = m_ref[k, 0]
             p1[pl.ds(n, g.rows), pl.ds(span * k, span)] = m
@@ -235,31 +252,60 @@
     return body
 
 
+def line_results(g, u_ref, along_x, along_r, end_r, along_y, end_y):
+    rows = row_index(g)
+    lanes = lane_index(g)
+    for ab in range(16):
+        u = [[u_ref[g.row(ab), g.lane(h, c)] for c in range(4)] for h in range(g.halves)]
+        fifth = next_lane([u[h][0] for h in range(g.halves)], lanes)
+        for h in range(g.halves):
+            r = line_operator(u[h] + [fifth[h]])
+            for c in range(4):
+                along_y[g.row(ab), g.lane(h, c)] = r[c]
+            end_y[g.row(ab), g.half(h)] = r[4]
+    for h in range(g.halves):
+        for c in range(4):
+            at = g.lane(h, c)
+            u = [[u_ref[g.row(4 * a + b), at] for b in range(4)] for a in range(4)]
+            for b in range(4):
+                r = line_operator([u[a][b] for a in range(4)] + [None])
+                for a in range(4):
+                    along_x[g.row(4 * a + b), at] = r[a]
+            for a in range(4):
+                r = line_operator(u[a] + [next_row(g, u[a][0], rows, 0.0)])
+                for b in range(4):
+                    along_r[g.row(4 * a + b), at] = r[b]
+                end_r[g.row(a), at] = r[4]
+
+
 def arrange_kernel(g):
-    def body(x_ref, s_ref, xd, sd, matrix_ref, buffer):
+    def body(x_ref, s_ref, xd, sd, matrix_ref, along_x, along_r, end_r, along_y, end_y, buffer):
         matrix = permutation()
         matrix_ref[...] = matrix
         for source, target in ((x_ref, xd), (s_ref, sd)):
+            blocks = [
+                source[:, :, pl.ds(g.wide * h, g.wide)].reshape(16 * g.rows, g.wide) for h in range(g.halves)
+            ]
+            blocks = exact_dot(blocks, matrix, ((1,), (0,)))
             for h in range(g.halves):
-                part = source[:, :, pl.ds(g.wide * h, g.wide)].reshape(16 * g.rows, g.wide)
-                part = exact_dot(part, matrix, ((1,), (0,)))
                 for c in range(4):
-                    buffer[4 * h + c] = part[:, LANES * c : LANES * (c + 1)]
+                    buffer[4 * h + c] = blocks[h][:, LANES * c : LANES * (c + 1)]
             for h in range(g.halves):
                 for c in range(4):
                     for a in range(4):
                         for b in range(4):
                             pick = pl.ds(4 * g.rows * a + b, g.rows, 4)
                             target[g.row(4 * a + b), g.lane(h, c)] = buffer[4 * h + c, pick, :]
+        line_results(g, xd, along_x, along_r, end_r, along_y, end_y)
 
     return body
 
 
 def first_kernel(g):
     def body(
-        xd, sd, m_ref, matrix_ref, r1, r2, r3, r4, rc,
+        xd, sd, along_x, along_r, end_r, along_y, end_y, m_ref, matrix_ref, r1, r2, r3, r4, rc,
         cx, cxp, cr, crp, cy, inv, z_ref, p1, p2, p3, p4,
-        planes, edges, vloc, buffer,
+        planes, edges, buffer,
     ):
         even_x, even_r, bottom, top = positions()
         rows = row_index(g)
@@ -268,25 +314,27 @@
         span = LANES * g.halves
         H = range(g.halves)
         matrix = matrix_ref[...]
+        low_all = jnp.where(even_r, r4[4:5, :], r3[4:5, :])
+        blocks = []
         for h in H:
             at = pl.ds(g.wide * h, g.wide)
             one, two = r1[0:n, at], r2[0:n, at]
-            both = jnp.concatenate([jnp.where(even_x, one, two), jnp.where(even_x, two, one)], 0)
-            both = exact_dot(both, matrix, ((1,), (0,)))
+            blocks += [jnp.where(even_x, one, two), jnp.where(even_x, two, one)]
+            one, two = r3[:, at], r4[:, at]
+            blocks += [jnp.where(even_r, one, two), jnp.where(even_r, two, one)]
+        blocks = exact_dot(blocks, matrix, ((1,), (0,)))
+        for h in H:
             for c in range(4):
-                buffer[4 * h + c] = both[:, LANES * c : LANES * (c + 1)]
+                lanes_c = slice(LANES * c, LANES * (c + 1))
+                buffer[4 * h + c, 0:n] = blocks[4 * h][:, lanes_c]
+                buffer[4 * h + c, n : 2 * n] = blocks[4 * h + 1][:, lanes_c]
+                edges[0:8, g.lane(h, c)] = blocks[4 * h + 2][:, lanes_c]
+                edges[8:16, g.lane(h, c)] = blocks[4 * h + 3][:, lanes_c]
             for c in range(4):
                 for b in range(4):
                     planes[g.row(b), g.lane(h, c)] = buffer[4 * h + c, pl.ds(b, g.rows, 4), :]
                     planes[g.row(4 + b), g.lane(h, c)] = buffer[4 * h + c, pl.ds(n + b, g.rows, 4), :]
-        one, two = r3[...], r4[...]
-        edges[0:8] = jnp.where(even_r, one, two)
-        edges[8:16] = jnp.where(even_r, two, one)
-        low_all = edges[12:13, :]
         low = [[jnp.where(bottom, 0.0, low_all[:, span * k + LANES * h : span * k + LANES * (h + 1)]) for h in H] for k in range(3)]
-        for h in H:
-            at = pl.ds(g.wide * h, g.wide)
-            edges[:, at] = exact_dot(edges[:, at], matrix, ((1,), (0,)))
         own = [[m_ref[k, 0, :, g.half(h)] for h in H] for k in range(3)]
         left = []
         for k in range(3):
@@ -337,7 +385,6 @@
             for b in range(4):
                 for h in H:
                     cy[g.row(4 * a + b), g.half(h)] = (W[a] * W[b]) * table_y[(min(a, 1), min(b, 1))][h]
-        local_apply(g, xd, cx, cxp, cr, crp, cy, vloc)
         behind = {}
         for key in table_y:
             behind[key] = prev_lane(table_y[key], lanes)
@@ -346,7 +393,20 @@
                 at = g.lane(h, c)
                 coef_x = [cx[g.row(b), at] for b in range(4)]
                 coef_r = [cr[g.row(a), at] for a in range(4)]
-                v = [[vloc[g.row(4 * a + b), at] for b in range(4)] for a in range(4)]
+                u = [[xd[g.row(4 * a + b), at] for b in range(4)] for a in range(4)]
+                v = [[None] * 4 for _ in range(4)]
+                for a in range(4):
+                    for b in range(4):
+                        rw = g.row(4 * a + b)
+                        v[a][b] = coef_x[b] * along_x[rw, at] + coef_r[a] * along_r[rw, at]
+                        v[a][b] = v[a][b] + cy[rw, g.half(h)] * along_y[rw, at]
+                        if c == 0:
+                            ends = [cy[rw, g.half(k)] * end_y[rw, g.half(k)] for k in H]
+                            v[a][b] = v[a][b] + prev_lane(ends, lanes)[h]
+                    v[a][0] = v[a][0] + prev_row(coef_r[a] * end_r[g.row(a), at], rows, 0.0)
+                    v[a][0] = v[a][0] + K[4][4] * (crp[g.row(a), at] * u[a][0])
+                for b in range(4):
+                    v[0][b] = v[0][b] + K[4][4] * (cxp[g.row(b), at] * u[0][b])
                 above_x = [planes[g.row(b), at] for b in range(4)]
                 below_x = [cxp[g.row(b), at] * planes[g.row(4 + b), at] for b in range(4)]
                 above_r = [jnp.where(top, 0.0, edges[pl.ds(a, 1), at]) for a in range(4)]
@@ -383,16 +443,18 @@
                     for b in range(4):
                         pick = pl.ds(4 * g.rows * a + b, g.rows, 4)
                         buffer[4 * h + c, pick, :] = source[g.row(4 * a + b), g.lane(h, c)]
+        blocks = [jnp.concatenate([buffer[4 * h + c] for c in range(4)], 1) for h in range(g.halves)]
+        blocks = exact_dot(blocks, matrix, ((1,), (1,)))
         for h in range(g.halves):
-            part = jnp.concatenate([buffer[4 * h + c] for c in range(4)], 1)
-            part = exact_dot(part, matrix, ((1,), (1,)))
-            target[:, pl.ds(g.wide * h, g.wide)] = part
-
-
-def inner_kernel(g, count, with_diagonal):
+            target[:, pl.ds(g.wide * h, g.wide)] = blocks[h]
+
+
+def inner_kernel(g, count, with_diagonal, earlier):
     def body(*refs):
         cx, cxp, cr, crp, cy, inv, matrix = refs[:7]
         many = refs[7 : 7 + count]
+        before = refs[7 + count : 7 + count + earlier]
+        refs = refs[:7] + many + refs[7 + count + earlier :]
         v_ref, dots, z_plain = refs[7 + count : 10 + count]
         buffer = refs[-1]
         newest = many[-1]
@@ -408,8 +470,16 @@
                         diagonal[at] = diag
                     weighted = diag * newest[at]
                     totals = [total + weighted * ref[at] for total, ref in zip(totals, many)]
-        for i in range(count):
-            dots[pl.ds(g.rows * i, g.rows), :] = totals[i]
+        if earlier:
+            parts = [ref[pl.ds(i, g.rows), :] for ref in before for i in range(0, ref.shape[0], g.rows)]
+            place = lane_index(g)
+            row = jnp.zeros((g.rows, LANES), F32)
+            for i, part in enumerate(parts + totals):
+                row = row + jnp.where(place == FOLD + i, jnp.sum(part, axis=1, keepdims=True), 0.0)
+            dots[...] = jnp.broadcast_to(jnp.sum(row, axis=0, keepdims=True), (g.rows, LANES))
+        else:
+            for i in range(count):
+                dots[pl.ds(g.rows * i, g.rows), :] = totals[i]
         restore(g, [newest], [z_plain], matrix[...], buffer)
         if with_diagonal:
             restore(g, [diagonal], [refs[10 + count]], matrix[...], buffer)
@@ -460,10 +530,10 @@
 
 
 def last_kernel(g, devices):
-    def body(vloc, cx, cr, z_ref, r1, r2, r3, r4, d0, d1, d2, v_ref, message):
+    def body(vloc, cx, cr, z_ref, r1, r2, r3, r4, dots, v_ref, message):
         even_x, even_r, bottom, top = positions()
         rows = row_index(g)
-        total = jnp.zeros((g.rows, LANES), F32)
+        totals = []
         for h in range(g.halves):
             for c in range(4):
                 at = g.lane(h, c)
@@ -473,20 +543,18 @@
                 halo = received(g, r1, r2, r3, r4, h, c, at, even_x, even_r, bottom, top)
                 add_halo(g, v, coef_x, coef_r, *halo, rows)
                 for a in range(4):
+                    total = jnp.zeros((g.rows, LANES), F32)
                     for b in range(4):
                         rw = g.row(4 * a + b)
                         v_ref[rw, at] = v[a][b]
                         total = total + z_ref[rw, at] * v[a][b]
-        parts = []
-        for ref in (d0, d1, d2):
-            for i in range(ref.shape[0] // g.rows):
-                parts.append(ref[pl.ds(g.rows * i, g.rows), :])
-        parts.append(total)
-        place = lax.broadcasted_iota(jnp.int32, (g.rows, LANES), 1)
-        out = jnp.zeros((g.rows, LANES), F32)
-        for i, part in enumerate(parts):
-            out = out + jnp.where(place == i, jnp.sum(part, axis=1, keepdims=True), 0.0)
-        row = jnp.sum(out, axis=0, keepdims=True)
+                    totals.append(total)
+        while len(totals) > 1:
+            totals = [sum(totals[i : i + 2]) for i in range(0, len(totals), 2)]
+        row = jnp.sum(totals[0], axis=0, keepdims=True)
+        row = row + pltpu.roll(row, FOLD, 1)
+        place = lax.broadcasted_iota(jnp.int32, (1, LANES), 1)
+        row = jnp.where(place < FOLD, row, dots[0:1])
         message[...] = jnp.broadcast_to(row, (devices, LANES))
 
     return body
@@ -508,7 +576,8 @@
     def body(sums, x_ref, diag, z0, z1, z2, v3, solution_hbm, residual_hbm, solution_ref, residual_ref, sems):
         total = jnp.sum(sums[...], axis=0, keepdims=True)
         place = lax.broadcasted_iota(jnp.int32, (1, LANES), 1)
-        dot = [jnp.sum(jnp.where(place == i, total, 0.0), axis=1, keepdims=True) for i in range(DOTS)]
+        picks = [place == FOLD + i for i in range(DOTS)] + [place < FOLD]
+        dot = [jnp.sum(jnp.where(pick, total, 0.0), axis=1, keepdims=True) for pick in picks]
         s00, s01, s11, s12, s22, m22 = dot
         m00 = s01 + SHIFT * s00
         m01 = s11 + SHIFT * s01
@@ -594,7 +663,7 @@
         (guess, pltpu.with_memory_space_constraint(metric, pltpu.HBM)),
         [natural, (metric.shape, F32)]
         + [((5 * count_r, 4 * count_y), F32)] * 2 + [((8, 4 * count_y), F32)] * 2 + [((8, count_y), F32)],
-        [pltpu.SemaphoreType.DMA((5,))],
+        [pltpu.SemaphoreType.DMA((17,))],
         in_specs=[HBM, HBM],
     )
     got = exchange(p1, p2, p3, p4)
@@ -604,26 +673,28 @@
     corner = lax.ppermute(corner, ("group", "rad"), diagonal)
     matrix = ((4 * LANES, 4 * LANES), BF16)
     tiles = pltpu.VMEM((4 * g.halves, 16 * count_r, LANES), F32)
-    xd, sd, matrix = call(
+    slim = ((16 * count_r, count_y), F32)
+    xd, sd, matrix, *lines = call(
         arrange_kernel(g),
         (x0, source_term),
-        [full, full, matrix],
+        [full, full, matrix, full, full, plane, full, slim],
         [tiles],
     )
     outs = [plane, plane, plane, plane, ((16 * count_r, count_y), F32), full, full]
     outs += [plane, plane, edge, edge]
     cx, cxp, cr, crp, cy, inv, z0, *send = call(
         first_kernel(g),
-        (xd, sd, m0, matrix, *got, corner),
+        (xd, sd, *lines, m0, matrix, *got, corner),
         outs,
-        [pltpu.VMEM((8 * count_r, 4 * count_y), F32), pltpu.VMEM((16, 4 * count_y), F32), pltpu.VMEM(*full), pltpu.VMEM((count_y // 32, 8 * count_r, LANES), F32)],
+        [pltpu.VMEM((8 * count_r, 4 * count_y), F32), pltpu.VMEM((16, 4 * count_y), F32), pltpu.VMEM((count_y // 32, 8 * count_r, LANES), F32)],
     )
 
-    def inner(many, with_diagonal):
+    def inner(many, with_diagonal, earlier=()):
+        rows = count_r if earlier else count_r * len(many)
         return call(
-            inner_kernel(g, len(many), with_diagonal),
-            (cx, cxp, cr, crp, cy, inv, matrix, *many),
-            [full, ((count_r * len(many), LANES), F32), full] + [full] * with_diagonal,
+            inner_kernel(g, len(many), with_diagonal, len(earlier)),
+            (cx, cxp, cr, crp, cy, inv, matrix, *many, *earlier),
+            [full, ((rows, LANES), F32), full] + [full] * with_diagonal,
             [pltpu.VMEM(*full)] * with_diagonal + [tiles],
         )
 
@@ -642,10 +713,10 @@
     vloc, d1, z1_n = inner((z0, z1), False)
     z2, send = step(vloc, got, (z1,), (SHIFT,))
     got = exchange(*send)
-    vloc, d2, z2_n = inner((z1, z2), False)
+    vloc, dots, z2_n = inner((z1, z2), False, (d0, d1))
     v3, message = call(
         last_kernel(g, nx * nr),
-        (vloc, cx, cr, z2, *got, d0, d1, d2),
+        (vloc, cx, cr, z2, *got, dots),
         [full, ((nx * nr, LANES), F32)],
     )
     sums = lax.all_to_all(message, ("group", "rad"), 0, 0, tiled=True)

time: 54.8 us -> 54.1 us (0.987)
  Pallas kernels: 13.3 us -> 10.8 us
  waiting for transfers between devices: 20.1 us -> 21.9 us
    pallas_call x11, Pallas kernels: 13.3 us -> 10.8 us  [call(): pl.pallas_call(body, in_specs=in_specs or [VMEM] * len(args), out_specs=o...]
    ppermute x16, waiting for transfers between devices: 8.71 us -> 10.7 us  [exchange(): got.append(lax.ppermute(value, axis, swaps(count, parity)))]
  transfers between devices with their start and end apart: 18 -> 18, of which waited for: 9 -> 10; matrix products, arithmetic and copies ran while one was open for 0% -> 0% of each run, Pallas kernels for 14% -> 11%
where the time goes in v2:
time: 54.1 us; the launch traced here: 53.9 us
  waiting for transfers between devices  21.9 us (40%)
  starting transfers between devices  20.4 us (38%)
  Pallas kernels  10.8 us (20%)
  between operations  0.74 us (1%)
    ppermute x16, starting transfers between devices, exchange(): got.append(lax.ppermute(value, axis, swaps(count, parity)))  17.7 us
    pallas_call x11, Pallas kernels, call(): pl.pallas_call(body, in_specs=in_specs or [VMEM] * len(args), out_specs=o...  10.8 us
    ppermute x16, waiting for transfers between devices, exchange(): got.append(lax.ppermute(value, axis, swaps(count, parity)))  10.7 us
    all_to_all x1, waiting for transfers between devices, steps(): sums = lax.all_to_all(message, ('group', 'rad'), 0, 0, tiled=True)  5.96 us
    ppermute x1, waiting for transfers between devices, steps(): corner = lax.ppermute(corner, ('group', 'rad'), diagonal)  5.31 us
    all_to_all x1, starting transfers between devices, steps(): sums = lax.all_to_all(message, ('group', 'rad'), 0, 0, tiled=True)  2.74 us
  transfers between devices with their start and end apart: 18, of which 10 were waited for; matrix products, arithmetic and copies ran while one was open for 0% of the time, Pallas kernels for 11%

profile of v2, /device:TPU:0, one launch (start us, length us, event | category | flops | bytes accessed | tf_op | source)
XLA Modules:
  0.0 53.9 jit_solution(12603631688969791784)
XLA Ops:
  0.6 0.0 copy-start
  0.6 1.2 %shard_map.50 = (f32[4,32,1024]{2,1,0:T(8,128)S(1)}, f32[3,1,8,256]{3,2,1,0:T(8,128)S(1)}, f32[40,1024]{1,0:T(8,128)S(1)}, f32[40,1024]{1,0:T(8,128)S(1)}, f32[8...) custom-call(f32[4,32,1024]{2,1,0:T(8,128)} %x_hbm.3, f32[3,1,8,256]{3,2,1,0:T(8,128)} %m_hbm.1), custom_call_target="tpu_custom_call" | custom-call | flops 1000000 | bytes 1000000 | tf_op jit(solution)/shard_map/pallas_call | solution.py:630
  1.9 3.0 %collective-permute-start = (f32[40,1024]{1,0:T(8,128)S(1)}, f32[40,1024]{1,0:T(8,128)S(1)}, u32[]{:S(2)}, u32[]{:S(2)}) collective-permute-start(f32[40,1024]{1,0:T(8,128)S(1)} %get-tuple-element.62), channel_id=1, source_target_pairs={{0,4},{4,0},{8,12},{12,8},{16,20},{20,16},{24,28},{28,24},{1,5},{5... | collective-permute-start | bytes 491528 | tf_op jit(solution)/shard_map/ppermute | solution.py:657
  4.9 3.6 %collective-permute-start.1 = (f32[40,1024]{1,0:T(8,128)S(1)}, f32[40,1024]{1,0:T(8,128)S(1)}, u32[]{:S(2)}, u32[]{:S(2)}) collective-permute-start(f32[40,1024]{1,0:T(8,128)S(1)} %get-tuple-element.63), channel_id=1, source_target_pairs={{0,28},{4,8},{8,4},{12,16},{16,12},{20,24},{24,20},{28,0},{1,29},{... | collective-permute-start | bytes 491528 | tf_op jit(solution)/shard_map/ppermute | solution.py:657
  8.5 0.0 collective-permute-start.2
  8.5 1.6 %collective-permute-start.3 = (f32[8,1024]{1,0:T(8,128)S(1)}, f32[8,1024]{1,0:T(8,128)S(1)}, u32[]{:S(2)}, u32[]{:S(2)}) collective-permute-start(f32[8,1024]{1,0:T(8,128)S(1)} %get-tuple-element.65), channel_id=1, source_target_pairs={{0,3},{1,2},{2,1},{3,0},{4,7},{5,6},{6,5},{7,4},{8,11},{9,10},{10,... | collective-permute-start | bytes 98312 | tf_op jit(solution)/shard_map/ppermute | solution.py:657
  10.1 0.0 collective-permute-start.4
  10.1 0.0 copy-done
  10.1 1.4 %shard_map.51 = (f32[128,1024]{1,0:T(8,128)S(1)}, f32[128,1024]{1,0:T(8,128)S(1)}, bf16[512,512]{1,0:T(8,128)(2,1)S(1)}, f32[128,1024]{1,0:T(8,128)S(1)}, f32[12...) custom-call(f32[4,32,1024]{2,1,0:T(8,128)S(1)} %get-tuple-element.52.x_ref, ...), custom_call_target="tpu_custom_call" | custom-call | flops 1000000 | bytes 1000000 | tf_op jit(solution)/shard_map/pallas_call | solution.py:630
  11.5 5.3 %collective-permute-done.4.rc = f32[8,256]{1,0:T(8,128)S(1)} collective-permute-done((f32[8,256]{1,0:T(8,128)S(1)}, f32[8,256]{1,0:T(8,128)S(1)}, u32[]{:S(2)}, u32[]{:S(2)}) %collective-permute-start.4) | collective-permute-done | bytes 8224 | tf_op jit(solution)/shard_map/ppermute | solution.py:673
  16.8 0.0 collective-permute-done.2.r3
  16.8 0.0 collective-permute-done.3.r4
  16.8 0.0 collective-permute-done.r1
  16.8 0.0 collective-permute-done.1.r2
  16.8 0.9 %shard_map.52 = (f32[32,1024]{1,0:T(8,128)S(1)}, f32[32,1024]{1,0:T(8,128)S(1)}, f32[32,1024]{1,0:T(8,128)S(1)}, f32[32,1024]{1,0:T(8,128)S(1)}, f32[128,256]{1,...) custom-call(f32[128,1024]{1,0:T(8,128)S(1)} %get-tuple-element.53.xd, ...), custom_call_target="tpu_custom_call" | custom-call | flops 1000000 | bytes 1000000 | tf_op jit(solution)/shard_map/pallas_call | solution.py:630
  17.7 0.1 collective-permute-start.5
  17.8 1.3 %collective-permute-start.6 = (f32[32,1024]{1,0:T(8,128)S(1)}, f32[32,1024]{1,0:T(8,128)S(1)}, u32[]{:S(2)}, u32[]{:S(2)}) collective-permute-start(f32[32,1024]{1,0:T(8,128)S(1)} %get-tuple-element.76), channel_id=1, source_target_pairs={{0,28},{4,8},{8,4},{12,16},{16,12},{20,24},{24,20},{28,0},{1,29},{... | collective-permute-start | bytes 393224 | tf_op jit(solution)/shard_map/ppermute | solution.py:657
  19.1 0.0 collective-permute-start.7
  19.1 1.6 %collective-permute-start.8 = (f32[16,256]{1,0:T(8,128)S(1)}, f32[16,256]{1,0:T(8,128)S(1)}, u32[]{:S(2)}, u32[]{:S(2)}) collective-permute-start(f32[16,256]{1,0:T(8,128)S(1)} %get-tuple-element.78), channel_id=1, source_target_pairs={{0,3},{1,2},{2,1},{3,0},{4,7},{5,6},{6,5},{7,4},{8,11},{9,10},{10,... | collective-permute-start | bytes 49160 | tf_op jit(solution)/shard_map/ppermute | solution.py:657
  20.7 1.3 %shard_map.53 = (f32[128,1024]{1,0:T(8,128)S(1)}, f32[8,128]{1,0:T(8,128)S(1)}, f32[128,1024]{1,0:T(8,128)S(1)}, f32[128,1024]{1,0:T(8,128)S(1)}) custom-call(f32[32,1024]{1,0:T(8,128)S(1)} %get-tuple-element.67.refs_0_.refs_1_.cx, f32[32,1024]{1,0:T(8,128)S(1)} %get-tuple-element.68.refs_1_, f32[32,1024]{1,0:T(8,128)S(1)} %get-tuple-element.69.refs_2_.cr, ...), custom_call_target="tpu_custom_call" | custom-call | flops 1000000 | bytes 1000000 | tf_op jit(solution)/shard_map/pallas_call | solution.py:630
  22.1 0.0 collective-permute-done.7.refs_6_
  22.1 0.2 collective-permute-done.8.refs_7_
  22.3 3.2 %collective-permute-done.5.refs_4_ = f32[32,1024]{1,0:T(8,128)S(1)} collective-permute-done((f32[32,1024]{1,0:T(8,128)S(1)}, f32[32,1024]{1,0:T(8,128)S(1)}, u32[]{:S(2)}, u32[]{:S(2)}) %collective-permute-start.5) | collective-permute-done | bytes 131104 | tf_op jit(solution)/shard_map/ppermute | solution.py:657
  25.6 0.0 collective-permute-done.6.refs_5_
  25.6 0.3 shard_map.54
  25.9 0.2 collective-permute-start.9
  26.1 1.4 %collective-permute-start.10 = (f32[32,1024]{1,0:T(8,128)S(1)}, f32[32,1024]{1,0:T(8,128)S(1)}, u32[]{:S(2)}, u32[]{:S(2)}) collective-permute-start(f32[32,1024]{1,0:T(8,128)S(1)} %get-tuple-element.82), channel_id=1, source_target_pairs={{0,28},{4,8},{8,4},{12,16},{16,12},{20,24},{24,20},{28,0},{1,29},{... | collective-permute-start | bytes 393224 | tf_op jit(solution)/shard_map/ppermute | solution.py:657
  27.5 0.0 collective-permute-start.11
  27.5 1.6 %collective-permute-start.12 = (f32[16,256]{1,0:T(8,128)S(1)}, f32[16,256]{1,0:T(8,128)S(1)}, u32[]{:S(2)}, u32[]{:S(2)}) collective-permute-start(f32[16,256]{1,0:T(8,128)S(1)} %get-tuple-element.84), channel_id=1, source_target_pairs={{0,3},{1,2},{2,1},{3,0},{4,7},{5,6},{6,5},{7,4},{8,11},{9,10},{10,... | collective-permute-start | bytes 49160 | tf_op jit(solution)/shard_map/ppermute | solution.py:657
  29.1 0.9 %shard_map.55 = (f32[128,1024]{1,0:T(8,128)S(1)}, f32[16,128]{1,0:T(8,128)S(1)}, f32[128,1024]{1,0:T(8,128)S(1)}) custom-call(f32[32,1024]{1,0:T(8,128)S(1)} %get-tuple-element.67.refs_0_.refs_1_.cx, f32[32,1024]{1,0:T(8,128)S(1)} %get-tuple-element.68.refs_1_, f32[32,1024]{1,0:T(8,128)S(1)} %get-tuple-element.69.refs_2_.cr, ...), custom_call_target="tpu_custom_call" | custom-call | flops 1000000 | bytes 1000000 | tf_op jit(solution)/shard_map/pallas_call | solution.py:630
  30.1 0.0 collective-permute-done.11.refs_6_
  30.1 0.6 %collective-permute-done.12.refs_7_ = f32[16,256]{1,0:T(8,128)S(1)} collective-permute-done((f32[16,256]{1,0:T(8,128)S(1)}, f32[16,256]{1,0:T(8,128)S(1)}, u32[]{:S(2)}, u32[]{:S(2)}) %collective-permute-start.12) | collective-permute-done | bytes 16416 | tf_op jit(solution)/shard_map/ppermute | solution.py:657
  30.7 1.5 %collective-permute-done.9.refs_4_ = f32[32,1024]{1,0:T(8,128)S(1)} collective-permute-done((f32[32,1024]{1,0:T(8,128)S(1)}, f32[32,1024]{1,0:T(8,128)S(1)}, u32[]{:S(2)}, u32[]{:S(2)}) %collective-permute-start.9) | collective-permute-done | bytes 131104 | tf_op jit(solution)/shard_map/ppermute | solution.py:657
  32.2 1.6 %collective-permute-done.10.refs_5_ = f32[32,1024]{1,0:T(8,128)S(1)} collective-permute-done((f32[32,1024]{1,0:T(8,128)S(1)}, f32[32,1024]{1,0:T(8,128)S(1)}, u32[]{:S(2)}, u32[]{:S(2)}) %collective-permute-start.10) | collective-permute-done | bytes 131104 | tf_op jit(solution)/shard_map/ppermute | solution.py:657
  33.7 0.3 shard_map.56
  34.0 0.2 collective-permute-start.13
  34.2 1.6 %collective-permute-start.14 = (f32[32,1024]{1,0:T(8,128)S(1)}, f32[32,1024]{1,0:T(8,128)S(1)}, u32[]{:S(2)}, u32[]{:S(2)}) collective-permute-start(f32[32,1024]{1,0:T(8,128)S(1)} %get-tuple-element.90), channel_id=1, source_target_pairs={{0,28},{4,8},{8,4},{12,16},{16,12},{20,24},{24,20},{28,0},{1,29},{... | collective-permute-start | bytes 393224 | tf_op jit(solution)/shard_map/ppermute | solution.py:657
  35.8 0.0 collective-permute-start.15
  35.8 1.4 %collective-permute-start.16 = (f32[16,256]{1,0:T(8,128)S(1)}, f32[16,256]{1,0:T(8,128)S(1)}, u32[]{:S(2)}, u32[]{:S(2)}) collective-permute-start(f32[16,256]{1,0:T(8,128)S(1)} %get-tuple-element.92), channel_id=1, source_target_pairs={{0,3},{1,2},{2,1},{3,0},{4,7},{5,6},{6,5},{7,4},{8,11},{9,10},{10,... | collective-permute-start | bytes 49160 | tf_op jit(solution)/shard_map/ppermute | solution.py:657
  37.3 1.1 %shard_map.57 = (f32[128,1024]{1,0:T(8,128)S(1)}, f32[8,128]{1,0:T(8,128)S(1)}, f32[128,1024]{1,0:T(8,128)S(1)}) custom-call(f32[32,1024]{1,0:T(8,128)S(1)} %get-tuple-element.67.refs_0_.refs_1_.cx, f32[32,1024]{1,0:T(8,128)S(1)} %get-tuple-element.68.refs_1_, f32[32,1024]{1,0:T(8,128)S(1)} %get-tuple-element.69.refs_2_.cr, ...), custom_call_target="tpu_custom_call" | custom-call | flops 1000000 | bytes 1000000 | tf_op jit(solution)/shard_map/pallas_call | solution.py:630
  38.4 0.0 collective-permute-done.15.r3
  38.4 0.6 %collective-permute-done.16.r4 = f32[16,256]{1,0:T(8,128)S(1)} collective-permute-done((f32[16,256]{1,0:T(8,128)S(1)}, f32[16,256]{1,0:T(8,128)S(1)}, u32[]{:S(2)}, u32[]{:S(2)}) %collective-permute-start.16) | collective-permute-done | bytes 16416 | tf_op jit(solution)/shard_map/ppermute | solution.py:657
  39.0 1.2 %collective-permute-done.13.r1 = f32[32,1024]{1,0:T(8,128)S(1)} collective-permute-done((f32[32,1024]{1,0:T(8,128)S(1)}, f32[32,1024]{1,0:T(8,128)S(1)}, u32[]{:S(2)}, u32[]{:S(2)}) %collective-permute-start.13) | collective-permute-done | bytes 131104 | tf_op jit(solution)/shard_map/ppermute | solution.py:657
  40.2 1.7 %collective-permute-done.14.r2 = f32[32,1024]{1,0:T(8,128)S(1)} collective-permute-done((f32[32,1024]{1,0:T(8,128)S(1)}, f32[32,1024]{1,0:T(8,128)S(1)}, u32[]{:S(2)}, u32[]{:S(2)}) %collective-permute-start.14) | collective-permute-done | bytes 131104 | tf_op jit(solution)/shard_map/ppermute | solution.py:657
  41.9 0.9 %shard_map.58 = (f32[128,1024]{1,0:T(8,128)S(1)}, f32[32,128]{1,0:T(8,128)}) custom-call(f32[128,1024]{1,0:T(8,128)S(1)} %get-tuple-element.88.vloc, f32[32,1024]{1,0:T(8,128)S(1)} %get-tuple-element.67.refs_0_.refs_1_.cx, f32[32,1024]{1,0:T(8,128)S(1)} %get-tuple-element.69.refs_2_.cr, f32[128,1024]{1,0:T(8,128)S(1)} %get-tuple-element.85.refs_8_.z_ref, ...), custom_call_target="tpu_custom_call" | custom-call | flops 1000000 | bytes 1000000 | tf_op jit(solution)/shard_map/pallas_call | solution.py:630
  42.8 2.7 %all-to-all-start = ((f32[32,1,128]{2,1,0:T(1,128)}), f32[32,1,128]{2,1,0:T(1,128)S(1)}, u32[]{:S(2)}, u32[]{:S(2)}) async-start(f32[32,1,128]{2,1,0:T(1,128)} %bitcast.1), calls=%async_computation | async-start | bytes 32768 | tf_op jit(solution)/shard_map/all_to_all | solution.py:722
  45.5 1.1 %shard_map.59 = (f32[128,1024]{1,0:T(8,128)S(1)}, f32[4,32,1024]{2,1,0:T(8,128)S(1)}) custom-call(f32[128,1024]{1,0:T(8,128)S(1)} %get-tuple-element.95.source, f32[4,32,1024]{2,1,0:T(8,128)} %x_hbm.3), custom_call_target="tpu_custom_call", output_to_operand_aliasing={{0}: (0, {})} | custom-call | flops 1000000 | bytes 1000000 | tf_op jit(solution)/shard_map/pallas_call | solution.py:630
  46.7 6.0 %all-to-all-done = f32[32,1,128]{2,1,0:T(1,128)S(1)} async-done(((f32[32,1,128]{2,1,0:T(1,128)}), f32[32,1,128]{2,1,0:T(1,128)S(1)}, u32[]{:S(2)}, u32[]{:S(2)}) %all-to-all-start) | async-done | bytes 16416 | tf_op jit(solution)/shard_map/all_to_all | solution.py:722
  52.6 1.3 %shard_map.60 = (f32[4,32,1024]{2,1,0:T(8,128)}, f32[4,32,1024]{2,1,0:T(8,128)}) custom-call(f32[32,128]{1,0:T(8,128)S(1)} %bitcast.4, f32[4,32,1024]{2,1,0:T(8,128)S(1)} %get-tuple-element.96.x_ref, f32[128,1024]{1,0:T(8,128)S(1)} %get-tuple-element.97.diag, f32[128,1024]{1,0:T(8,128)S(1)} %get-tuple-element.98.z0, f32[128,1024]{1,0:T(8,128)S(1)} %get-tuple-element.99.z1, ...), custom_call_target="tpu_custom_call" | custom-call | flops 1000000 | bytes 1000000 | tf_op jit(solution)/shard_map/pallas_call | solution.py:630
Async XLA Ops:
  0.6 9.5 %copy-start = (f32[4,32,1024]{2,1,0:T(8,128)S(1)}, f32[4,32,1024]{2,1,0:T(8,128)}, u32[]{:S(2)}) copy-start(f32[4,32,1024]{2,1,0:T(8,128)} %s_ref.1) | copy-start | bytes 1572868
  1.9 14.9 %collective-permute-start = (f32[40,1024]{1,0:T(8,128)S(1)}, f32[40,1024]{1,0:T(8,128)S(1)}, u32[]{:S(2)}, u32[]{:S(2)}) collective-permute-start(f32[40,1024]{1,0:T(8,128)S(1)} %get-tuple-element.62), channel_id=1, source_target_pairs={{0,4},{4,0},{8,12},{12,8},{16,20},{20,16},{24,28},{28,24},{1,5},{5... | collective-permute-start | bytes 491528 | tf_op jit(solution)/shard_map/ppermute | solution.py:657
  4.9 11.9 %collective-permute-start.1 = (f32[40,1024]{1,0:T(8,128)S(1)}, f32[40,1024]{1,0:T(8,128)S(1)}, u32[]{:S(2)}, u32[]{:S(2)}) collective-permute-start(f32[40,1024]{1,0:T(8,128)S(1)} %get-tuple-element.63), channel_id=1, source_target_pairs={{0,28},{4,8},{8,4},{12,16},{16,12},{20,24},{24,20},{28,0},{1,29},{... | collective-permute-start | bytes 491528 | tf_op jit(solution)/shard_map/ppermute | solution.py:657
  8.5 8.3 %collective-permute-start.2 = (f32[8,1024]{1,0:T(8,128)S(1)}, f32[8,1024]{1,0:T(8,128)S(1)}, u32[]{:S(2)}, u32[]{:S(2)}) collective-permute-start(f32[8,1024]{1,0:T(8,128)S(1)} %get-tuple-element.64), channel_id=1, source_target_pairs={{0,1},{1,0},{2,3},{3,2},{4,5},{5,4},{6,7},{7,6},{8,9},{9,8},{10,11... | collective-permute-start | bytes 98312 | tf_op jit(solution)/shard_map/ppermute | solution.py:657
  8.5 8.3 %collective-permute-start.3 = (f32[8,1024]{1,0:T(8,128)S(1)}, f32[8,1024]{1,0:T(8,128)S(1)}, u32[]{:S(2)}, u32[]{:S(2)}) collective-permute-start(f32[8,1024]{1,0:T(8,128)S(1)} %get-tuple-element.65), channel_id=1, source_target_pairs={{0,3},{1,2},{2,1},{3,0},{4,7},{5,6},{6,5},{7,4},{8,11},{9,10},{10,... | collective-permute-start | bytes 98312 | tf_op jit(solution)/shard_map/ppermute | solution.py:657
  10.1 6.7 %collective-permute-start.4 = (f32[8,256]{1,0:T(8,128)S(1)}, f32[8,256]{1,0:T(8,128)S(1)}, u32[]{:S(2)}, u32[]{:S(2)}) collective-permute-start(f32[8,256]{1,0:T(8,128)S(1)} %get-tuple-element.66), channel_id=1, source_target_pairs={{0,5},{1,6},{2,7},{3,4},{4,9},{5,10},{6,11},{7,8},{8,13},{9,14},{1... | collective-permute-start | bytes 24584 | tf_op jit(solution)/shard_map/ppermute | solution.py:673
  17.7 7.8 %collective-permute-start.5 = (f32[32,1024]{1,0:T(8,128)S(1)}, f32[32,1024]{1,0:T(8,128)S(1)}, u32[]{:S(2)}, u32[]{:S(2)}) collective-permute-start(f32[32,1024]{1,0:T(8,128)S(1)} %get-tuple-element.75), channel_id=1, source_target_pairs={{0,4},{4,0},{8,12},{12,8},{16,20},{20,16},{24,28},{28,24},{1,5},{5... | collective-permute-start | bytes 393224 | tf_op jit(solution)/shard_map/ppermute | solution.py:657
  17.8 7.8 %collective-permute-start.6 = (f32[32,1024]{1,0:T(8,128)S(1)}, f32[32,1024]{1,0:T(8,128)S(1)}, u32[]{:S(2)}, u32[]{:S(2)}) collective-permute-start(f32[32,1024]{1,0:T(8,128)S(1)} %get-tuple-element.76), channel_id=1, source_target_pairs={{0,28},{4,8},{8,4},{12,16},{16,12},{20,24},{24,20},{28,0},{1,29},{... | collective-permute-start | bytes 393224 | tf_op jit(solution)/shard_map/ppermute | solution.py:657
  19.1 2.9 %collective-permute-start.7 = (f32[16,256]{1,0:T(8,128)S(1)}, f32[16,256]{1,0:T(8,128)S(1)}, u32[]{:S(2)}, u32[]{:S(2)}) collective-permute-start(f32[16,256]{1,0:T(8,128)S(1)} %get-tuple-element.77), channel_id=1, source_target_pairs={{0,1},{1,0},{2,3},{3,2},{4,5},{5,4},{6,7},{7,6},{8,9},{9,8},{10,11... | collective-permute-start | bytes 49160 | tf_op jit(solution)/shard_map/ppermute | solution.py:657
  19.1 3.2 %collective-permute-start.8 = (f32[16,256]{1,0:T(8,128)S(1)}, f32[16,256]{1,0:T(8,128)S(1)}, u32[]{:S(2)}, u32[]{:S(2)}) collective-permute-start(f32[16,256]{1,0:T(8,128)S(1)} %get-tuple-element.78), channel_id=1, source_target_pairs={{0,3},{1,2},{2,1},{3,0},{4,7},{5,6},{6,5},{7,4},{8,11},{9,10},{10,... | collective-permute-start | bytes 49160 | tf_op jit(solution)/shard_map/ppermute | solution.py:657
  25.9 6.3 %collective-permute-start.9 = (f32[32,1024]{1,0:T(8,128)S(1)}, f32[32,1024]{1,0:T(8,128)S(1)}, u32[]{:S(2)}, u32[]{:S(2)}) collective-permute-start(f32[32,1024]{1,0:T(8,128)S(1)} %get-tuple-element.81), channel_id=1, source_target_pairs={{0,4},{4,0},{8,12},{12,8},{16,20},{20,16},{24,28},{28,24},{1,5},{5... | collective-permute-start | bytes 393224 | tf_op jit(solution)/shard_map/ppermute | solution.py:657
  26.1 7.7 %collective-permute-start.10 = (f32[32,1024]{1,0:T(8,128)S(1)}, f32[32,1024]{1,0:T(8,128)S(1)}, u32[]{:S(2)}, u32[]{:S(2)}) collective-permute-start(f32[32,1024]{1,0:T(8,128)S(1)} %get-tuple-element.82), channel_id=1, source_target_pairs={{0,28},{4,8},{8,4},{12,16},{16,12},{20,24},{24,20},{28,0},{1,29},{... | collective-permute-start | bytes 393224 | tf_op jit(solution)/shard_map/ppermute | solution.py:657
  27.5 2.6 %collective-permute-start.11 = (f32[16,256]{1,0:T(8,128)S(1)}, f32[16,256]{1,0:T(8,128)S(1)}, u32[]{:S(2)}, u32[]{:S(2)}) collective-permute-start(f32[16,256]{1,0:T(8,128)S(1)} %get-tuple-element.83), channel_id=1, source_target_pairs={{0,1},{1,0},{2,3},{3,2},{4,5},{5,4},{6,7},{7,6},{8,9},{9,8},{10,11... | collective-permute-start | bytes 49160 | tf_op jit(solution)/shard_map/ppermute | solution.py:657
  27.5 3.2 %collective-permute-start.12 = (f32[16,256]{1,0:T(8,128)S(1)}, f32[16,256]{1,0:T(8,128)S(1)}, u32[]{:S(2)}, u32[]{:S(2)}) collective-permute-start(f32[16,256]{1,0:T(8,128)S(1)} %get-tuple-element.84), channel_id=1, source_target_pairs={{0,3},{1,2},{2,1},{3,0},{4,7},{5,6},{6,5},{7,4},{8,11},{9,10},{10,... | collective-permute-start | bytes 49160 | tf_op jit(solution)/shard_map/ppermute | solution.py:657
  34.0 6.1 %collective-permute-start.13 = (f32[32,1024]{1,0:T(8,128)S(1)}, f32[32,1024]{1,0:T(8,128)S(1)}, u32[]{:S(2)}, u32[]{:S(2)}) collective-permute-start(f32[32,1024]{1,0:T(8,128)S(1)} %get-tuple-element.89), channel_id=1, source_target_pairs={{0,4},{4,0},{8,12},{12,8},{16,20},{20,16},{24,28},{28,24},{1,5},{5... | collective-permute-start | bytes 393224 | tf_op jit(solution)/shard_map/ppermute | solution.py:657
  34.2 7.7 %collective-permute-start.14 = (f32[32,1024]{1,0:T(8,128)S(1)}, f32[32,1024]{1,0:T(8,128)S(1)}, u32[]{:S(2)}, u32[]{:S(2)}) collective-permute-start(f32[32,1024]{1,0:T(8,128)S(1)} %get-tuple-element.90), channel_id=1, source_target_pairs={{0,28},{4,8},{8,4},{12,16},{16,12},{20,24},{24,20},{28,0},{1,29},{... | collective-permute-start | bytes 393224 | tf_op jit(solution)/shard_map/ppermute | solution.py:657
  35.8 2.5 %collective-permute-start.15 = (f32[16,256]{1,0:T(8,128)S(1)}, f32[16,256]{1,0:T(8,128)S(1)}, u32[]{:S(2)}, u32[]{:S(2)}) collective-permute-start(f32[16,256]{1,0:T(8,128)S(1)} %get-tuple-element.91), channel_id=1, source_target_pairs={{0,1},{1,0},{2,3},{3,2},{4,5},{5,4},{6,7},{7,6},{8,9},{9,8},{10,11... | collective-permute-start | bytes 49160 | tf_op jit(solution)/shard_map/ppermute | solution.py:657
  35.8 3.2 %collective-permute-start.16 = (f32[16,256]{1,0:T(8,128)S(1)}, f32[16,256]{1,0:T(8,128)S(1)}, u32[]{:S(2)}, u32[]{:S(2)}) collective-permute-start(f32[16,256]{1,0:T(8,128)S(1)} %get-tuple-element.92), channel_id=1, source_target_pairs={{0,3},{1,2},{2,1},{3,0},{4,7},{5,6},{6,5},{7,4},{8,11},{9,10},{10,... | collective-permute-start | bytes 49160 | tf_op jit(solution)/shard_map/ppermute | solution.py:657
  42.8 9.8 %all-to-all-start = ((f32[32,1,128]{2,1,0:T(1,128)}), f32[32,1,128]{2,1,0:T(1,128)S(1)}, u32[]{:S(2)}, u32[]{:S(2)}) async-start(f32[32,1,128]{2,1,0:T(1,128)} %bitcast.1), calls=%async_computation | async-start | bytes 32768 | tf_op jit(solution)/shard_map/all_to_all | solution.py:722

commit v3 on v2

--- a/solution.py
+++ b/solution.py
@@ -560,20 +560,8 @@
     return body
 
 
-def restore_kernel(g):
-    def body(source, x_hbm, target, x_ref, buffer, sems):
-        loads = [pltpu.make_async_copy(x_hbm.at[a], x_ref.at[a], sems.at[a]) for a in range(4)]
-        for load in loads:
-            load.start()
-        restore(g, [source], [target], permutation(), buffer)
-        for load in loads:
-            load.wait()
-
-    return body
-
-
 def finish_kernel(g):
-    def body(sums, x_ref, diag, z0, z1, z2, v3, solution_hbm, residual_hbm, solution_ref, residual_ref, sems):
+    def body(sums, x_ref, diag, z0, z1, z2, v_ref, matrix, solution_hbm, residual_hbm, solution_ref, residual_ref, v3, buffer, sems):
         total = jnp.sum(sums[...], axis=0, keepdims=True)
         place = lax.broadcasted_iota(jnp.int32, (1, LANES), 1)
         picks = [place == FOLD + i for i in range(DOTS)] + [place < FOLD]
@@ -598,14 +586,16 @@
         e0 = 1.0 - SHIFT * c0
         e1 = c0 + SHIFT * c1
         copies = []
-        for a in range(4):
-            at = pl.ds(4 * g.rows * a, 4 * g.rows)
-            p0, p1, p2 = z0[at], z1[at], z2[at]
-            residual_ref[a] = diag[at] * (e0 * p0 - (e1 * p1 + c1 * p2)) - c2 * v3[at]
-            copies.append(pltpu.make_async_copy(residual_ref.at[a], residual_hbm.at[a], sems.at[4 + a]))
+        cuts = [(a, pl.ds(4 * g.rows * b, 4 * g.rows)) for a in range(4) for b in range(4 // 4)]
+        rows = [pl.ds(4 * g.rows * i, 4 * g.rows) for i in range(len(cuts))]
+        for n, (to, at) in enumerate(zip(cuts, rows)):
+            solution_ref[to] = x_ref[to] + (c0 * z0[at] + (c1 * z1[at] + c2 * z2[at]))
+            copies.append(pltpu.make_async_copy(solution_ref.at[to], solution_hbm.at[to], sems.at[n]))
             copies[-1].start()
-            solution_ref[a] = x_ref[a] + (c0 * p0 + (c1 * p1 + c2 * p2))
-            copies.append(pltpu.make_async_copy(solution_ref.at[a], solution_hbm.at[a], sems.at[a]))
+        restore(g, [v_ref], [v3], matrix[...], buffer)
+        for n, (to, at) in enumerate(zip(cuts, rows)):
+            residual_ref[to] = diag[at] * (e0 * z0[at] - (e1 * z1[at] + c1 * z2[at])) - c2 * v3[at]
+            copies.append(pltpu.make_async_copy(residual_ref.at[to], residual_hbm.at[to], sems.at[len(cuts) + n]))
             copies[-1].start()
         for copy in copies:
             copy.wait()
@@ -720,20 +710,12 @@
         [full, ((nx * nr, LANES), F32)],
     )
     sums = lax.all_to_all(message, ("group", "rad"), 0, 0, tiled=True)
-    v3_n, x0 = call(
-        restore_kernel(g),
-        (v3, guess),
-        [full, natural],
-        [tiles, pltpu.SemaphoreType.DMA((4,))],
-        in_specs=[VMEM, HBM],
-        aliases={0: 0},
-    )
     return tuple(
         call(
             finish_kernel(g),
-            (sums, x0, diag_n, z0_n, z1_n, z2_n, v3_n),
+            (sums, x0, diag_n, z0_n, z1_n, z2_n, v3, matrix),
             [natural, natural],
-            [pltpu.VMEM(*natural)] * 2 + [pltpu.SemaphoreType.DMA((8,))],
+            [pltpu.VMEM(*natural)] * 2 + [pltpu.VMEM(*full), tiles, pltpu.SemaphoreType.DMA((8,))],
             out_specs=[HBM, HBM],
         )
     )

time: 54.1 us -> 53.6 us (level)
  blocking collectives: 0 us -> 9.72 us
  waiting for transfers between devices: 21.9 us -> 16 us
  starting transfers between devices: 20.4 us -> 17.7 us
  Pallas kernels: 10.8 us -> 9.34 us
    all_to_all x0 -> x1, blocking collectives: none -> 9.72 us  [steps(): sums = lax.all_to_all(message, ('group', 'rad'), 0, 0, tiled=True)]
    all_to_all x1 -> x0, waiting for transfers between devices: 5.96 us -> none  [steps(): sums = lax.all_to_all(message, ('group', 'rad'), 0, 0, tiled=True)]
    all_to_all x1 -> x0, starting transfers between devices: 2.74 us -> none  [steps(): sums = lax.all_to_all(message, ('group', 'rad'), 0, 0, tiled=True)]
    pallas_call x11 -> x10, Pallas kernels: 10.8 us -> 9.34 us  [call(): pl.pallas_call(body, in_specs=in_specs or [VMEM] * len(args), out_specs=o...]
  transfers between devices with their start and end apart: 18 -> 17, of which waited for: 10 -> 9; matrix products, arithmetic and copies ran while one was open for 0% -> 0% of each run, Pallas kernels for 11% -> 9%
where the time goes in v3:
time: 53.6 us; the launch traced here: 53.5 us
  starting transfers between devices  17.7 us (33%)
  waiting for transfers between devices  16 us (30%)
  blocking collectives  9.72 us (18%)
  Pallas kernels  9.34 us (17%)
  between operations  0.73 us (1%)
    ppermute x16, starting transfers between devices, exchange(): got.append(lax.ppermute(value, axis, swaps(count, parity)))  17.7 us
    ppermute x16, waiting for transfers between devices, exchange(): got.append(lax.ppermute(value, axis, swaps(count, parity)))  10.7 us
    all_to_all x1, blocking collectives, steps(): sums = lax.all_to_all(message, ('group', 'rad'), 0, 0, tiled=True)  9.72 us
    pallas_call x10, Pallas kernels, call(): pl.pallas_call(body, in_specs=in_specs or [VMEM] * len(args), out_specs=o...  9.34 us
    ppermute x1, waiting for transfers between devices, steps(): corner = lax.ppermute(corner, ('group', 'rad'), diagonal)  5.31 us
  transfers between devices with their start and end apart: 17, of which 9 were waited for; matrix products, arithmetic and copies ran while one was open for 0% of the time, Pallas kernels for 9%

profile of v3, /device:TPU:0, one launch (start us, length us, event | category | flops | bytes accessed | tf_op | source)
XLA Modules:
  0.0 53.5 jit_solution(16634544504328149322)
XLA Ops:
  0.6 0.0 copy-start
  0.6 1.2 %shard_map.50 = (f32[4,32,1024]{2,1,0:T(8,128)S(1)}, f32[3,1,8,256]{3,2,1,0:T(8,128)S(1)}, f32[40,1024]{1,0:T(8,128)S(1)}, f32[40,1024]{1,0:T(8,128)S(1)}, f32[8...) custom-call(f32[4,32,1024]{2,1,0:T(8,128)} %x_hbm.1, f32[3,1,8,256]{3,2,1,0:T(8,128)} %m_hbm.1), custom_call_target="tpu_custom_call" | custom-call | flops 1000000 | bytes 1000000 | tf_op jit(solution)/shard_map/pallas_call | solution.py:620
  1.9 3.0 %collective-permute-start = (f32[40,1024]{1,0:T(8,128)S(1)}, f32[40,1024]{1,0:T(8,128)S(1)}, u32[]{:S(2)}, u32[]{:S(2)}) collective-permute-start(f32[40,1024]{1,0:T(8,128)S(1)} %get-tuple-element.60), channel_id=1, source_target_pairs={{0,4},{4,0},{8,12},{12,8},{16,20},{20,16},{24,28},{28,24},{1,5},{5... | collective-permute-start | bytes 491528 | tf_op jit(solution)/shard_map/ppermute | solution.py:647
  4.9 3.6 %collective-permute-start.1 = (f32[40,1024]{1,0:T(8,128)S(1)}, f32[40,1024]{1,0:T(8,128)S(1)}, u32[]{:S(2)}, u32[]{:S(2)}) collective-permute-start(f32[40,1024]{1,0:T(8,128)S(1)} %get-tuple-element.61), channel_id=1, source_target_pairs={{0,28},{4,8},{8,4},{12,16},{16,12},{20,24},{24,20},{28,0},{1,29},{... | collective-permute-start | bytes 491528 | tf_op jit(solution)/shard_map/ppermute | solution.py:647
  8.5 0.0 collective-permute-start.2
  8.5 1.6 %collective-permute-start.3 = (f32[8,1024]{1,0:T(8,128)S(1)}, f32[8,1024]{1,0:T(8,128)S(1)}, u32[]{:S(2)}, u32[]{:S(2)}) collective-permute-start(f32[8,1024]{1,0:T(8,128)S(1)} %get-tuple-element.63), channel_id=1, source_target_pairs={{0,3},{1,2},{2,1},{3,0},{4,7},{5,6},{6,5},{7,4},{8,11},{9,10},{10,... | collective-permute-start | bytes 98312 | tf_op jit(solution)/shard_map/ppermute | solution.py:647
  10.1 0.0 collective-permute-start.4
  10.1 0.0 copy-done
  10.1 1.4 %shard_map.51 = (f32[128,1024]{1,0:T(8,128)S(1)}, f32[128,1024]{1,0:T(8,128)S(1)}, bf16[512,512]{1,0:T(8,128)(2,1)S(1)}, f32[128,1024]{1,0:T(8,128)S(1)}, f32[12...) custom-call(f32[4,32,1024]{2,1,0:T(8,128)S(1)} %get-tuple-element.50.x_ref, ...), custom_call_target="tpu_custom_call" | custom-call | flops 1000000 | bytes 1000000 | tf_op jit(solution)/shard_map/pallas_call | solution.py:620
  11.5 5.3 %collective-permute-done.4.rc = f32[8,256]{1,0:T(8,128)S(1)} collective-permute-done((f32[8,256]{1,0:T(8,128)S(1)}, f32[8,256]{1,0:T(8,128)S(1)}, u32[]{:S(2)}, u32[]{:S(2)}) %collective-permute-start.4) | collective-permute-done | bytes 8224 | tf_op jit(solution)/shard_map/ppermute | solution.py:663
  16.8 0.0 collective-permute-done.2.r3
  16.8 0.0 collective-permute-done.3.r4
  16.8 0.0 collective-permute-done.r1
  16.8 0.0 collective-permute-done.1.r2
  16.8 0.9 %shard_map.52 = (f32[32,1024]{1,0:T(8,128)S(1)}, f32[32,1024]{1,0:T(8,128)S(1)}, f32[32,1024]{1,0:T(8,128)S(1)}, f32[32,1024]{1,0:T(8,128)S(1)}, f32[128,256]{1,...) custom-call(f32[128,1024]{1,0:T(8,128)S(1)} %get-tuple-element.51.xd, ...), custom_call_target="tpu_custom_call" | custom-call | flops 1000000 | bytes 1000000 | tf_op jit(solution)/shard_map/pallas_call | solution.py:620
  17.7 0.1 collective-permute-start.5
  17.8 1.3 %collective-permute-start.6 = (f32[32,1024]{1,0:T(8,128)S(1)}, f32[32,1024]{1,0:T(8,128)S(1)}, u32[]{:S(2)}, u32[]{:S(2)}) collective-permute-start(f32[32,1024]{1,0:T(8,128)S(1)} %get-tuple-element.74), channel_id=1, source_target_pairs={{0,28},{4,8},{8,4},{12,16},{16,12},{20,24},{24,20},{28,0},{1,29},{... | collective-permute-start | bytes 393224 | tf_op jit(solution)/shard_map/ppermute | solution.py:647
  19.1 0.0 collective-permute-start.7
  19.1 1.6 %collective-permute-start.8 = (f32[16,256]{1,0:T(8,128)S(1)}, f32[16,256]{1,0:T(8,128)S(1)}, u32[]{:S(2)}, u32[]{:S(2)}) collective-permute-start(f32[16,256]{1,0:T(8,128)S(1)} %get-tuple-element.76), channel_id=1, source_target_pairs={{0,3},{1,2},{2,1},{3,0},{4,7},{5,6},{6,5},{7,4},{8,11},{9,10},{10,... | collective-permute-start | bytes 49160 | tf_op jit(solution)/shard_map/ppermute | solution.py:647
  20.7 1.3 %shard_map.53 = (f32[128,1024]{1,0:T(8,128)S(1)}, f32[8,128]{1,0:T(8,128)S(1)}, f32[128,1024]{1,0:T(8,128)S(1)}, f32[128,1024]{1,0:T(8,128)S(1)}) custom-call(f32[32,1024]{1,0:T(8,128)S(1)} %get-tuple-element.65.refs_0_.refs_1_.cx, f32[32,1024]{1,0:T(8,128)S(1)} %get-tuple-element.66.refs_1_, f32[32,1024]{1,0:T(8,128)S(1)} %get-tuple-element.67.refs_2_.cr, ...), custom_call_target="tpu_custom_call" | custom-call | flops 1000000 | bytes 1000000 | tf_op jit(solution)/shard_map/pallas_call | solution.py:620
  22.1 0.0 collective-permute-done.7.refs_6_
  22.1 0.2 collective-permute-done.8.refs_7_
  22.3 3.3 %collective-permute-done.5.refs_4_ = f32[32,1024]{1,0:T(8,128)S(1)} collective-permute-done((f32[32,1024]{1,0:T(8,128)S(1)}, f32[32,1024]{1,0:T(8,128)S(1)}, u32[]{:S(2)}, u32[]{:S(2)}) %collective-permute-start.5) | collective-permute-done | bytes 131104 | tf_op jit(solution)/shard_map/ppermute | solution.py:647
  25.6 0.0 collective-permute-done.6.refs_5_
  25.6 0.3 shard_map.54
  25.9 0.2 collective-permute-start.9
  26.1 1.4 %collective-permute-start.10 = (f32[32,1024]{1,0:T(8,128)S(1)}, f32[32,1024]{1,0:T(8,128)S(1)}, u32[]{:S(2)}, u32[]{:S(2)}) collective-permute-start(f32[32,1024]{1,0:T(8,128)S(1)} %get-tuple-element.80), channel_id=1, source_target_pairs={{0,28},{4,8},{8,4},{12,16},{16,12},{20,24},{24,20},{28,0},{1,29},{... | collective-permute-start | bytes 393224 | tf_op jit(solution)/shard_map/ppermute | solution.py:647
  27.5 0.0 collective-permute-start.11
  27.5 1.6 %collective-permute-start.12 = (f32[16,256]{1,0:T(8,128)S(1)}, f32[16,256]{1,0:T(8,128)S(1)}, u32[]{:S(2)}, u32[]{:S(2)}) collective-permute-start(f32[16,256]{1,0:T(8,128)S(1)} %get-tuple-element.82), channel_id=1, source_target_pairs={{0,3},{1,2},{2,1},{3,0},{4,7},{5,6},{6,5},{7,4},{8,11},{9,10},{10,... | collective-permute-start | bytes 49160 | tf_op jit(solution)/shard_map/ppermute | solution.py:647
  29.1 0.9 %shard_map.55 = (f32[128,1024]{1,0:T(8,128)S(1)}, f32[16,128]{1,0:T(8,128)S(1)}, f32[128,1024]{1,0:T(8,128)S(1)}) custom-call(f32[32,1024]{1,0:T(8,128)S(1)} %get-tuple-element.65.refs_0_.refs_1_.cx, f32[32,1024]{1,0:T(8,128)S(1)} %get-tuple-element.66.refs_1_, f32[32,1024]{1,0:T(8,128)S(1)} %get-tuple-element.67.refs_2_.cr, ...), custom_call_target="tpu_custom_call" | custom-call | flops 1000000 | bytes 1000000 | tf_op jit(solution)/shard_map/pallas_call | solution.py:620
  30.1 0.0 collective-permute-done.11.refs_6_
  30.1 0.6 %collective-permute-done.12.refs_7_ = f32[16,256]{1,0:T(8,128)S(1)} collective-permute-done((f32[16,256]{1,0:T(8,128)S(1)}, f32[16,256]{1,0:T(8,128)S(1)}, u32[]{:S(2)}, u32[]{:S(2)}) %collective-permute-start.12) | collective-permute-done | bytes 16416 | tf_op jit(solution)/shard_map/ppermute | solution.py:647
  30.7 1.5 %collective-permute-done.9.refs_4_ = f32[32,1024]{1,0:T(8,128)S(1)} collective-permute-done((f32[32,1024]{1,0:T(8,128)S(1)}, f32[32,1024]{1,0:T(8,128)S(1)}, u32[]{:S(2)}, u32[]{:S(2)}) %collective-permute-start.9) | collective-permute-done | bytes 131104 | tf_op jit(solution)/shard_map/ppermute | solution.py:647
  32.1 1.6 %collective-permute-done.10.refs_5_ = f32[32,1024]{1,0:T(8,128)S(1)} collective-permute-done((f32[32,1024]{1,0:T(8,128)S(1)}, f32[32,1024]{1,0:T(8,128)S(1)}, u32[]{:S(2)}, u32[]{:S(2)}) %collective-permute-start.10) | collective-permute-done | bytes 131104 | tf_op jit(solution)/shard_map/ppermute | solution.py:647
  33.7 0.3 shard_map.56
  34.0 0.2 collective-permute-start.13
  34.2 1.6 %collective-permute-start.14 = (f32[32,1024]{1,0:T(8,128)S(1)}, f32[32,1024]{1,0:T(8,128)S(1)}, u32[]{:S(2)}, u32[]{:S(2)}) collective-permute-start(f32[32,1024]{1,0:T(8,128)S(1)} %get-tuple-element.88), channel_id=1, source_target_pairs={{0,28},{4,8},{8,4},{12,16},{16,12},{20,24},{24,20},{28,0},{1,29},{... | collective-permute-start | bytes 393224 | tf_op jit(solution)/shard_map/ppermute | solution.py:647
  35.8 0.0 collective-permute-start.15
  35.8 1.4 %collective-permute-start.16 = (f32[16,256]{1,0:T(8,128)S(1)}, f32[16,256]{1,0:T(8,128)S(1)}, u32[]{:S(2)}, u32[]{:S(2)}) collective-permute-start(f32[16,256]{1,0:T(8,128)S(1)} %get-tuple-element.90), channel_id=1, source_target_pairs={{0,3},{1,2},{2,1},{3,0},{4,7},{5,6},{6,5},{7,4},{8,11},{9,10},{10,... | collective-permute-start | bytes 49160 | tf_op jit(solution)/shard_map/ppermute | solution.py:647
  37.3 1.1 %shard_map.57 = (f32[128,1024]{1,0:T(8,128)S(1)}, f32[8,128]{1,0:T(8,128)S(1)}, f32[128,1024]{1,0:T(8,128)S(1)}) custom-call(f32[32,1024]{1,0:T(8,128)S(1)} %get-tuple-element.65.refs_0_.refs_1_.cx, f32[32,1024]{1,0:T(8,128)S(1)} %get-tuple-element.66.refs_1_, f32[32,1024]{1,0:T(8,128)S(1)} %get-tuple-element.67.refs_2_.cr, ...), custom_call_target="tpu_custom_call" | custom-call | flops 1000000 | bytes 1000000 | tf_op jit(solution)/shard_map/pallas_call | solution.py:620
  38.4 0.0 collective-permute-done.15.r3
  38.4 0.6 %collective-permute-done.16.r4 = f32[16,256]{1,0:T(8,128)S(1)} collective-permute-done((f32[16,256]{1,0:T(8,128)S(1)}, f32[16,256]{1,0:T(8,128)S(1)}, u32[]{:S(2)}, u32[]{:S(2)}) %collective-permute-start.16) | collective-permute-done | bytes 16416 | tf_op jit(solution)/shard_map/ppermute | solution.py:647
  39.0 1.2 %collective-permute-done.13.r1 = f32[32,1024]{1,0:T(8,128)S(1)} collective-permute-done((f32[32,1024]{1,0:T(8,128)S(1)}, f32[32,1024]{1,0:T(8,128)S(1)}, u32[]{:S(2)}, u32[]{:S(2)}) %collective-permute-start.13) | collective-permute-done | bytes 131104 | tf_op jit(solution)/shard_map/ppermute | solution.py:647
  40.2 1.7 %collective-permute-done.14.r2 = f32[32,1024]{1,0:T(8,128)S(1)} collective-permute-done((f32[32,1024]{1,0:T(8,128)S(1)}, f32[32,1024]{1,0:T(8,128)S(1)}, u32[]{:S(2)}, u32[]{:S(2)}) %collective-permute-start.14) | collective-permute-done | bytes 131104 | tf_op jit(solution)/shard_map/ppermute | solution.py:647
  41.9 0.3 shard_map.58
  42.2 9.7 %all_to_all.11 = f32[32,1,128]{2,1,0:T(1,128)S(1)} all-to-all(f32[32,1,128]{2,1,0:T(1,128)S(1)} %bitcast.5), channel_id=1, replica_groups=mesh['group'=8,'rad'=4] {'group','rad'}, dimensions={0} | all-to-all | bytes 32768 | tf_op jit(solution)/shard_map/all_to_all | solution.py:712
  51.9 1.6 %shard_map.59 = (f32[4,32,1024]{2,1,0:T(8,128)}, f32[4,32,1024]{2,1,0:T(8,128)}) custom-call(f32[32,128]{1,0:T(8,128)S(1)} %bitcast.4, f32[4,32,1024]{2,1,0:T(8,128)S(1)} %get-tuple-element.50.x_ref, f32[128,1024]{1,0:T(8,128)S(1)} %get-tuple-element.93.diag, f32[128,1024]{1,0:T(8,128)S(1)} %get-tuple-element.94.z0, f32[128,1024]{1,0:T(8,128)S(1)} %get-tuple-element.95.z1, ...), custom_call_target="tpu_custom_call" | custom-call | flops 1000000 | bytes 1000000 | tf_op jit(solution)/shard_map/pallas_call | solution.py:620
Async XLA Ops:
  0.6 9.5 %copy-start = (f32[4,32,1024]{2,1,0:T(8,128)S(1)}, f32[4,32,1024]{2,1,0:T(8,128)}, u32[]{:S(2)}) copy-start(f32[4,32,1024]{2,1,0:T(8,128)} %s_ref.1) | copy-start | bytes 1572868
  1.9 14.9 %collective-permute-start = (f32[40,1024]{1,0:T(8,128)S(1)}, f32[40,1024]{1,0:T(8,128)S(1)}, u32[]{:S(2)}, u32[]{:S(2)}) collective-permute-start(f32[40,1024]{1,0:T(8,128)S(1)} %get-tuple-element.60), channel_id=1, source_target_pairs={{0,4},{4,0},{8,12},{12,8},{16,20},{20,16},{24,28},{28,24},{1,5},{5... | collective-permute-start | bytes 491528 | tf_op jit(solution)/shard_map/ppermute | solution.py:647
  4.9 11.9 %collective-permute-start.1 = (f32[40,1024]{1,0:T(8,128)S(1)}, f32[40,1024]{1,0:T(8,128)S(1)}, u32[]{:S(2)}, u32[]{:S(2)}) collective-permute-start(f32[40,1024]{1,0:T(8,128)S(1)} %get-tuple-element.61), channel_id=1, source_target_pairs={{0,28},{4,8},{8,4},{12,16},{16,12},{20,24},{24,20},{28,0},{1,29},{... | collective-permute-start | bytes 491528 | tf_op jit(solution)/shard_map/ppermute | solution.py:647
  8.5 8.3 %collective-permute-start.2 = (f32[8,1024]{1,0:T(8,128)S(1)}, f32[8,1024]{1,0:T(8,128)S(1)}, u32[]{:S(2)}, u32[]{:S(2)}) collective-permute-start(f32[8,1024]{1,0:T(8,128)S(1)} %get-tuple-element.62), channel_id=1, source_target_pairs={{0,1},{1,0},{2,3},{3,2},{4,5},{5,4},{6,7},{7,6},{8,9},{9,8},{10,11... | collective-permute-start | bytes 98312 | tf_op jit(solution)/shard_map/ppermute | solution.py:647
  8.5 8.3 %collective-permute-start.3 = (f32[8,1024]{1,0:T(8,128)S(1)}, f32[8,1024]{1,0:T(8,128)S(1)}, u32[]{:S(2)}, u32[]{:S(2)}) collective-permute-start(f32[8,1024]{1,0:T(8,128)S(1)} %get-tuple-element.63), channel_id=1, source_target_pairs={{0,3},{1,2},{2,1},{3,0},{4,7},{5,6},{6,5},{7,4},{8,11},{9,10},{10,... | collective-permute-start | bytes 98312 | tf_op jit(solution)/shard_map/ppermute | solution.py:647
  10.1 6.7 %collective-permute-start.4 = (f32[8,256]{1,0:T(8,128)S(1)}, f32[8,256]{1,0:T(8,128)S(1)}, u32[]{:S(2)}, u32[]{:S(2)}) collective-permute-start(f32[8,256]{1,0:T(8,128)S(1)} %get-tuple-element.64), channel_id=1, source_target_pairs={{0,5},{1,6},{2,7},{3,4},{4,9},{5,10},{6,11},{7,8},{8,13},{9,14},{1... | collective-permute-start | bytes 24584 | tf_op jit(solution)/shard_map/ppermute | solution.py:663
  17.7 7.8 %collective-permute-start.5 = (f32[32,1024]{1,0:T(8,128)S(1)}, f32[32,1024]{1,0:T(8,128)S(1)}, u32[]{:S(2)}, u32[]{:S(2)}) collective-permute-start(f32[32,1024]{1,0:T(8,128)S(1)} %get-tuple-element.73), channel_id=1, source_target_pairs={{0,4},{4,0},{8,12},{12,8},{16,20},{20,16},{24,28},{28,24},{1,5},{5... | collective-permute-start | bytes 393224 | tf_op jit(solution)/shard_map/ppermute | solution.py:647
  17.8 7.8 %collective-permute-start.6 = (f32[32,1024]{1,0:T(8,128)S(1)}, f32[32,1024]{1,0:T(8,128)S(1)}, u32[]{:S(2)}, u32[]{:S(2)}) collective-permute-start(f32[32,1024]{1,0:T(8,128)S(1)} %get-tuple-element.74), channel_id=1, source_target_pairs={{0,28},{4,8},{8,4},{12,16},{16,12},{20,24},{24,20},{28,0},{1,29},{... | collective-permute-start | bytes 393224 | tf_op jit(solution)/shard_map/ppermute | solution.py:647
  19.1 2.9 %collective-permute-start.7 = (f32[16,256]{1,0:T(8,128)S(1)}, f32[16,256]{1,0:T(8,128)S(1)}, u32[]{:S(2)}, u32[]{:S(2)}) collective-permute-start(f32[16,256]{1,0:T(8,128)S(1)} %get-tuple-element.75), channel_id=1, source_target_pairs={{0,1},{1,0},{2,3},{3,2},{4,5},{5,4},{6,7},{7,6},{8,9},{9,8},{10,11... | collective-permute-start | bytes 49160 | tf_op jit(solution)/shard_map/ppermute | solution.py:647
  19.1 3.2 %collective-permute-start.8 = (f32[16,256]{1,0:T(8,128)S(1)}, f32[16,256]{1,0:T(8,128)S(1)}, u32[]{:S(2)}, u32[]{:S(2)}) collective-permute-start(f32[16,256]{1,0:T(8,128)S(1)} %get-tuple-element.76), channel_id=1, source_target_pairs={{0,3},{1,2},{2,1},{3,0},{4,7},{5,6},{6,5},{7,4},{8,11},{9,10},{10,... | collective-permute-start | bytes 49160 | tf_op jit(solution)/shard_map/ppermute | solution.py:647
  25.9 6.3 %collective-permute-start.9 = (f32[32,1024]{1,0:T(8,128)S(1)}, f32[32,1024]{1,0:T(8,128)S(1)}, u32[]{:S(2)}, u32[]{:S(2)}) collective-permute-start(f32[32,1024]{1,0:T(8,128)S(1)} %get-tuple-element.79), channel_id=1, source_target_pairs={{0,4},{4,0},{8,12},{12,8},{16,20},{20,16},{24,28},{28,24},{1,5},{5... | collective-permute-start | bytes 393224 | tf_op jit(solution)/shard_map/ppermute | solution.py:647
  26.1 7.7 %collective-permute-start.10 = (f32[32,1024]{1,0:T(8,128)S(1)}, f32[32,1024]{1,0:T(8,128)S(1)}, u32[]{:S(2)}, u32[]{:S(2)}) collective-permute-start(f32[32,1024]{1,0:T(8,128)S(1)} %get-tuple-element.80), channel_id=1, source_target_pairs={{0,28},{4,8},{8,4},{12,16},{16,12},{20,24},{24,20},{28,0},{1,29},{... | collective-permute-start | bytes 393224 | tf_op jit(solution)/shard_map/ppermute | solution.py:647
  27.5 2.6 %collective-permute-start.11 = (f32[16,256]{1,0:T(8,128)S(1)}, f32[16,256]{1,0:T(8,128)S(1)}, u32[]{:S(2)}, u32[]{:S(2)}) collective-permute-start(f32[16,256]{1,0:T(8,128)S(1)} %get-tuple-element.81), channel_id=1, source_target_pairs={{0,1},{1,0},{2,3},{3,2},{4,5},{5,4},{6,7},{7,6},{8,9},{9,8},{10,11... | collective-permute-start | bytes 49160 | tf_op jit(solution)/shard_map/ppermute | solution.py:647
  27.5 3.2 %collective-permute-start.12 = (f32[16,256]{1,0:T(8,128)S(1)}, f32[16,256]{1,0:T(8,128)S(1)}, u32[]{:S(2)}, u32[]{:S(2)}) collective-permute-start(f32[16,256]{1,0:T(8,128)S(1)} %get-tuple-element.82), channel_id=1, source_target_pairs={{0,3},{1,2},{2,1},{3,0},{4,7},{5,6},{6,5},{7,4},{8,11},{9,10},{10,... | collective-permute-start | bytes 49160 | tf_op jit(solution)/shard_map/ppermute | solution.py:647
  34.0 6.1 %collective-permute-start.13 = (f32[32,1024]{1,0:T(8,128)S(1)}, f32[32,1024]{1,0:T(8,128)S(1)}, u32[]{:S(2)}, u32[]{:S(2)}) collective-permute-start(f32[32,1024]{1,0:T(8,128)S(1)} %get-tuple-element.87), channel_id=1, source_target_pairs={{0,4},{4,0},{8,12},{12,8},{16,20},{20,16},{24,28},{28,24},{1,5},{5... | collective-permute-start | bytes 393224 | tf_op jit(solution)/shard_map/ppermute | solution.py:647
  34.2 7.7 %collective-permute-start.14 = (f32[32,1024]{1,0:T(8,128)S(1)}, f32[32,1024]{1,0:T(8,128)S(1)}, u32[]{:S(2)}, u32[]{:S(2)}) collective-permute-start(f32[32,1024]{1,0:T(8,128)S(1)} %get-tuple-element.88), channel_id=1, source_target_pairs={{0,28},{4,8},{8,4},{12,16},{16,12},{20,24},{24,20},{28,0},{1,29},{... | collective-permute-start | bytes 393224 | tf_op jit(solution)/shard_map/ppermute | solution.py:647
  35.8 2.6 %collective-permute-start.15 = (f32[16,256]{1,0:T(8,128)S(1)}, f32[16,256]{1,0:T(8,128)S(1)}, u32[]{:S(2)}, u32[]{:S(2)}) collective-permute-start(f32[16,256]{1,0:T(8,128)S(1)} %get-tuple-element.89), channel_id=1, source_target_pairs={{0,1},{1,0},{2,3},{3,2},{4,5},{5,4},{6,7},{7,6},{8,9},{9,8},{10,11... | collective-permute-start | bytes 49160 | tf_op jit(solution)/shard_map/ppermute | solution.py:647
  35.8 3.2 %collective-permute-start.16 = (f32[16,256]{1,0:T(8,128)S(1)}, f32[16,256]{1,0:T(8,128)S(1)}, u32[]{:S(2)}, u32[]{:S(2)}) collective-permute-start(f32[16,256]{1,0:T(8,128)S(1)} %get-tuple-element.90), channel_id=1, source_target_pairs={{0,3},{1,2},{2,1},{3,0},{4,7},{5,6},{6,5},{7,4},{8,11},{9,10},{10,... | collective-permute-start | bytes 49160 | tf_op jit(solution)/shard_map/ppermute | solution.py:647

commit v4 on v3

--- a/solution.py
+++ b/solution.py
@@ -12,7 +12,6 @@
 BF16 = jnp.bfloat16
 LANES = 128
 ROWS = 8
-SHIFT = 1.145
 DOTS = 5
 FOLD = LANES // 2
 
@@ -61,6 +60,13 @@
 
 def last_row(u):
     return K[4][0] * u[0] + K[4][1] * u[1] + K[4][2] * u[2] + K[4][3] * u[3]
+
+
+def tree_sum(values):
+    while len(values) > 1:
+        pairs = [values[i] + values[i + 1] for i in range(0, len(values) - 1, 2)]
+        values = pairs + values[len(values) - len(values) % 2 :]
+    return values[0]
 
 
 class Shape:
@@ -459,9 +465,10 @@
         buffer = refs[-1]
         newest = many[-1]
         local_apply(g, newest, cx, cxp, cr, crp, cy, v_ref)
-        totals = [jnp.zeros((g.rows, LANES), F32)] * count
+        terms = [[] for _ in range(count)]
         diagonal = refs[-2] if with_diagonal else None
         for ab in range(16):
+            group = [[] for _ in range(count)]
             for h in range(g.halves):
                 for c in range(4):
                     at = (g.row(ab), g.lane(h, c))
@@ -469,7 +476,11 @@
                     if with_diagonal:
                         diagonal[at] = diag
                     weighted = diag * newest[at]
-                    totals = [total + weighted * ref[at] for total, ref in zip(totals, many)]
+                    for values, ref in zip(group, many):
+                        values.append(weighted * ref[at])
+            for values, part in zip(terms, group):
+                values.append(tree_sum(part))
+        totals = [tree_sum(values) for values in terms]
         if earlier:
             parts = [ref[pl.ds(i, g.rows), :] for ref in before for i in range(0, ref.shape[0], g.rows)]
             place = lane_index(g)
@@ -500,11 +511,10 @@
     return above_x, below_x, above_r, below_r
 
 
-def next_kernel(g, pulls):
+def next_kernel(g):
     def body(*refs):
         vloc, cx, cr, inv, r1, r2, r3, r4 = refs[:8]
-        earlier = refs[8 : 8 + len(pulls)]
-        z_ref, p1, p2, p3, p4 = refs[8 + len(pulls) :]
+        z_ref, p1, p2, p3, p4 = refs[8:]
         even_x, even_r, bottom, top = positions()
         rows = row_index(g)
         for h in range(g.halves):
@@ -519,11 +529,8 @@
                 for a in range(4):
                     for b in range(4):
                         rw = g.row(4 * a + b)
-                        value = inv[rw, at] * v[a][b]
-                        for ref, pull in zip(earlier, pulls):
-                            value = value - pull * ref[rw, at]
-                        z[a][b] = value
-                        z_ref[rw, at] = value
+                        z[a][b] = inv[rw, at] * v[a][b]
+                        z_ref[rw, at] = z[a][b]
                 send_planes(g, z, at, h, c, coef_x, coef_r, even_x, even_r, (p1, p2, p3, p4))
 
     return body
@@ -543,15 +550,10 @@
                 halo = received(g, r1, r2, r3, r4, h, c, at, even_x, even_r, bottom, top)
                 add_halo(g, v, coef_x, coef_r, *halo, rows)
                 for a in range(4):
-                    total = jnp.zeros((g.rows, LANES), F32)
                     for b in range(4):
-                        rw = g.row(4 * a + b)
-                        v_ref[rw, at] = v[a][b]
-                        total = total + z_ref[rw, at] * v[a][b]
-                    totals.append(total)
-        while len(totals) > 1:
-            totals = [sum(totals[i : i + 2]) for i in range(0, len(totals), 2)]
-        row = jnp.sum(totals[0], axis=0, keepdims=True)
+                        v_ref[g.row(4 * a + b), at] = v[a][b]
+                    totals.append(tree_sum([z_ref[g.row(4 * a + b), at] * v[a][b] for b in range(4)]))
+        row = jnp.sum(tree_sum(totals), axis=0, keepdims=True)
         row = row + pltpu.roll(row, FOLD, 1)
         place = lax.broadcasted_iota(jnp.int32, (1, LANES), 1)
         row = jnp.where(place < FOLD, row, dots[0:1])
@@ -567,11 +569,7 @@
         picks = [place == FOLD + i for i in range(DOTS)] + [place < FOLD]
         dot = [jnp.sum(jnp.where(pick, total, 0.0), axis=1, keepdims=True) for pick in picks]
         s00, s01, s11, s12, s22, m22 = dot
-        m00 = s01 + SHIFT * s00
-        m01 = s11 + SHIFT * s01
-        m02 = s12 + SHIFT * s11
-        m11 = m02
-        m12 = s22 + SHIFT * s12
+        m00, m01, m02, m11, m12 = s01, s11, s12, s12, s22
         l10 = m01 / m00
         l20 = m02 / m00
         d1 = m11 - l10 * m01
@@ -583,8 +581,6 @@
         c2 = y2 / d2
         c1 = y1 / d1 - l21 * c2
         c0 = s00 / m00 - l10 * c1 - l20 * c2
-        e0 = 1.0 - SHIFT * c0
-        e1 = c0 + SHIFT * c1
         copies = []
         cuts = [(a, pl.ds(4 * g.rows * b, 4 * g.rows)) for a in range(4) for b in range(4 // 4)]
         rows = [pl.ds(4 * g.rows * i, 4 * g.rows) for i in range(len(cuts))]
@@ -594,7 +590,7 @@
             copies[-1].start()
         restore(g, [v_ref], [v3], matrix[...], buffer)
         for n, (to, at) in enumerate(zip(cuts, rows)):
-            residual_ref[to] = diag[at] * (e0 * z0[at] - (e1 * z1[at] + c1 * z2[at])) - c2 * v3[at]
+            residual_ref[to] = diag[at] * (z0[at] - (c0 * z1[at] + c1 * z2[at])) - c2 * v3[at]
             copies.append(pltpu.make_async_copy(residual_ref.at[to], residual_hbm.at[to], sems.at[len(cuts) + n]))
             copies[-1].start()
         for copy in copies:
@@ -688,20 +684,20 @@
             [pltpu.VMEM(*full)] * with_diagonal + [tiles],
         )
 
-    def step(vloc, got, earlier, pulls):
+    def step(vloc, got):
         z, *send = call(
-            next_kernel(g, pulls),
-            (vloc, cx, cr, inv, *got, *earlier),
+            next_kernel(g),
+            (vloc, cx, cr, inv, *got),
             [full, plane, plane, edge, edge],
         )
         return z, send
 
     got = exchange(*send)
     vloc, d0, z0_n, diag_n = inner((z0,), True)
-    z1, send = step(vloc, got, (z0,), (SHIFT,))
+    z1, send = step(vloc, got)
     got = exchange(*send)
     vloc, d1, z1_n = inner((z0, z1), False)
-    z2, send = step(vloc, got, (z1,), (SHIFT,))
+    z2, send = step(vloc, got)
     got = exchange(*send)
     vloc, dots, z2_n = inner((z1, z2), False, (d0, d1))
     v3, message = call(

time: 53.6 us -> 53.5 us (level)
  no operation moved by 1% of the time
where the time goes in v4:
time: 53.5 us; the launch traced here: 53.4 us
  starting transfers between devices  17.7 us (33%)
  waiting for transfers between devices  16 us (30%)
  blocking collectives  9.73 us (18%)
  Pallas kernels  9.19 us (17%)
  between operations  0.74 us (1%)
    ppermute x16, starting transfers between devices, exchange(): got.append(lax.ppermute(value, axis, swaps(count, parity)))  17.7 us
    ppermute x16, waiting for transfers between devices, exchange(): got.append(lax.ppermute(value, axis, swaps(count, parity)))  10.7 us
    all_to_all x1, blocking collectives, steps(): sums = lax.all_to_all(message, ('group', 'rad'), 0, 0, tiled=True)  9.73 us
    pallas_call x10, Pallas kernels, call(): pl.pallas_call(body, in_specs=in_specs or [VMEM] * len(args), out_specs=o...  9.19 us
    ppermute x1, waiting for transfers between devices, steps(): corner = lax.ppermute(corner, ('group', 'rad'), diagonal)  5.32 us
  transfers between devices with their start and end apart: 17, of which 9 were waited for; matrix products, arithmetic and copies ran while one was open for 0% of the time, Pallas kernels for 9%

profile of v4, /device:TPU:0, one launch (start us, length us, event | category | flops | bytes accessed | tf_op | source)
XLA Modules:
  0.0 53.4 jit_solution(9884341384871067654)
XLA Ops:
  0.6 0.0 copy-start
  0.6 1.2 %shard_map.50 = (f32[4,32,1024]{2,1,0:T(8,128)S(1)}, f32[3,1,8,256]{3,2,1,0:T(8,128)S(1)}, f32[40,1024]{1,0:T(8,128)S(1)}, f32[40,1024]{1,0:T(8,128)S(1)}, f32[8...) custom-call(f32[4,32,1024]{2,1,0:T(8,128)} %x_hbm.1, f32[3,1,8,256]{3,2,1,0:T(8,128)} %m_hbm.1), custom_call_target="tpu_custom_call" | custom-call | flops 1000000 | bytes 1000000 | tf_op jit(solution)/shard_map/pallas_call | solution.py:616
  1.9 3.0 %collective-permute-start = (f32[40,1024]{1,0:T(8,128)S(1)}, f32[40,1024]{1,0:T(8,128)S(1)}, u32[]{:S(2)}, u32[]{:S(2)}) collective-permute-start(f32[40,1024]{1,0:T(8,128)S(1)} %get-tuple-element.60), channel_id=1, source_target_pairs={{0,4},{4,0},{8,12},{12,8},{16,20},{20,16},{24,28},{28,24},{1,5},{5... | collective-permute-start | bytes 491528 | tf_op jit(solution)/shard_map/ppermute | solution.py:643
  4.9 3.6 %collective-permute-start.1 = (f32[40,1024]{1,0:T(8,128)S(1)}, f32[40,1024]{1,0:T(8,128)S(1)}, u32[]{:S(2)}, u32[]{:S(2)}) collective-permute-start(f32[40,1024]{1,0:T(8,128)S(1)} %get-tuple-element.61), channel_id=1, source_target_pairs={{0,28},{4,8},{8,4},{12,16},{16,12},{20,24},{24,20},{28,0},{1,29},{... | collective-permute-start | bytes 491528 | tf_op jit(solution)/shard_map/ppermute | solution.py:643
  8.5 0.0 collective-permute-start.2
  8.5 1.6 %collective-permute-start.3 = (f32[8,1024]{1,0:T(8,128)S(1)}, f32[8,1024]{1,0:T(8,128)S(1)}, u32[]{:S(2)}, u32[]{:S(2)}) collective-permute-start(f32[8,1024]{1,0:T(8,128)S(1)} %get-tuple-element.63), channel_id=1, source_target_pairs={{0,3},{1,2},{2,1},{3,0},{4,7},{5,6},{6,5},{7,4},{8,11},{9,10},{10,... | collective-permute-start | bytes 98312 | tf_op jit(solution)/shard_map/ppermute | solution.py:643
  10.1 0.0 collective-permute-start.4
  10.1 0.0 copy-done
  10.1 1.3 %shard_map.51 = (f32[128,1024]{1,0:T(8,128)S(1)}, f32[128,1024]{1,0:T(8,128)S(1)}, bf16[512,512]{1,0:T(8,128)(2,1)S(1)}, f32[128,1024]{1,0:T(8,128)S(1)}, f32[12...) custom-call(f32[4,32,1024]{2,1,0:T(8,128)S(1)} %get-tuple-element.50.x_ref, ...), custom_call_target="tpu_custom_call" | custom-call | flops 1000000 | bytes 1000000 | tf_op jit(solution)/shard_map/pallas_call | solution.py:616
  11.5 5.3 %collective-permute-done.4.rc = f32[8,256]{1,0:T(8,128)S(1)} collective-permute-done((f32[8,256]{1,0:T(8,128)S(1)}, f32[8,256]{1,0:T(8,128)S(1)}, u32[]{:S(2)}, u32[]{:S(2)}) %collective-permute-start.4) | collective-permute-done | bytes 8224 | tf_op jit(solution)/shard_map/ppermute | solution.py:659
  16.8 0.0 collective-permute-done.2.r3
  16.8 0.0 collective-permute-done.3.r4
  16.8 0.0 collective-permute-done.r1
  16.8 0.0 collective-permute-done.1.r2
  16.8 0.9 %shard_map.52 = (f32[32,1024]{1,0:T(8,128)S(1)}, f32[32,1024]{1,0:T(8,128)S(1)}, f32[32,1024]{1,0:T(8,128)S(1)}, f32[32,1024]{1,0:T(8,128)S(1)}, f32[128,256]{1,...) custom-call(f32[128,1024]{1,0:T(8,128)S(1)} %get-tuple-element.51.xd, ...), custom_call_target="tpu_custom_call" | custom-call | flops 1000000 | bytes 1000000 | tf_op jit(solution)/shard_map/pallas_call | solution.py:616
  17.7 0.1 collective-permute-start.5
  17.8 1.3 %collective-permute-start.6 = (f32[32,1024]{1,0:T(8,128)S(1)}, f32[32,1024]{1,0:T(8,128)S(1)}, u32[]{:S(2)}, u32[]{:S(2)}) collective-permute-start(f32[32,1024]{1,0:T(8,128)S(1)} %get-tuple-element.74), channel_id=1, source_target_pairs={{0,28},{4,8},{8,4},{12,16},{16,12},{20,24},{24,20},{28,0},{1,29},{... | collective-permute-start | bytes 393224 | tf_op jit(solution)/shard_map/ppermute | solution.py:643
  19.1 0.0 collective-permute-start.7
  19.1 1.6 %collective-permute-start.8 = (f32[16,256]{1,0:T(8,128)S(1)}, f32[16,256]{1,0:T(8,128)S(1)}, u32[]{:S(2)}, u32[]{:S(2)}) collective-permute-start(f32[16,256]{1,0:T(8,128)S(1)} %get-tuple-element.76), channel_id=1, source_target_pairs={{0,3},{1,2},{2,1},{3,0},{4,7},{5,6},{6,5},{7,4},{8,11},{9,10},{10,... | collective-permute-start | bytes 49160 | tf_op jit(solution)/shard_map/ppermute | solution.py:643
  20.7 1.3 %shard_map.53 = (f32[128,1024]{1,0:T(8,128)S(1)}, f32[8,128]{1,0:T(8,128)S(1)}, f32[128,1024]{1,0:T(8,128)S(1)}, f32[128,1024]{1,0:T(8,128)S(1)}) custom-call(f32[32,1024]{1,0:T(8,128)S(1)} %get-tuple-element.65.refs_0_.refs_1_.cx, f32[32,1024]{1,0:T(8,128)S(1)} %get-tuple-element.66.refs_1_, f32[32,1024]{1,0:T(8,128)S(1)} %get-tuple-element.67.refs_2_.cr, ...), custom_call_target="tpu_custom_call" | custom-call | flops 1000000 | bytes 1000000 | tf_op jit(solution)/shard_map/pallas_call | solution.py:616
  22.1 0.0 collective-permute-done.7.refs_6_
  22.1 0.2 collective-permute-done.8.refs_7_
  22.3 3.2 %collective-permute-done.5.refs_4_ = f32[32,1024]{1,0:T(8,128)S(1)} collective-permute-done((f32[32,1024]{1,0:T(8,128)S(1)}, f32[32,1024]{1,0:T(8,128)S(1)}, u32[]{:S(2)}, u32[]{:S(2)}) %collective-permute-start.5) | collective-permute-done | bytes 131104 | tf_op jit(solution)/shard_map/ppermute | solution.py:643
  25.6 0.0 collective-permute-done.6.refs_5_
  25.6 0.3 shard_map.54
  25.8 0.2 collective-permute-start.9
  26.0 1.4 %collective-permute-start.10 = (f32[32,1024]{1,0:T(8,128)S(1)}, f32[32,1024]{1,0:T(8,128)S(1)}, u32[]{:S(2)}, u32[]{:S(2)}) collective-permute-start(f32[32,1024]{1,0:T(8,128)S(1)} %get-tuple-element.80), channel_id=1, source_target_pairs={{0,28},{4,8},{8,4},{12,16},{16,12},{20,24},{24,20},{28,0},{1,29},{... | collective-permute-start | bytes 393224 | tf_op jit(solution)/shard_map/ppermute | solution.py:643
  27.4 0.0 collective-permute-start.11
  27.4 1.6 %collective-permute-start.12 = (f32[16,256]{1,0:T(8,128)S(1)}, f32[16,256]{1,0:T(8,128)S(1)}, u32[]{:S(2)}, u32[]{:S(2)}) collective-permute-start(f32[16,256]{1,0:T(8,128)S(1)} %get-tuple-element.82), channel_id=1, source_target_pairs={{0,3},{1,2},{2,1},{3,0},{4,7},{5,6},{6,5},{7,4},{8,11},{9,10},{10,... | collective-permute-start | bytes 49160 | tf_op jit(solution)/shard_map/ppermute | solution.py:643
  29.1 1.0 %shard_map.55 = (f32[128,1024]{1,0:T(8,128)S(1)}, f32[16,128]{1,0:T(8,128)S(1)}, f32[128,1024]{1,0:T(8,128)S(1)}) custom-call(f32[32,1024]{1,0:T(8,128)S(1)} %get-tuple-element.65.refs_0_.refs_1_.cx, f32[32,1024]{1,0:T(8,128)S(1)} %get-tuple-element.66.refs_1_, f32[32,1024]{1,0:T(8,128)S(1)} %get-tuple-element.67.refs_2_.cr, ...), custom_call_target="tpu_custom_call" | custom-call | flops 1000000 | bytes 1000000 | tf_op jit(solution)/shard_map/pallas_call | solution.py:616
  30.1 0.0 collective-permute-done.11.refs_6_
  30.1 0.5 collective-permute-done.12.refs_7_
  30.6 1.5 %collective-permute-done.9.refs_4_ = f32[32,1024]{1,0:T(8,128)S(1)} collective-permute-done((f32[32,1024]{1,0:T(8,128)S(1)}, f32[32,1024]{1,0:T(8,128)S(1)}, u32[]{:S(2)}, u32[]{:S(2)}) %collective-permute-start.9) | collective-permute-done | bytes 131104 | tf_op jit(solution)/shard_map/ppermute | solution.py:643
  32.1 1.6 %collective-permute-done.10.refs_5_ = f32[32,1024]{1,0:T(8,128)S(1)} collective-permute-done((f32[32,1024]{1,0:T(8,128)S(1)}, f32[32,1024]{1,0:T(8,128)S(1)}, u32[]{:S(2)}, u32[]{:S(2)}) %collective-permute-start.10) | collective-permute-done | bytes 131104 | tf_op jit(solution)/shard_map/ppermute | solution.py:643
  33.7 0.3 shard_map.56
  34.0 0.2 collective-permute-start.13
  34.1 1.6 %collective-permute-start.14 = (f32[32,1024]{1,0:T(8,128)S(1)}, f32[32,1024]{1,0:T(8,128)S(1)}, u32[]{:S(2)}, u32[]{:S(2)}) collective-permute-start(f32[32,1024]{1,0:T(8,128)S(1)} %get-tuple-element.88), channel_id=1, source_target_pairs={{0,28},{4,8},{8,4},{12,16},{16,12},{20,24},{24,20},{28,0},{1,29},{... | collective-permute-start | bytes 393224 | tf_op jit(solution)/shard_map/ppermute | solution.py:643
  35.7 0.0 collective-permute-start.15
  35.7 1.4 %collective-permute-start.16 = (f32[16,256]{1,0:T(8,128)S(1)}, f32[16,256]{1,0:T(8,128)S(1)}, u32[]{:S(2)}, u32[]{:S(2)}) collective-permute-start(f32[16,256]{1,0:T(8,128)S(1)} %get-tuple-element.90), channel_id=1, source_target_pairs={{0,3},{1,2},{2,1},{3,0},{4,7},{5,6},{6,5},{7,4},{8,11},{9,10},{10,... | collective-permute-start | bytes 49160 | tf_op jit(solution)/shard_map/ppermute | solution.py:643
  37.2 1.0 %shard_map.57 = (f32[128,1024]{1,0:T(8,128)S(1)}, f32[8,128]{1,0:T(8,128)S(1)}, f32[128,1024]{1,0:T(8,128)S(1)}) custom-call(f32[32,1024]{1,0:T(8,128)S(1)} %get-tuple-element.65.refs_0_.refs_1_.cx, f32[32,1024]{1,0:T(8,128)S(1)} %get-tuple-element.66.refs_1_, f32[32,1024]{1,0:T(8,128)S(1)} %get-tuple-element.67.refs_2_.cr, ...), custom_call_target="tpu_custom_call" | custom-call | flops 1000000 | bytes 1000000 | tf_op jit(solution)/shard_map/pallas_call | solution.py:616
  38.2 0.0 collective-permute-done.15.r3
  38.2 0.7 %collective-permute-done.16.r4 = f32[16,256]{1,0:T(8,128)S(1)} collective-permute-done((f32[16,256]{1,0:T(8,128)S(1)}, f32[16,256]{1,0:T(8,128)S(1)}, u32[]{:S(2)}, u32[]{:S(2)}) %collective-permute-start.16) | collective-permute-done | bytes 16416 | tf_op jit(solution)/shard_map/ppermute | solution.py:643
  38.9 1.2 %collective-permute-done.13.r1 = f32[32,1024]{1,0:T(8,128)S(1)} collective-permute-done((f32[32,1024]{1,0:T(8,128)S(1)}, f32[32,1024]{1,0:T(8,128)S(1)}, u32[]{:S(2)}, u32[]{:S(2)}) %collective-permute-start.13) | collective-permute-done | bytes 131104 | tf_op jit(solution)/shard_map/ppermute | solution.py:643
  40.1 1.7 %collective-permute-done.14.r2 = f32[32,1024]{1,0:T(8,128)S(1)} collective-permute-done((f32[32,1024]{1,0:T(8,128)S(1)}, f32[32,1024]{1,0:T(8,128)S(1)}, u32[]{:S(2)}, u32[]{:S(2)}) %collective-permute-start.14) | collective-permute-done | bytes 131104 | tf_op jit(solution)/shard_map/ppermute | solution.py:643
  41.8 0.3 shard_map.58
  42.1 9.7 %all_to_all.11 = f32[32,1,128]{2,1,0:T(1,128)S(1)} all-to-all(f32[32,1,128]{2,1,0:T(1,128)S(1)} %bitcast.5), channel_id=1, replica_groups=mesh['group'=8,'rad'=4] {'group','rad'}, dimensions={0} | all-to-all | bytes 32768 | tf_op jit(solution)/shard_map/all_to_all | solution.py:708
  51.8 1.6 %shard_map.59 = (f32[4,32,1024]{2,1,0:T(8,128)}, f32[4,32,1024]{2,1,0:T(8,128)}) custom-call(f32[32,128]{1,0:T(8,128)S(1)} %bitcast.4, f32[4,32,1024]{2,1,0:T(8,128)S(1)} %get-tuple-element.50.x_ref, f32[128,1024]{1,0:T(8,128)S(1)} %get-tuple-element.93.diag, f32[128,1024]{1,0:T(8,128)S(1)} %get-tuple-element.94.z0, f32[128,1024]{1,0:T(8,128)S(1)} %get-tuple-element.95.z1, ...), custom_call_target="tpu_custom_call" | custom-call | flops 1000000 | bytes 1000000 | tf_op jit(solution)/shard_map/pallas_call | solution.py:616
Async XLA Ops:
  0.6 9.5 %copy-start = (f32[4,32,1024]{2,1,0:T(8,128)S(1)}, f32[4,32,1024]{2,1,0:T(8,128)}, u32[]{:S(2)}) copy-start(f32[4,32,1024]{2,1,0:T(8,128)} %s_ref.1) | copy-start | bytes 1572868
  1.9 14.9 %collective-permute-start = (f32[40,1024]{1,0:T(8,128)S(1)}, f32[40,1024]{1,0:T(8,128)S(1)}, u32[]{:S(2)}, u32[]{:S(2)}) collective-permute-start(f32[40,1024]{1,0:T(8,128)S(1)} %get-tuple-element.60), channel_id=1, source_target_pairs={{0,4},{4,0},{8,12},{12,8},{16,20},{20,16},{24,28},{28,24},{1,5},{5... | collective-permute-start | bytes 491528 | tf_op jit(solution)/shard_map/ppermute | solution.py:643
  4.9 11.9 %collective-permute-start.1 = (f32[40,1024]{1,0:T(8,128)S(1)}, f32[40,1024]{1,0:T(8,128)S(1)}, u32[]{:S(2)}, u32[]{:S(2)}) collective-permute-start(f32[40,1024]{1,0:T(8,128)S(1)} %get-tuple-element.61), channel_id=1, source_target_pairs={{0,28},{4,8},{8,4},{12,16},{16,12},{20,24},{24,20},{28,0},{1,29},{... | collective-permute-start | bytes 491528 | tf_op jit(solution)/shard_map/ppermute | solution.py:643
  8.5 8.3 %collective-permute-start.2 = (f32[8,1024]{1,0:T(8,128)S(1)}, f32[8,1024]{1,0:T(8,128)S(1)}, u32[]{:S(2)}, u32[]{:S(2)}) collective-permute-start(f32[8,1024]{1,0:T(8,128)S(1)} %get-tuple-element.62), channel_id=1, source_target_pairs={{0,1},{1,0},{2,3},{3,2},{4,5},{5,4},{6,7},{7,6},{8,9},{9,8},{10,11... | collective-permute-start | bytes 98312 | tf_op jit(solution)/shard_map/ppermute | solution.py:643
  8.5 8.3 %collective-permute-start.3 = (f32[8,1024]{1,0:T(8,128)S(1)}, f32[8,1024]{1,0:T(8,128)S(1)}, u32[]{:S(2)}, u32[]{:S(2)}) collective-permute-start(f32[8,1024]{1,0:T(8,128)S(1)} %get-tuple-element.63), channel_id=1, source_target_pairs={{0,3},{1,2},{2,1},{3,0},{4,7},{5,6},{6,5},{7,4},{8,11},{9,10},{10,... | collective-permute-start | bytes 98312 | tf_op jit(solution)/shard_map/ppermute | solution.py:643
  10.1 6.7 %collective-permute-start.4 = (f32[8,256]{1,0:T(8,128)S(1)}, f32[8,256]{1,0:T(8,128)S(1)}, u32[]{:S(2)}, u32[]{:S(2)}) collective-permute-start(f32[8,256]{1,0:T(8,128)S(1)} %get-tuple-element.64), channel_id=1, source_target_pairs={{0,5},{1,6},{2,7},{3,4},{4,9},{5,10},{6,11},{7,8},{8,13},{9,14},{1... | collective-permute-start | bytes 24584 | tf_op jit(solution)/shard_map/ppermute | solution.py:659
  17.7 7.8 %collective-permute-start.5 = (f32[32,1024]{1,0:T(8,128)S(1)}, f32[32,1024]{1,0:T(8,128)S(1)}, u32[]{:S(2)}, u32[]{:S(2)}) collective-permute-start(f32[32,1024]{1,0:T(8,128)S(1)} %get-tuple-element.73), channel_id=1, source_target_pairs={{0,4},{4,0},{8,12},{12,8},{16,20},{20,16},{24,28},{28,24},{1,5},{5... | collective-permute-start | bytes 393224 | tf_op jit(solution)/shard_map/ppermute | solution.py:643
  17.8 7.8 %collective-permute-start.6 = (f32[32,1024]{1,0:T(8,128)S(1)}, f32[32,1024]{1,0:T(8,128)S(1)}, u32[]{:S(2)}, u32[]{:S(2)}) collective-permute-start(f32[32,1024]{1,0:T(8,128)S(1)} %get-tuple-element.74), channel_id=1, source_target_pairs={{0,28},{4,8},{8,4},{12,16},{16,12},{20,24},{24,20},{28,0},{1,29},{... | collective-permute-start | bytes 393224 | tf_op jit(solution)/shard_map/ppermute | solution.py:643
  19.1 2.9 %collective-permute-start.7 = (f32[16,256]{1,0:T(8,128)S(1)}, f32[16,256]{1,0:T(8,128)S(1)}, u32[]{:S(2)}, u32[]{:S(2)}) collective-permute-start(f32[16,256]{1,0:T(8,128)S(1)} %get-tuple-element.75), channel_id=1, source_target_pairs={{0,1},{1,0},{2,3},{3,2},{4,5},{5,4},{6,7},{7,6},{8,9},{9,8},{10,11... | collective-permute-start | bytes 49160 | tf_op jit(solution)/shard_map/ppermute | solution.py:643
  19.1 3.2 %collective-permute-start.8 = (f32[16,256]{1,0:T(8,128)S(1)}, f32[16,256]{1,0:T(8,128)S(1)}, u32[]{:S(2)}, u32[]{:S(2)}) collective-permute-start(f32[16,256]{1,0:T(8,128)S(1)} %get-tuple-element.76), channel_id=1, source_target_pairs={{0,3},{1,2},{2,1},{3,0},{4,7},{5,6},{6,5},{7,4},{8,11},{9,10},{10,... | collective-permute-start | bytes 49160 | tf_op jit(solution)/shard_map/ppermute | solution.py:643
  25.8 6.3 %collective-permute-start.9 = (f32[32,1024]{1,0:T(8,128)S(1)}, f32[32,1024]{1,0:T(8,128)S(1)}, u32[]{:S(2)}, u32[]{:S(2)}) collective-permute-start(f32[32,1024]{1,0:T(8,128)S(1)} %get-tuple-element.79), channel_id=1, source_target_pairs={{0,4},{4,0},{8,12},{12,8},{16,20},{20,16},{24,28},{28,24},{1,5},{5... | collective-permute-start | bytes 393224 | tf_op jit(solution)/shard_map/ppermute | solution.py:643
  26.0 7.7 %collective-permute-start.10 = (f32[32,1024]{1,0:T(8,128)S(1)}, f32[32,1024]{1,0:T(8,128)S(1)}, u32[]{:S(2)}, u32[]{:S(2)}) collective-permute-start(f32[32,1024]{1,0:T(8,128)S(1)} %get-tuple-element.80), channel_id=1, source_target_pairs={{0,28},{4,8},{8,4},{12,16},{16,12},{20,24},{24,20},{28,0},{1,29},{... | collective-permute-start | bytes 393224 | tf_op jit(solution)/shard_map/ppermute | solution.py:643
  27.4 2.6 %collective-permute-start.11 = (f32[16,256]{1,0:T(8,128)S(1)}, f32[16,256]{1,0:T(8,128)S(1)}, u32[]{:S(2)}, u32[]{:S(2)}) collective-permute-start(f32[16,256]{1,0:T(8,128)S(1)} %get-tuple-element.81), channel_id=1, source_target_pairs={{0,1},{1,0},{2,3},{3,2},{4,5},{5,4},{6,7},{7,6},{8,9},{9,8},{10,11... | collective-permute-start | bytes 49160 | tf_op jit(solution)/shard_map/ppermute | solution.py:643
  27.4 3.2 %collective-permute-start.12 = (f32[16,256]{1,0:T(8,128)S(1)}, f32[16,256]{1,0:T(8,128)S(1)}, u32[]{:S(2)}, u32[]{:S(2)}) collective-permute-start(f32[16,256]{1,0:T(8,128)S(1)} %get-tuple-element.82), channel_id=1, source_target_pairs={{0,3},{1,2},{2,1},{3,0},{4,7},{5,6},{6,5},{7,4},{8,11},{9,10},{10,... | collective-permute-start | bytes 49160 | tf_op jit(solution)/shard_map/ppermute | solution.py:643
  34.0 6.1 %collective-permute-start.13 = (f32[32,1024]{1,0:T(8,128)S(1)}, f32[32,1024]{1,0:T(8,128)S(1)}, u32[]{:S(2)}, u32[]{:S(2)}) collective-permute-start(f32[32,1024]{1,0:T(8,128)S(1)} %get-tuple-element.87), channel_id=1, source_target_pairs={{0,4},{4,0},{8,12},{12,8},{16,20},{20,16},{24,28},{28,24},{1,5},{5... | collective-permute-start | bytes 393224 | tf_op jit(solution)/shard_map/ppermute | solution.py:643
  34.1 7.7 %collective-permute-start.14 = (f32[32,1024]{1,0:T(8,128)S(1)}, f32[32,1024]{1,0:T(8,128)S(1)}, u32[]{:S(2)}, u32[]{:S(2)}) collective-permute-start(f32[32,1024]{1,0:T(8,128)S(1)} %get-tuple-element.88), channel_id=1, source_target_pairs={{0,28},{4,8},{8,4},{12,16},{16,12},{20,24},{24,20},{28,0},{1,29},{... | collective-permute-start | bytes 393224 | tf_op jit(solution)/shard_map/ppermute | solution.py:643
  35.7 2.5 %collective-permute-start.15 = (f32[16,256]{1,0:T(8,128)S(1)}, f32[16,256]{1,0:T(8,128)S(1)}, u32[]{:S(2)}, u32[]{:S(2)}) collective-permute-start(f32[16,256]{1,0:T(8,128)S(1)} %get-tuple-element.89), channel_id=1, source_target_pairs={{0,1},{1,0},{2,3},{3,2},{4,5},{5,4},{6,7},{7,6},{8,9},{9,8},{10,11... | collective-permute-start | bytes 49160 | tf_op jit(solution)/shard_map/ppermute | solution.py:643
  35.7 3.2 %collective-permute-start.16 = (f32[16,256]{1,0:T(8,128)S(1)}, f32[16,256]{1,0:T(8,128)S(1)}, u32[]{:S(2)}, u32[]{:S(2)}) collective-permute-start(f32[16,256]{1,0:T(8,128)S(1)} %get-tuple-element.90), channel_id=1, source_target_pairs={{0,3},{1,2},{2,1},{3,0},{4,7},{5,6},{6,5},{7,4},{8,11},{9,10},{10,... | collective-permute-start | bytes 49160 | tf_op jit(solution)/shard_map/ppermute | solution.py:643

commit v5 on v3

--- a/solution.py
+++ b/solution.py
@@ -12,7 +12,7 @@
 BF16 = jnp.bfloat16
 LANES = 128
 ROWS = 8
-SHIFT = 1.145
+SHIFT = 0.5
 DOTS = 5
 FOLD = LANES // 2
 
@@ -61,6 +61,13 @@
 
 def last_row(u):
     return K[4][0] * u[0] + K[4][1] * u[1] + K[4][2] * u[2] + K[4][3] * u[3]
+
+
+def tree_sum(values):
+    while len(values) > 1:
+        pairs = [values[i] + values[i + 1] for i in range(0, len(values) - 1, 2)]
+        values = pairs + values[len(values) - len(values) % 2 :]
+    return values[0]
 
 
 class Shape:
@@ -459,9 +466,10 @@
         buffer = refs[-1]
         newest = many[-1]
         local_apply(g, newest, cx, cxp, cr, crp, cy, v_ref)
-        totals = [jnp.zeros((g.rows, LANES), F32)] * count
+        terms = [[] for _ in range(count)]
         diagonal = refs[-2] if with_diagonal else None
         for ab in range(16):
+            group = [[] for _ in range(count)]
             for h in range(g.halves):
                 for c in range(4):
                     at = (g.row(ab), g.lane(h, c))
@@ -469,7 +477,11 @@
                     if with_diagonal:
                         diagonal[at] = diag
                     weighted = diag * newest[at]
-                    totals = [total + weighted * ref[at] for total, ref in zip(totals, many)]
+                    for values, ref in zip(group, many):
+                        values.append(weighted * ref[at])
+            for values, part in zip(terms, group):
+                values.append(tree_sum(part))
+        totals = [tree_sum(values) for values in terms]
         if earlier:
             parts = [ref[pl.ds(i, g.rows), :] for ref in before for i in range(0, ref.shape[0], g.rows)]
             place = lane_index(g)
@@ -543,15 +555,10 @@
                 halo = received(g, r1, r2, r3, r4, h, c, at, even_x, even_r, bottom, top)
                 add_halo(g, v, coef_x, coef_r, *halo, rows)
                 for a in range(4):
-                    total = jnp.zeros((g.rows, LANES), F32)
                     for b in range(4):
-                        rw = g.row(4 * a + b)
-                        v_ref[rw, at] = v[a][b]
-                        total = total + z_ref[rw, at] * v[a][b]
-                    totals.append(total)
-        while len(totals) > 1:
-            totals = [sum(totals[i : i + 2]) for i in range(0, len(totals), 2)]
-        row = jnp.sum(totals[0], axis=0, keepdims=True)
+                        v_ref[g.row(4 * a + b), at] = v[a][b]
+                    totals.append(tree_sum([z_ref[g.row(4 * a + b), at] * v[a][b] for b in range(4)]))
+        row = jnp.sum(tree_sum(totals), axis=0, keepdims=True)
         row = row + pltpu.roll(row, FOLD, 1)
         place = lax.broadcasted_iota(jnp.int32, (1, LANES), 1)
         row = jnp.where(place < FOLD, row, dots[0:1])

time: 53.6 us -> 53.6 us (level)
  no operation moved by 1% of the time
where the time goes in v5:
time: 53.6 us; the launch traced here: 53.5 us
  starting transfers between devices  17.7 us (33%)
  waiting for transfers between devices  16 us (30%)
  blocking collectives  9.72 us (18%)
  Pallas kernels  9.32 us (17%)
  between operations  0.74 us (1%)
    ppermute x16, starting transfers between devices, exchange(): got.append(lax.ppermute(value, axis, swaps(count, parity)))  17.7 us
    ppermute x16, waiting for transfers between devices, exchange(): got.append(lax.ppermute(value, axis, swaps(count, parity)))  10.7 us
    all_to_all x1, blocking collectives, steps(): sums = lax.all_to_all(message, ('group', 'rad'), 0, 0, tiled=True)  9.72 us
    pallas_call x10, Pallas kernels, call(): pl.pallas_call(body, in_specs=in_specs or [VMEM] * len(args), out_specs=o...  9.32 us
    ppermute x1, waiting for transfers between devices, steps(): corner = lax.ppermute(corner, ('group', 'rad'), diagonal)  5.31 us
  transfers between devices with their start and end apart: 17, of which 9 were waited for; matrix products, arithmetic and copies ran while one was open for 0% of the time, Pallas kernels for 9%

profile of v5, /device:TPU:0, one launch (start us, length us, event | category | flops | bytes accessed | tf_op | source)
XLA Modules:
  0.0 53.5 jit_solution(16776633331814186342)
XLA Ops:
  0.6 0.0 copy-start
  0.6 1.2 %shard_map.50 = (f32[4,32,1024]{2,1,0:T(8,128)S(1)}, f32[3,1,8,256]{3,2,1,0:T(8,128)S(1)}, f32[40,1024]{1,0:T(8,128)S(1)}, f32[40,1024]{1,0:T(8,128)S(1)}, f32[8...) custom-call(f32[4,32,1024]{2,1,0:T(8,128)} %x_hbm.1, f32[3,1,8,256]{3,2,1,0:T(8,128)} %m_hbm.1), custom_call_target="tpu_custom_call" | custom-call | flops 1000000 | bytes 1000000 | tf_op jit(solution)/shard_map/pallas_call | solution.py:627
  1.9 3.0 %collective-permute-start = (f32[40,1024]{1,0:T(8,128)S(1)}, f32[40,1024]{1,0:T(8,128)S(1)}, u32[]{:S(2)}, u32[]{:S(2)}) collective-permute-start(f32[40,1024]{1,0:T(8,128)S(1)} %get-tuple-element.60), channel_id=1, source_target_pairs={{0,4},{4,0},{8,12},{12,8},{16,20},{20,16},{24,28},{28,24},{1,5},{5... | collective-permute-start | bytes 491528 | tf_op jit(solution)/shard_map/ppermute | solution.py:654
  4.9 3.6 %collective-permute-start.1 = (f32[40,1024]{1,0:T(8,128)S(1)}, f32[40,1024]{1,0:T(8,128)S(1)}, u32[]{:S(2)}, u32[]{:S(2)}) collective-permute-start(f32[40,1024]{1,0:T(8,128)S(1)} %get-tuple-element.61), channel_id=1, source_target_pairs={{0,28},{4,8},{8,4},{12,16},{16,12},{20,24},{24,20},{28,0},{1,29},{... | collective-permute-start | bytes 491528 | tf_op jit(solution)/shard_map/ppermute | solution.py:654
  8.5 0.0 collective-permute-start.2
  8.5 1.6 %collective-permute-start.3 = (f32[8,1024]{1,0:T(8,128)S(1)}, f32[8,1024]{1,0:T(8,128)S(1)}, u32[]{:S(2)}, u32[]{:S(2)}) collective-permute-start(f32[8,1024]{1,0:T(8,128)S(1)} %get-tuple-element.63), channel_id=1, source_target_pairs={{0,3},{1,2},{2,1},{3,0},{4,7},{5,6},{6,5},{7,4},{8,11},{9,10},{10,... | collective-permute-start | bytes 98312 | tf_op jit(solution)/shard_map/ppermute | solution.py:654
  10.1 0.0 collective-permute-start.4
  10.1 0.0 copy-done
  10.1 1.4 %shard_map.51 = (f32[128,1024]{1,0:T(8,128)S(1)}, f32[128,1024]{1,0:T(8,128)S(1)}, bf16[512,512]{1,0:T(8,128)(2,1)S(1)}, f32[128,1024]{1,0:T(8,128)S(1)}, f32[12...) custom-call(f32[4,32,1024]{2,1,0:T(8,128)S(1)} %get-tuple-element.50.x_ref, ...), custom_call_target="tpu_custom_call" | custom-call | flops 1000000 | bytes 1000000 | tf_op jit(solution)/shard_map/pallas_call | solution.py:627
  11.5 5.3 %collective-permute-done.4.rc = f32[8,256]{1,0:T(8,128)S(1)} collective-permute-done((f32[8,256]{1,0:T(8,128)S(1)}, f32[8,256]{1,0:T(8,128)S(1)}, u32[]{:S(2)}, u32[]{:S(2)}) %collective-permute-start.4) | collective-permute-done | bytes 8224 | tf_op jit(solution)/shard_map/ppermute | solution.py:670
  16.8 0.0 collective-permute-done.2.r3
  16.8 0.0 collective-permute-done.3.r4
  16.8 0.0 collective-permute-done.r1
  16.8 0.0 collective-permute-done.1.r2
  16.8 0.9 %shard_map.52 = (f32[32,1024]{1,0:T(8,128)S(1)}, f32[32,1024]{1,0:T(8,128)S(1)}, f32[32,1024]{1,0:T(8,128)S(1)}, f32[32,1024]{1,0:T(8,128)S(1)}, f32[128,256]{1,...) custom-call(f32[128,1024]{1,0:T(8,128)S(1)} %get-tuple-element.51.xd, ...), custom_call_target="tpu_custom_call" | custom-call | flops 1000000 | bytes 1000000 | tf_op jit(solution)/shard_map/pallas_call | solution.py:627
  17.7 0.1 collective-permute-start.5
  17.8 1.3 %collective-permute-start.6 = (f32[32,1024]{1,0:T(8,128)S(1)}, f32[32,1024]{1,0:T(8,128)S(1)}, u32[]{:S(2)}, u32[]{:S(2)}) collective-permute-start(f32[32,1024]{1,0:T(8,128)S(1)} %get-tuple-element.74), channel_id=1, source_target_pairs={{0,28},{4,8},{8,4},{12,16},{16,12},{20,24},{24,20},{28,0},{1,29},{... | collective-permute-start | bytes 393224 | tf_op jit(solution)/shard_map/ppermute | solution.py:654
  19.1 0.0 collective-permute-start.7
  19.1 1.6 %collective-permute-start.8 = (f32[16,256]{1,0:T(8,128)S(1)}, f32[16,256]{1,0:T(8,128)S(1)}, u32[]{:S(2)}, u32[]{:S(2)}) collective-permute-start(f32[16,256]{1,0:T(8,128)S(1)} %get-tuple-element.76), channel_id=1, source_target_pairs={{0,3},{1,2},{2,1},{3,0},{4,7},{5,6},{6,5},{7,4},{8,11},{9,10},{10,... | collective-permute-start | bytes 49160 | tf_op jit(solution)/shard_map/ppermute | solution.py:654
  20.7 1.3 %shard_map.53 = (f32[128,1024]{1,0:T(8,128)S(1)}, f32[8,128]{1,0:T(8,128)S(1)}, f32[128,1024]{1,0:T(8,128)S(1)}, f32[128,1024]{1,0:T(8,128)S(1)}) custom-call(f32[32,1024]{1,0:T(8,128)S(1)} %get-tuple-element.65.refs_0_.refs_1_.cx, f32[32,1024]{1,0:T(8,128)S(1)} %get-tuple-element.66.refs_1_, f32[32,1024]{1,0:T(8,128)S(1)} %get-tuple-element.67.refs_2_.cr, ...), custom_call_target="tpu_custom_call" | custom-call | flops 1000000 | bytes 1000000 | tf_op jit(solution)/shard_map/pallas_call | solution.py:627
  22.1 0.0 collective-permute-done.7.refs_6_
  22.1 0.2 collective-permute-done.8.refs_7_
  22.3 3.3 %collective-permute-done.5.refs_4_ = f32[32,1024]{1,0:T(8,128)S(1)} collective-permute-done((f32[32,1024]{1,0:T(8,128)S(1)}, f32[32,1024]{1,0:T(8,128)S(1)}, u32[]{:S(2)}, u32[]{:S(2)}) %collective-permute-start.5) | collective-permute-done | bytes 131104 | tf_op jit(solution)/shard_map/ppermute | solution.py:654
  25.6 0.0 collective-permute-done.6.refs_5_
  25.6 0.3 shard_map.54
  25.9 0.2 collective-permute-start.9
  26.1 1.4 %collective-permute-start.10 = (f32[32,1024]{1,0:T(8,128)S(1)}, f32[32,1024]{1,0:T(8,128)S(1)}, u32[]{:S(2)}, u32[]{:S(2)}) collective-permute-start(f32[32,1024]{1,0:T(8,128)S(1)} %get-tuple-element.80), channel_id=1, source_target_pairs={{0,28},{4,8},{8,4},{12,16},{16,12},{20,24},{24,20},{28,0},{1,29},{... | collective-permute-start | bytes 393224 | tf_op jit(solution)/shard_map/ppermute | solution.py:654
  27.5 0.0 collective-permute-start.11
  27.5 1.6 %collective-permute-start.12 = (f32[16,256]{1,0:T(8,128)S(1)}, f32[16,256]{1,0:T(8,128)S(1)}, u32[]{:S(2)}, u32[]{:S(2)}) collective-permute-start(f32[16,256]{1,0:T(8,128)S(1)} %get-tuple-element.82), channel_id=1, source_target_pairs={{0,3},{1,2},{2,1},{3,0},{4,7},{5,6},{6,5},{7,4},{8,11},{9,10},{10,... | collective-permute-start | bytes 49160 | tf_op jit(solution)/shard_map/ppermute | solution.py:654
  29.1 1.0 %shard_map.55 = (f32[128,1024]{1,0:T(8,128)S(1)}, f32[16,128]{1,0:T(8,128)S(1)}, f32[128,1024]{1,0:T(8,128)S(1)}) custom-call(f32[32,1024]{1,0:T(8,128)S(1)} %get-tuple-element.65.refs_0_.refs_1_.cx, f32[32,1024]{1,0:T(8,128)S(1)} %get-tuple-element.66.refs_1_, f32[32,1024]{1,0:T(8,128)S(1)} %get-tuple-element.67.refs_2_.cr, ...), custom_call_target="tpu_custom_call" | custom-call | flops 1000000 | bytes 1000000 | tf_op jit(solution)/shard_map/pallas_call | solution.py:627
  30.1 0.0 collective-permute-done.11.refs_6_
  30.1 0.5 collective-permute-done.12.refs_7_
  30.6 1.5 %collective-permute-done.9.refs_4_ = f32[32,1024]{1,0:T(8,128)S(1)} collective-permute-done((f32[32,1024]{1,0:T(8,128)S(1)}, f32[32,1024]{1,0:T(8,128)S(1)}, u32[]{:S(2)}, u32[]{:S(2)}) %collective-permute-start.9) | collective-permute-done | bytes 131104 | tf_op jit(solution)/shard_map/ppermute | solution.py:654
  32.1 1.6 %collective-permute-done.10.refs_5_ = f32[32,1024]{1,0:T(8,128)S(1)} collective-permute-done((f32[32,1024]{1,0:T(8,128)S(1)}, f32[32,1024]{1,0:T(8,128)S(1)}, u32[]{:S(2)}, u32[]{:S(2)}) %collective-permute-start.10) | collective-permute-done | bytes 131104 | tf_op jit(solution)/shard_map/ppermute | solution.py:654
  33.7 0.3 shard_map.56
  34.0 0.2 collective-permute-start.13
  34.2 1.6 %collective-permute-start.14 = (f32[32,1024]{1,0:T(8,128)S(1)}, f32[32,1024]{1,0:T(8,128)S(1)}, u32[]{:S(2)}, u32[]{:S(2)}) collective-permute-start(f32[32,1024]{1,0:T(8,128)S(1)} %get-tuple-element.88), channel_id=1, source_target_pairs={{0,28},{4,8},{8,4},{12,16},{16,12},{20,24},{24,20},{28,0},{1,29},{... | collective-permute-start | bytes 393224 | tf_op jit(solution)/shard_map/ppermute | solution.py:654
  35.8 0.0 collective-permute-start.15
  35.8 1.4 %collective-permute-start.16 = (f32[16,256]{1,0:T(8,128)S(1)}, f32[16,256]{1,0:T(8,128)S(1)}, u32[]{:S(2)}, u32[]{:S(2)}) collective-permute-start(f32[16,256]{1,0:T(8,128)S(1)} %get-tuple-element.90), channel_id=1, source_target_pairs={{0,3},{1,2},{2,1},{3,0},{4,7},{5,6},{6,5},{7,4},{8,11},{9,10},{10,... | collective-permute-start | bytes 49160 | tf_op jit(solution)/shard_map/ppermute | solution.py:654
  37.3 1.0 %shard_map.57 = (f32[128,1024]{1,0:T(8,128)S(1)}, f32[8,128]{1,0:T(8,128)S(1)}, f32[128,1024]{1,0:T(8,128)S(1)}) custom-call(f32[32,1024]{1,0:T(8,128)S(1)} %get-tuple-element.65.refs_0_.refs_1_.cx, f32[32,1024]{1,0:T(8,128)S(1)} %get-tuple-element.66.refs_1_, f32[32,1024]{1,0:T(8,128)S(1)} %get-tuple-element.67.refs_2_.cr, ...), custom_call_target="tpu_custom_call" | custom-call | flops 1000000 | bytes 1000000 | tf_op jit(solution)/shard_map/pallas_call | solution.py:627
  38.3 0.0 collective-permute-done.15.r3
  38.3 0.7 %collective-permute-done.16.r4 = f32[16,256]{1,0:T(8,128)S(1)} collective-permute-done((f32[16,256]{1,0:T(8,128)S(1)}, f32[16,256]{1,0:T(8,128)S(1)}, u32[]{:S(2)}, u32[]{:S(2)}) %collective-permute-start.16) | collective-permute-done | bytes 16416 | tf_op jit(solution)/shard_map/ppermute | solution.py:654
  39.0 1.2 %collective-permute-done.13.r1 = f32[32,1024]{1,0:T(8,128)S(1)} collective-permute-done((f32[32,1024]{1,0:T(8,128)S(1)}, f32[32,1024]{1,0:T(8,128)S(1)}, u32[]{:S(2)}, u32[]{:S(2)}) %collective-permute-start.13) | collective-permute-done | bytes 131104 | tf_op jit(solution)/shard_map/ppermute | solution.py:654
  40.2 1.7 %collective-permute-done.14.r2 = f32[32,1024]{1,0:T(8,128)S(1)} collective-permute-done((f32[32,1024]{1,0:T(8,128)S(1)}, f32[32,1024]{1,0:T(8,128)S(1)}, u32[]{:S(2)}, u32[]{:S(2)}) %collective-permute-start.14) | collective-permute-done | bytes 131104 | tf_op jit(solution)/shard_map/ppermute | solution.py:654
  41.9 0.3 shard_map.58
  42.2 9.7 %all_to_all.11 = f32[32,1,128]{2,1,0:T(1,128)S(1)} all-to-all(f32[32,1,128]{2,1,0:T(1,128)S(1)} %bitcast.5), channel_id=1, replica_groups=mesh['group'=8,'rad'=4] {'group','rad'}, dimensions={0} | all-to-all | bytes 32768 | tf_op jit(solution)/shard_map/all_to_all | solution.py:719
  51.9 1.6 %shard_map.59 = (f32[4,32,1024]{2,1,0:T(8,128)}, f32[4,32,1024]{2,1,0:T(8,128)}) custom-call(f32[32,128]{1,0:T(8,128)S(1)} %bitcast.4, f32[4,32,1024]{2,1,0:T(8,128)S(1)} %get-tuple-element.50.x_ref, f32[128,1024]{1,0:T(8,128)S(1)} %get-tuple-element.93.diag, f32[128,1024]{1,0:T(8,128)S(1)} %get-tuple-element.94.z0, f32[128,1024]{1,0:T(8,128)S(1)} %get-tuple-element.95.z1, ...), custom_call_target="tpu_custom_call" | custom-call | flops 1000000 | bytes 1000000 | tf_op jit(solution)/shard_map/pallas_call | solution.py:627
Async XLA Ops:
  0.6 9.5 %copy-start = (f32[4,32,1024]{2,1,0:T(8,128)S(1)}, f32[4,32,1024]{2,1,0:T(8,128)}, u32[]{:S(2)}) copy-start(f32[4,32,1024]{2,1,0:T(8,128)} %s_ref.1) | copy-start | bytes 1572868
  1.9 14.9 %collective-permute-start = (f32[40,1024]{1,0:T(8,128)S(1)}, f32[40,1024]{1,0:T(8,128)S(1)}, u32[]{:S(2)}, u32[]{:S(2)}) collective-permute-start(f32[40,1024]{1,0:T(8,128)S(1)} %get-tuple-element.60), channel_id=1, source_target_pairs={{0,4},{4,0},{8,12},{12,8},{16,20},{20,16},{24,28},{28,24},{1,5},{5... | collective-permute-start | bytes 491528 | tf_op jit(solution)/shard_map/ppermute | solution.py:654
  4.9 11.9 %collective-permute-start.1 = (f32[40,1024]{1,0:T(8,128)S(1)}, f32[40,1024]{1,0:T(8,128)S(1)}, u32[]{:S(2)}, u32[]{:S(2)}) collective-permute-start(f32[40,1024]{1,0:T(8,128)S(1)} %get-tuple-element.61), channel_id=1, source_target_pairs={{0,28},{4,8},{8,4},{12,16},{16,12},{20,24},{24,20},{28,0},{1,29},{... | collective-permute-start | bytes 491528 | tf_op jit(solution)/shard_map/ppermute | solution.py:654
  8.5 8.3 %collective-permute-start.2 = (f32[8,1024]{1,0:T(8,128)S(1)}, f32[8,1024]{1,0:T(8,128)S(1)}, u32[]{:S(2)}, u32[]{:S(2)}) collective-permute-start(f32[8,1024]{1,0:T(8,128)S(1)} %get-tuple-element.62), channel_id=1, source_target_pairs={{0,1},{1,0},{2,3},{3,2},{4,5},{5,4},{6,7},{7,6},{8,9},{9,8},{10,11... | collective-permute-start | bytes 98312 | tf_op jit(solution)/shard_map/ppermute | solution.py:654
  8.5 8.3 %collective-permute-start.3 = (f32[8,1024]{1,0:T(8,128)S(1)}, f32[8,1024]{1,0:T(8,128)S(1)}, u32[]{:S(2)}, u32[]{:S(2)}) collective-permute-start(f32[8,1024]{1,0:T(8,128)S(1)} %get-tuple-element.63), channel_id=1, source_target_pairs={{0,3},{1,2},{2,1},{3,0},{4,7},{5,6},{6,5},{7,4},{8,11},{9,10},{10,... | collective-permute-start | bytes 98312 | tf_op jit(solution)/shard_map/ppermute | solution.py:654
  10.1 6.7 %collective-permute-start.4 = (f32[8,256]{1,0:T(8,128)S(1)}, f32[8,256]{1,0:T(8,128)S(1)}, u32[]{:S(2)}, u32[]{:S(2)}) collective-permute-start(f32[8,256]{1,0:T(8,128)S(1)} %get-tuple-element.64), channel_id=1, source_target_pairs={{0,5},{1,6},{2,7},{3,4},{4,9},{5,10},{6,11},{7,8},{8,13},{9,14},{1... | collective-permute-start | bytes 24584 | tf_op jit(solution)/shard_map/ppermute | solution.py:670
  17.7 7.8 %collective-permute-start.5 = (f32[32,1024]{1,0:T(8,128)S(1)}, f32[32,1024]{1,0:T(8,128)S(1)}, u32[]{:S(2)}, u32[]{:S(2)}) collective-permute-start(f32[32,1024]{1,0:T(8,128)S(1)} %get-tuple-element.73), channel_id=1, source_target_pairs={{0,4},{4,0},{8,12},{12,8},{16,20},{20,16},{24,28},{28,24},{1,5},{5... | collective-permute-start | bytes 393224 | tf_op jit(solution)/shard_map/ppermute | solution.py:654
  17.8 7.8 %collective-permute-start.6 = (f32[32,1024]{1,0:T(8,128)S(1)}, f32[32,1024]{1,0:T(8,128)S(1)}, u32[]{:S(2)}, u32[]{:S(2)}) collective-permute-start(f32[32,1024]{1,0:T(8,128)S(1)} %get-tuple-element.74), channel_id=1, source_target_pairs={{0,28},{4,8},{8,4},{12,16},{16,12},{20,24},{24,20},{28,0},{1,29},{... | collective-permute-start | bytes 393224 | tf_op jit(solution)/shard_map/ppermute | solution.py:654
  19.1 2.9 %collective-permute-start.7 = (f32[16,256]{1,0:T(8,128)S(1)}, f32[16,256]{1,0:T(8,128)S(1)}, u32[]{:S(2)}, u32[]{:S(2)}) collective-permute-start(f32[16,256]{1,0:T(8,128)S(1)} %get-tuple-element.75), channel_id=1, source_target_pairs={{0,1},{1,0},{2,3},{3,2},{4,5},{5,4},{6,7},{7,6},{8,9},{9,8},{10,11... | collective-permute-start | bytes 49160 | tf_op jit(solution)/shard_map/ppermute | solution.py:654
  19.1 3.2 %collective-permute-start.8 = (f32[16,256]{1,0:T(8,128)S(1)}, f32[16,256]{1,0:T(8,128)S(1)}, u32[]{:S(2)}, u32[]{:S(2)}) collective-permute-start(f32[16,256]{1,0:T(8,128)S(1)} %get-tuple-element.76), channel_id=1, source_target_pairs={{0,3},{1,2},{2,1},{3,0},{4,7},{5,6},{6,5},{7,4},{8,11},{9,10},{10,... | collective-permute-start | bytes 49160 | tf_op jit(solution)/shard_map/ppermute | solution.py:654
  25.9 6.3 %collective-permute-start.9 = (f32[32,1024]{1,0:T(8,128)S(1)}, f32[32,1024]{1,0:T(8,128)S(1)}, u32[]{:S(2)}, u32[]{:S(2)}) collective-permute-start(f32[32,1024]{1,0:T(8,128)S(1)} %get-tuple-element.79), channel_id=1, source_target_pairs={{0,4},{4,0},{8,12},{12,8},{16,20},{20,16},{24,28},{28,24},{1,5},{5... | collective-permute-start | bytes 393224 | tf_op jit(solution)/shard_map/ppermute | solution.py:654
  26.1 7.7 %collective-permute-start.10 = (f32[32,1024]{1,0:T(8,128)S(1)}, f32[32,1024]{1,0:T(8,128)S(1)}, u32[]{:S(2)}, u32[]{:S(2)}) collective-permute-start(f32[32,1024]{1,0:T(8,128)S(1)} %get-tuple-element.80), channel_id=1, source_target_pairs={{0,28},{4,8},{8,4},{12,16},{16,12},{20,24},{24,20},{28,0},{1,29},{... | collective-permute-start | bytes 393224 | tf_op jit(solution)/shard_map/ppermute | solution.py:654
  27.5 2.6 %collective-permute-start.11 = (f32[16,256]{1,0:T(8,128)S(1)}, f32[16,256]{1,0:T(8,128)S(1)}, u32[]{:S(2)}, u32[]{:S(2)}) collective-permute-start(f32[16,256]{1,0:T(8,128)S(1)} %get-tuple-element.81), channel_id=1, source_target_pairs={{0,1},{1,0},{2,3},{3,2},{4,5},{5,4},{6,7},{7,6},{8,9},{9,8},{10,11... | collective-permute-start | bytes 49160 | tf_op jit(solution)/shard_map/ppermute | solution.py:654
  27.5 3.2 %collective-permute-start.12 = (f32[16,256]{1,0:T(8,128)S(1)}, f32[16,256]{1,0:T(8,128)S(1)}, u32[]{:S(2)}, u32[]{:S(2)}) collective-permute-start(f32[16,256]{1,0:T(8,128)S(1)} %get-tuple-element.82), channel_id=1, source_target_pairs={{0,3},{1,2},{2,1},{3,0},{4,7},{5,6},{6,5},{7,4},{8,11},{9,10},{10,... | collective-permute-start | bytes 49160 | tf_op jit(solution)/shard_map/ppermute | solution.py:654
  34.0 6.1 %collective-permute-start.13 = (f32[32,1024]{1,0:T(8,128)S(1)}, f32[32,1024]{1,0:T(8,128)S(1)}, u32[]{:S(2)}, u32[]{:S(2)}) collective-permute-start(f32[32,1024]{1,0:T(8,128)S(1)} %get-tuple-element.87), channel_id=1, source_target_pairs={{0,4},{4,0},{8,12},{12,8},{16,20},{20,16},{24,28},{28,24},{1,5},{5... | collective-permute-start | bytes 393224 | tf_op jit(solution)/shard_map/ppermute | solution.py:654
  34.2 7.7 %collective-permute-start.14 = (f32[32,1024]{1,0:T(8,128)S(1)}, f32[32,1024]{1,0:T(8,128)S(1)}, u32[]{:S(2)}, u32[]{:S(2)}) collective-permute-start(f32[32,1024]{1,0:T(8,128)S(1)} %get-tuple-element.88), channel_id=1, source_target_pairs={{0,28},{4,8},{8,4},{12,16},{16,12},{20,24},{24,20},{28,0},{1,29},{... | collective-permute-start | bytes 393224 | tf_op jit(solution)/shard_map/ppermute | solution.py:654
  35.8 2.5 %collective-permute-start.15 = (f32[16,256]{1,0:T(8,128)S(1)}, f32[16,256]{1,0:T(8,128)S(1)}, u32[]{:S(2)}, u32[]{:S(2)}) collective-permute-start(f32[16,256]{1,0:T(8,128)S(1)} %get-tuple-element.89), channel_id=1, source_target_pairs={{0,1},{1,0},{2,3},{3,2},{4,5},{5,4},{6,7},{7,6},{8,9},{9,8},{10,11... | collective-permute-start | bytes 49160 | tf_op jit(solution)/shard_map/ppermute | solution.py:654
  35.8 3.2 %collective-permute-start.16 = (f32[16,256]{1,0:T(8,128)S(1)}, f32[16,256]{1,0:T(8,128)S(1)}, u32[]{:S(2)}, u32[]{:S(2)}) collective-permute-start(f32[16,256]{1,0:T(8,128)S(1)} %get-tuple-element.90), channel_id=1, source_target_pairs={{0,3},{1,2},{2,1},{3,0},{4,7},{5,6},{6,5},{7,4},{8,11},{9,10},{10,... | collective-permute-start | bytes 49160 | tf_op jit(solution)/shard_map/ppermute | solution.py:654
